TPU v7x, 128 devices: a whole 4x4x4 slice. The times are simulated.
128 devices in a mesh: grp: 8 (over x, core), dev: 16 (over z, y).
Axes of the slice: x: 4, y: 4, z: 4, core: 2. Of those that a mesh axis runs over, the one named last changes fastest.
Arguments:
- transition: float32 [256, 256, 256], P(('grp', 'dev')), as said below
- observe: float32 [256, 64, 256], P(('grp', 'dev')), may hold values from -0.375 to 0.375
- noise_obs: float32 [256, 64], P(('grp', 'dev')), may hold values from 100 to 1000
- measured: float32 [256, 64], P(('grp', 'dev')), may hold values from -60 to 60
- noise_state: float32 [256, 256], replicated, as said below
- prior_mean: float32 [256], replicated, may hold values from -6 to 6
- prior_cov: float32 [256, 256], replicated, as said below
Outputs:
- means: float32 [256, 256], P(('grp', 'dev'))
- covs: float32 [256, 256, 256], P(('grp', 'dev'))
Inputs may be any that keep to these rules, and one draw needn't show every extreme that they name: `transition`: each matrix is (I + G) / sqrt(1.0625) with G of independent entries of deviation 0.25 / sqrt(256). `noise_state`: symmetric positive definite, 0.001 (I + E) with E symmetric of spectral norm well under one. `prior_cov`: symmetric positive definite, I + E with E symmetric of spectral norm well under one.
All inputs are finite; a program needn't handle non-finite values.
Results may differ from a plain program's by a relative error of at most 0.0003.
Values sent between devices are 32-bit elements; how exact they have to be, the bound alone decides.
No kernel may reach another device: no remote copies, remote signals or barrier semaphores. Data moves between devices by JAX's collectives and lax.ppermute only.
A program may use at most 128 MiB of HBM per device.

v0:
```python
import jax
import jax.numpy as jnp
from jax import lax
from jax.sharding import Mesh
from jax.sharding import PartitionSpec as P

GRP = ("grp_0", "grp_1")
DEV = ("dev_0", "dev_1")
GRP_DEV = ("grp_0", "grp_1", "dev_0", "dev_1")


def filled_with(x, identity):
    return jax.tree.map(
        lambda part, zero: jnp.zeros_like(part) + jnp.asarray(zero, part.dtype), x, identity
    )


def entering_2(x, axes, combine, identity):
    before = start = filled_with(x, identity)
    so_far = x
    for axis in reversed(axes):
        length, here = (lax.axis_size(axis), lax.axis_index(axis))
        pieces = jax.tree.map(lambda part: lax.all_gather(part, axis), so_far)
        inside, so_far = (start, start)
        for k in range(length):
            passed = k < here
            so_far = combine(so_far, jax.tree.map(lambda part: part[k], pieces))
            inside = jax.tree.map(lambda new, old: jnp.where(passed, new, old), so_far, inside)
        before = combine(inside, before)
    return before


def product(left, right):
    return jnp.matmul(left, right, precision=lax.Precision.HIGHEST)


def invert_batch(innovation):
    high = lax.Precision.HIGHEST
    width = innovation.shape[1]
    eye = jnp.eye(width, dtype=jnp.float32)
    inverse_diag = 1.0 / jnp.diagonal(innovation, axis1=1, axis2=2)
    guess = eye[None] * inverse_diag[:, None, :]
    for sweep in range(3):
        residue = 2.0 * eye[None] - jnp.einsum("kab,kbc->kac", innovation, guess, precision=high)
        guess = jnp.einsum("kab,kbc->kac", guess, residue, precision=high)
    return guess


def build_elements(transition, observe, noise_obs, measured, noise_state):
    high = lax.Precision.HIGHEST
    sensed = jnp.einsum("kon,nm->kom", observe, noise_state, precision=high)
    innovation = jnp.einsum("kon,kmn->kom", sensed, observe, precision=high)
    innovation = innovation + jax.vmap(jnp.diag)(noise_obs)
    inverse = invert_batch(innovation)
    seen = jnp.einsum("kon,knm->kom", observe, transition, precision=high)
    solved_seen = jnp.einsum("kop,kpm->kom", inverse, seen, precision=high)
    solved_sensed = jnp.einsum("kop,kpm->kom", inverse, sensed, precision=high)
    solved_value = jnp.einsum("kop,kp->ko", inverse, measured, precision=high)
    moved = transition - jnp.einsum("kon,kom->knm", sensed, solved_seen, precision=high)
    offset = jnp.einsum("kon,ko->kn", sensed, solved_value, precision=high)
    spread = noise_state[None] - jnp.einsum("kon,kom->knm", sensed, solved_sensed, precision=high)
    info_vec = jnp.einsum("kon,ko->kn", seen, solved_value, precision=high)
    info_mat = jnp.einsum("kon,kom->knm", seen, solved_seen, precision=high)
    return (moved, offset, spread, info_vec, info_mat)


def resolvent(spread, info_mat):
    width = spread.shape[0]
    eye = jnp.eye(width, dtype=jnp.float32)
    coupled = product(spread, info_mat)
    column_bound = jnp.max(jnp.sum(jnp.abs(coupled), axis=0))
    row_bound = jnp.max(jnp.sum(jnp.abs(coupled), axis=1))
    bound = jnp.minimum(column_bound, row_bound)
    system = eye + coupled
    guess = 2.0 / (2.0 + bound) * eye
    for sweep in range(8):
        guess = product(guess, 2.0 * eye - product(system, guess))
    return guess


def combine(first, second):
    move_a, off_a, spr_a, vec_a, mat_a = first
    move_b, off_b, spr_b, vec_b, mat_b = second
    settle = resolvent(spr_a, mat_b)
    mixer = product(move_b, settle)
    moved = product(mixer, move_a)
    offset = product(mixer, off_a + product(spr_a, vec_b)) + off_b
    spread = product(product(mixer, spr_a), move_b.T) + spr_b
    back = product(move_a.T, settle.T)
    info_vec = product(back, vec_b - product(mat_b, off_a)) + vec_a
    info_mat = product(product(back, mat_b), move_a) + mat_a
    return (moved, offset, spread, info_vec, info_mat)


def apply_state(first, second):
    move_a, off_a, spr_a, vec_a, mat_a = first
    move_b, off_b, spr_b, vec_b, mat_b = second
    mixer = product(move_b, resolvent(spr_a, mat_b))
    offset = product(mixer, off_a + product(spr_a, vec_b)) + off_b
    spread = product(product(mixer, spr_a), move_b.T) + spr_b
    return (offset, spread)


def on_device(transition, observe, noise_obs, measured, noise_state, prior_mean, prior_cov):
    elements = build_elements(transition, observe, noise_obs, measured, noise_state)
    width = noise_state.shape[0]
    square_zero = jnp.zeros((width, width), jnp.float32)
    vector_zero = jnp.zeros((width,), jnp.float32)
    identity = (
        jnp.eye(width, dtype=jnp.float32),
        vector_zero,
        square_zero,
        vector_zero,
        square_zero,
    )
    prior = (square_zero, prior_mean, prior_cov, vector_zero, square_zero)
    leading = tuple((part[0] for part in elements))
    folded = combine(prior, leading)
    is_first = jnp.logical_and(lax.axis_index(GRP) == 0, lax.axis_index(DEV) == 0)
    leading = jax.tree.map(
        lambda chosen, plain: jnp.where(is_first, chosen, plain), folded, leading
    )
    running = leading
    prefixes = [running]
    running = combine(running, tuple((part[1] for part in elements)))
    prefixes.append(running)
    entering = entering_2(running, GRP_DEV, combine, identity)
    results = [apply_state(entering, prefix) for prefix in prefixes]
    means = jnp.stack([item[0] for item in results])
    covs = jnp.stack([item[1] for item in results])
    return (means, covs)


def solution(mesh):
    split = Mesh(mesh.devices.reshape(4, 2, 4, 4), ("grp_0", "grp_1", "dev_0", "dev_1"))
    return jax.shard_map(
        on_device,
        mesh=split,
        in_specs=(
            P(GRP_DEV, None, None),
            P(GRP_DEV, None, None),
            P(GRP_DEV, None),
            P(GRP_DEV, None),
            P(),
            P(),
            P(),
        ),
        out_specs=(P(GRP_DEV, None), P(GRP_DEV, None, None)),
        check_vma=False,
    )
```

profile of v0, /device:TPU:0, one launch (start us, length us, event | category | flops | bytes accessed | tf_op | source)
XLA Modules:
  0.0 527.0 jit_solution(10950341743668132544)
XLA Ops:
  7.3 1.3 fusion.86
  8.6 1.6 fusion.479
  10.2 1.2 convolution_add_fusion.30
  15.5 1.5 fusion.481
  30.1 1.6 convolution_subtract_fusion
  42.4 1.1 convolution_add_fusion.28
  43.9 1.1 fusion.498
  45.5 1.1 convolution_add_fusion.26
  48.0 1.1 fusion.674
  51.5 10.2 %all-gather.20 = f32[4,1,256]{2,1,0:T(1,128)S(1)} all-gather(f32[1,1,256]{2,1,0:T(1,128)S(1)} %bitcast.1136), channel_id=14, replica_groups=mesh['grp_0'=4,'grp_1'=2,'dev_0'=4,'dev_1'=4] {'dev_1'}, dimensions={0}, use_global_device_ids=true | all-gather | bytes 5120 | tf_op jit(solution)/shard_map/all_gather | solution.py:23
  62.7 7.2 %all-gather.21 = f32[4,1,256]{2,1,0:T(1,128)S(1)} all-gather(f32[1,1,256]{2,1,0:T(1,128)S(1)} %bitcast.1151), channel_id=15, replica_groups=mesh['grp_0'=4,'grp_1'=2,'dev_0'=4,'dev_1'=4] {'dev_1'}, dimensions={0}, use_global_device_ids=true | all-gather | bytes 5120 | tf_op jit(solution)/shard_map/all_gather | solution.py:23
  80.4 16.0 %all-gather.38.cloned.1.call-done = f32[1024,256]{1,0:T(8,128)} async-done(((f32[256,256]{1,0:T(8,128)}), f32[1024,256]{1,0:T(8,128)}) %all-gather.38.cloned.1.call-update) | async-done | bytes 1048592 | tf_op jit(solution)/shard_map/all_gather | solution.py:23
  96.4 1.3 fusion.127
  98.8 23.7 %all-gather.42.cloned.1.call-done = f32[1024,256]{1,0:T(8,128)} async-done(((f32[256,256]{1,0:T(8,128)}), f32[1024,256]{1,0:T(8,128)}) %all-gather.42.cloned.1.call-update) | async-done | bytes 1048592 | tf_op jit(solution)/shard_map/all_gather | solution.py:23
  122.6 1.4 convolution_add_fusion.27
  133.9 1.3 fusion.544
  136.4 1.4 convolution_add_fusion.25
  147.4 1.3 fusion.543
  149.1 1.5 fusion.540
  151.0 1.4 convolution_add_fusion.24
  162.8 2.1 select_select_fusion.2
  173.8 1.1 convolution_add_fusion.22
  175.7 9.9 %all-gather.23 = f32[4,1,256]{2,1,0:T(1,128)S(1)} all-gather(f32[1,1,256]{2,1,0:T(1,128)S(1)} %bitcast.1292), channel_id=17, replica_groups=mesh['grp_0'=4,'grp_1'=2,'dev_0'=4,'dev_1'=4] {'dev_0'}, dimensions={0}, use_global_device_ids=true | all-gather | bytes 5120 | tf_op jit(solution)/shard_map/all_gather | solution.py:23
  195.2 1.1 fusion.74
  197.2 7.0 %all-gather.22 = f32[4,1,256]{2,1,0:T(1,128)S(1)} all-gather(f32[1,1,256]{2,1,0:T(1,128)S(1)} %bitcast.1263), channel_id=16, replica_groups=mesh['grp_0'=4,'grp_1'=2,'dev_0'=4,'dev_1'=4] {'dev_0'}, dimensions={0}, use_global_device_ids=true | all-gather | bytes 5120 | tf_op jit(solution)/shard_map/all_gather | solution.py:23
  205.9 1.1 fusion.541
  208.1 1.1 convolution_add_fusion.15
  219.6 8.3 %all-gather.44.cloned.1.call-done = f32[1024,256]{1,0:T(8,128)} async-done(((f32[256,256]{1,0:T(8,128)}), f32[1024,256]{1,0:T(8,128)}) %all-gather.44.cloned.1.call-update) | async-done | bytes 1048592 | tf_op jit(solution)/shard_map/all_gather | solution.py:23
  227.9 1.3 fusion.115
  229.9 24.7 %all-gather.48.cloned.1.call-done = f32[1024,256]{1,0:T(8,128)} async-done(((f32[256,256]{1,0:T(8,128)}), f32[1024,256]{1,0:T(8,128)}) %all-gather.48.cloned.1.call-update) | async-done | bytes 1048592 | tf_op jit(solution)/shard_map/all_gather | solution.py:23
  254.6 1.4 convolution_add_fusion.19
  265.8 1.3 fusion.590
  268.2 1.4 convolution_add_fusion.18
  278.9 1.3 fusion.589
  280.6 1.1 fusion.586
  282.9 1.4 convolution_add_fusion.17
  294.2 1.3 fusion.588
  298.2 1.2 fusion.77
  299.5 2.1 select_select_fusion.1
  312.4 1.1 fusion.607
  316.5 1.8 all-gather.24
  322.1 2.2 all-gather.7
  324.6 2.6 all-gather.6
  336.9 2.2 all-gather.8
  340.7 2.0 all-gather.25
  356.0 1.2 fusion.605
  357.4 1.2 convolution_add_fusion.8
  358.6 1.1 fusion.78
  359.7 2.2 select_select_fusion
  363.0 9.9 %all-gather.27 = f32[4,1,256]{2,1,0:T(1,128)S(1)} all-gather(f32[1,1,256]{2,1,0:T(1,128)S(1)} %bitcast.1291), channel_id=21, replica_groups=mesh['grp_0'=4,'grp_1'=2,'dev_0'=4,'dev_1'=4] {'grp_0'}, dimensions={0}, use_global_device_ids=true | all-gather | bytes 5120 | tf_op jit(solution)/shard_map/all_gather | solution.py:23
  382.7 7.0 %all-gather.26 = f32[4,1,256]{2,1,0:T(1,128)S(1)} all-gather(f32[1,1,256]{2,1,0:T(1,128)S(1)} %bitcast.1272), channel_id=20, replica_groups=mesh['grp_0'=4,'grp_1'=2,'dev_0'=4,'dev_1'=4] {'grp_0'}, dimensions={0}, use_global_device_ids=true | all-gather | bytes 5120 | tf_op jit(solution)/shard_map/all_gather | solution.py:23
  394.2 1.1 fusion.664
  395.4 1.1 fusion.662
  396.5 1.1 convolution_add_fusion.3
  406.7 8.4 %all-gather.50.cloned.1.call-done = f32[1024,256]{1,0:T(8,128)} async-done(((f32[256,256]{1,0:T(8,128)}), f32[1024,256]{1,0:T(8,128)}) %all-gather.50.cloned.1.call-update) | async-done | bytes 1048592 | tf_op jit(solution)/shard_map/all_gather | solution.py:23
  415.1 1.3 fusion.97
  417.2 24.1 %all-gather.54.cloned.1.call-done = f32[1024,256]{1,0:T(8,128)} async-done(((f32[256,256]{1,0:T(8,128)}), f32[1024,256]{1,0:T(8,128)}) %all-gather.54.cloned.1.call-update) | async-done | bytes 1048592 | tf_op jit(solution)/shard_map/all_gather | solution.py:23
  441.2 1.4 convolution_add_fusion.7
  443.0 1.5 abs_reduce_fusion.10
  454.3 1.4 convolution_add_fusion.6
  455.9 1.5 abs_reduce_fusion.8
  467.2 1.4 convolution_add_fusion.5
  468.9 1.5 abs_reduce_fusion.6
  480.7 1.4 fusion.4
  (818 shorter events, 249.0 us)
Async XLA Ops:
  7.2 10.5 %copy-start = (f32[256,256]{1,0:T(8,128)S(1)}, f32[256,256]{1,0:T(8,128)}, u32[]{:S(2)}) copy-start(f32[256,256]{1,0:T(8,128)} %param.13) | copy-start | bytes 786436
  7.2 63.1 %all-gather.40.cloned.1.call-start = ((), (), s32[]{:S(2)}) async-start(), calls=%async_computation.1 | async-start | bytes 1310720 | tf_op jit(solution)/shard_map/all_gather | solution.py:23
  10.2 5.1 copy-start.63
  11.4 5.6 %copy-start.59 = (f32[2,256,256]{2,1,0:T(8,128)S(1)}, f32[2,256,256]{2,1,0:T(8,128)}, u32[]{:S(2)}) copy-start(f32[2,256,256]{2,1,0:T(8,128)} %param.7) | copy-start | bytes 1572868
  27.5 2.5 copy-start.72
  30.0 12.3 %copy-start.42 = (f32[256,256]{1,0:T(8,128)}, f32[256,256]{1,0:T(8,128)S(1)}, u32[]{:S(2)}) copy-start(f32[256,256]{1,0:T(8,128)S(1)} %convolution_select_fusion) | copy-start | bytes 786436
  31.7 4.9 copy-start.61
  43.5 3.3 copy-start.74
  43.5 52.9 %all-gather.38.cloned.1.call-start = ((), (), s32[]{:S(2)}) async-start(), calls=%async_computation | async-start | bytes 1310720 | tf_op jit(solution)/shard_map/all_gather | solution.py:23
  43.9 5.8 %copy-start.73 = (f32[256]{0:T(256)S(1)}, f32[256]{0:T(256)}, u32[]{:S(2)}) copy-start(f32[256]{0:T(256)} %param.12) | copy-start | bytes 3076
  45.1 77.5 %all-gather.42.cloned.1.call-start = ((), (), s32[]{:S(2)}) async-start(), calls=%async_computation.2 | async-start | bytes 1310720 | tf_op jit(solution)/shard_map/all_gather | solution.py:23
  46.6 162.9 %all-gather.46.cloned.1.call-start = ((), (), s32[]{:S(2)}) async-start(), calls=%async_computation.4 | async-start | bytes 1310720 | tf_op jit(solution)/shard_map/all_gather | solution.py:23
  79.0 45.3 %copy-start.3 = (f32[1024,256]{1,0:T(8,128)S(1)}, f32[1024,256]{1,0:T(8,128)}, u32[]{:S(2)}) copy-start(f32[1024,256]{1,0:T(8,128)} %all-gather.40.cloned.1.call-done) | copy-start | bytes 3145732
  132.3 2.9 copy-start.10
  145.8 2.9 copy-start.11
  149.1 3.3 copy-start.4
  162.0 3.6 copy-start.19
  162.4 4.6 copy-start.40
  164.9 4.4 copy-start.8
  164.9 3.5 copy-start.5
  164.9 3.8 copy-start.26
  165.7 4.3 copy-start.32
  168.0 3.5 copy-start.45
  168.0 3.6 copy-start.34
  171.3 3.6 copy-start.51
  174.9 53.0 %all-gather.44.cloned.1.call-start = ((), (), s32[]{:S(2)}) async-start(), calls=%async_computation.3 | async-start | bytes 1310720 | tf_op jit(solution)/shard_map/all_gather | solution.py:23
  196.3 10.8 %copy-start.9 = (f32[256,256]{1,0:T(8,128)S(1)}, f32[256,256]{1,0:T(8,128)}, u32[]{:S(2)}) copy-start(f32[256,256]{1,0:T(8,128)} %copy-done.8) | copy-start | bytes 786436
  196.3 11.8 %copy-start.46 = (f32[256,256]{1,0:T(8,128)S(1)}, f32[256,256]{1,0:T(8,128)}, u32[]{:S(2)}) copy-start(f32[256,256]{1,0:T(8,128)} %copy-done.45) | copy-start | bytes 786436
  196.3 11.8 %copy-start.48 = (f32[256,256]{1,0:T(8,128)S(1)}, f32[256,256]{1,0:T(8,128)}, u32[]{:S(2)}) copy-start(f32[256,256]{1,0:T(8,128)} %convolution_add_fusion.22) | copy-start | bytes 786436
  196.3 11.8 %copy-start.52 = (f32[256,256]{1,0:T(8,128)S(1)}, f32[256,256]{1,0:T(8,128)}, u32[]{:S(2)}) copy-start(f32[256,256]{1,0:T(8,128)} %copy-done.51) | copy-start | bytes 786436
  196.3 11.8 %copy-start.54 = (f32[256,256]{1,0:T(8,128)S(1)}, f32[256,256]{1,0:T(8,128)}, u32[]{:S(2)}) copy-start(f32[256,256]{1,0:T(8,128)} %copy-done.53) | copy-start | bytes 786436
  204.2 50.3 %all-gather.48.cloned.1.call-start = ((), (), s32[]{:S(2)}) async-start(), calls=%async_computation.5 | async-start | bytes 1310720 | tf_op jit(solution)/shard_map/all_gather | solution.py:23
  209.2 188.4 %all-gather.52.cloned.1.call-start = ((), (), s32[]{:S(2)}) async-start(), calls=%async_computation.7 | async-start | bytes 1310720 | tf_op jit(solution)/shard_map/all_gather | solution.py:23
  218.2 37.8 %copy-start.2 = (f32[1024,256]{1,0:T(8,128)S(1)}, f32[1024,256]{1,0:T(8,128)}, u32[]{:S(2)}) copy-start(f32[1024,256]{1,0:T(8,128)} %all-gather.46.cloned.1.call-done) | copy-start | bytes 3145732
  229.2 25.3 %copy-start.20 = (f32[256,256]{1,0:T(8,128)}, f32[256,256]{1,0:T(8,128)S(1)}, u32[]{:S(2)}) copy-start(f32[256,256]{1,0:T(8,128)S(1)} %fusion.115) | copy-start | bytes 786436
  264.2 2.9 copy-start.13
  277.4 2.9 copy-start.14
  280.6 3.7 copy-start.6
  292.5 2.9 copy-start.15
  293.3 2.9 copy-start.21
  293.3 4.3 copy-start.7
  297.9 3.9 copy-start.17
  310.6 3.6 copy-start.37
  311.0 3.8 copy-start.30
  311.4 4.1 copy-start.33
  311.4 4.8 copy-start.31
  311.8 7.6 %copy-start.28 = (f32[256,256]{1,0:T(8,128)}, f32[256,256]{1,0:T(8,128)S(1)}, u32[]{:S(2)}) copy-start(f32[256,256]{1,0:T(8,128)S(1)} %fusion.583) | copy-start | bytes 786436
  320.5 3.8 copy-start.55
  320.8 3.8 copy-start.70
  321.2 3.3 copy-start.57
  334.3 2.6 copy-start.67
  336.2 6.4 %copy-start.50 = (f32[256,256]{1,0:T(8,128)S(1)}, f32[256,256]{1,0:T(8,128)}, u32[]{:S(2)}) copy-start(f32[256,256]{1,0:T(8,128)} %copy-done.49) | copy-start | bytes 786436
  336.2 6.4 %copy-start.56 = (f32[256,256]{1,0:T(8,128)S(1)}, f32[256,256]{1,0:T(8,128)}, u32[]{:S(2)}) copy-start(f32[256,256]{1,0:T(8,128)} %copy-done.55) | copy-start | bytes 786436
  336.2 6.4 %copy-start.58 = (f32[256,256]{1,0:T(8,128)S(1)}, f32[256,256]{1,0:T(8,128)}, u32[]{:S(2)}) copy-start(f32[256,256]{1,0:T(8,128)} %copy-done.57) | copy-start | bytes 786436
  336.3 6.4 %copy-start.71 = (f32[256,256]{1,0:T(8,128)S(1)}, f32[256,256]{1,0:T(8,128)}, u32[]{:S(2)}) copy-start(f32[256,256]{1,0:T(8,128)} %fusion.607) | copy-start | bytes 786436
  358.6 56.5 %all-gather.50.cloned.1.call-start = ((), (), s32[]{:S(2)}) async-start(), calls=%async_computation.6 | async-start | bytes 1310720 | tf_op jit(solution)/shard_map/all_gather | solution.py:23
  380.2 9.5 %copy-start.27 = (f32[256,256]{1,0:T(8,128)S(1)}, f32[256,256]{1,0:T(8,128)}, u32[]{:S(2)}) copy-start(f32[256,256]{1,0:T(8,128)} %fusion.541) | copy-start | bytes 786436
  380.2 9.5 %copy-start.29 = (f32[256,256]{1,0:T(8,128)S(1)}, f32[256,256]{1,0:T(8,128)}, u32[]{:S(2)}) copy-start(f32[256,256]{1,0:T(8,128)} %copy-done.28) | copy-start | bytes 786436
  391.6 49.6 %all-gather.54.cloned.1.call-start = ((), (), s32[]{:S(2)}) async-start(), calls=%async_computation.8 | async-start | bytes 1310720 | tf_op jit(solution)/shard_map/all_gather | solution.py:23
  392.1 4.4 copy-start.47
  478.9 3.2 copy-start.69
  493.1 3.3 copy-start.36
  508.0 2.4 copy-start.44
  516.9 3.3 copy-start.1
  (20 other events, 33.4 us)
Sparse Core Ops, SparseCore 0:
  43.6 26.6 all-gather.39
  71.9 24.4 all-gather.37
  98.1 24.4 all-gather.41
  175.1 24.6 all-gather.45
  204.4 23.5 all-gather.43
  230.0 24.5 all-gather.47
  358.7 24.2 all-gather.51
  391.7 23.3 all-gather.49
  416.8 24.4 all-gather.53
where the time goes:
time: 537 us; the launch traced here: 527 us
  matrix products  272 us (51%)
  waiting for transfers between devices  106 us (20%)
  blocking collectives  61.9 us (12%)
  between operations  48.1 us (9%)
  other arithmetic  33.4 us (6%)
    dot_general x564, matrix products, product(): return jnp.matmul(left, right, precision=lax.Precision.HIGHEST)  259 us
    all_gather x9, waiting for transfers between devices, entering_2(): pieces = jax.tree.map(lambda part: lax.all_gather(part, axis), so_far)  106 us
    all_gather x11, blocking collectives, entering_2(): pieces = jax.tree.map(lambda part: lax.all_gather(part, axis), so_far)  61.9 us
    reduce_max x18, other arithmetic, resolvent(): row_bound = jnp.max(jnp.sum(jnp.abs(coupled), axis=1))  11.2 us
    reduce_max x18, other arithmetic, resolvent(): column_bound = jnp.max(jnp.sum(jnp.abs(coupled), axis=0))  11 us
  transfers between devices with their start and end apart: 9, of which 7 were waited for; matrix products, arithmetic and copies ran while one was open for 14% of the time, Pallas kernels for 0%

commit v1 on v0

v1 whole, which is shorter than its diff:
```python
import functools

import jax
import jax.numpy as jnp
from jax import lax
from jax.experimental import pallas as pl
from jax.experimental.pallas import tpu as pltpu
from jax.sharding import Mesh
from jax.sharding import PartitionSpec as P


AXES = ("x", "c", "z", "y")
N = 256
O = 64
V = 16
ROWS = 2 * N + V
TOL = 1e-6
F32 = jnp.float32
BF16 = jnp.bfloat16


def split(x):
    high = x.astype(BF16)
    low = (x - high.astype(F32)).astype(BF16)
    return high, low


def dot3(a, b, dims=((1,), (0,))):
    def one(p, q):
        return lax.dot_general(p, q, (dims, ((), ())), preferred_element_type=F32)

    return one(a[0], b[0]) + (one(a[0], b[1]) + one(a[1], b[0]))


def rows(*parts):
    return tuple(jnp.concatenate([p[i] for p in parts], axis=0) for i in range(2))


def row_col(n):
    return (
        lax.broadcasted_iota(jnp.int32, (n, n), 0),
        lax.broadcasted_iota(jnp.int32, (n, n), 1),
    )


def resolvents(coupled, stacks):
    n = coupled[0].shape[0]
    row, col = row_col(n)
    eye = jnp.where(row == col, 1.0, 0.0).astype(F32)
    rate = jnp.float32(0.0)
    for each, stack in zip(coupled, stacks):
        size = jnp.abs(each)
        bound = jnp.minimum(
            jnp.max(jnp.sum(size, axis=0, keepdims=True)), jnp.sqrt(jnp.sum(size * size))
        )
        scale = 2.0 / (2.0 + bound)
        error = eye - scale * (eye + each)
        stack[0:n, :] = scale * (eye + error)
        stack[n:, :] = error
        rate = jnp.maximum(rate, jnp.minimum(bound * scale * 0.5, 0.9999998))

    @pl.when(rate * rate > TOL)
    def _():
        for stack in stacks:
            factor = split(stack[n:, :])
            stack[n:, :] = dot3(factor, factor)

    def sweep(rate):
        for stack in stacks:
            both = split(stack[...])
            fresh = dot3(both, (both[0][n:], both[1][n:]))
            stack[0:n, :] = stack[0:n, :] + fresh[0:n]
            stack[n:, :] = fresh[n:]
        return rate * rate

    lax.while_loop(lambda rate: rate > TOL, sweep, rate * rate)
    return [stack[0:n, :] for stack in stacks]


def unpack(ref):
    move = ref[0:N, :]
    both = ref[N : 2 * N, :]
    vecs = ref[2 * N :, :]
    row, col = row_col(N)
    turned = both.T
    spread = jnp.where(row <= col, both, turned)
    info = jnp.where(row == col, vecs[2:3, :], jnp.where(row > col, both, turned))
    return move, spread, info, vecs


def pack(ref, move, spread, info, offset, info_vec):
    row, col = row_col(N)
    ref[0:N, :] = move
    ref[N : 2 * N, :] = jnp.where(row <= col, spread, info)
    diag = jnp.sum(jnp.where(row == col, info, 0.0), axis=0, keepdims=True)
    place = lax.broadcasted_iota(jnp.int32, (V, N), 0)
    ref[2 * N :, :] = jnp.where(
        place == 0, offset, jnp.where(place == 1, info_vec, jnp.where(place == 2, diag, 0.0))
    )


def combine(firsts, seconds, stacks):
    pairs = []
    for (move_a, spr_a, mat_a, vecs_a), (move_b, spr_b, mat_b, vecs_b) in zip(firsts, seconds):
        move_a2, spr_a2, mat_b2 = split(move_a), split(spr_a), split(mat_b)
        up = dot3(rows(mat_b2, split(vecs_b)), spr_a2)
        seen = dot3(rows(move_a2, split(vecs_a)), mat_b2)
        pairs.append((up, seen, move_a2, spr_a2))
    settled = resolvents([pair[0][0:N] for pair in pairs], stacks)
    out = []
    for first, second, pair, settle in zip(firsts, seconds, pairs, settled):
        up, seen, move_a2, spr_a2 = pair
        move_b, spr_b, _, vecs_b = second
        _, _, mat_a, vecs_a = first
        row_r = vecs_a + up[N + 1 : N + 2]
        row_s = vecs_b[1:2] - seen[N : N + 1]
        third2 = split(dot3(rows(move_a2, spr_a2, split(row_r)), split(settle)))
        fourth = dot3(third2, split(move_b))
        back2 = (third2[0][0:N], third2[1][0:N])
        fifth = dot3(
            rows(split(seen[0:N]), split(jnp.broadcast_to(row_s, (V, N)))), back2, ((1,), (1,))
        )
        spread = dot3(split(move_b.T), split(fourth[N : 2 * N])) + spr_b
        out.append(
            (
                fourth[0:N],
                spread,
                fifth[0:N] + mat_a,
                fourth[2 * N : 2 * N + 1] + vecs_b[0:1],
                fifth[N : N + 1] + vecs_a[1:2],
            )
        )
    return out


def apply_state(mean, cov, seconds, stacks):
    cov2 = split(cov)
    ups = [dot3(rows(split(mat_b), split(vecs_b)), cov2) for _, _, mat_b, vecs_b in seconds]
    settled = resolvents([up[0:N] for up in ups], stacks)
    out = []
    for (move_b, spr_b, _, vecs_b), up, settle in zip(seconds, ups, settled):
        row_r = mean + up[N + 1 : N + 2]
        third = dot3(rows(cov2, split(row_r)), split(settle))
        fourth = dot3(split(third), split(move_b))
        spread = dot3(split(move_b.T), split(fourth[0:N])) + spr_b
        out.append((fourth[N:] + vecs_b[0:1], spread))
    return out


def build_kernel(
    trans_in, obs_in, noise_in, meas_in, state_in, two_ref, pair, trans, obs, noise, meas,
    noise_state, sems, stack, small_a, small_b,
):
    copies = [
        pltpu.make_async_copy(source, target, sems.at[k])
        for k, (source, target) in enumerate(
            (
                (obs_in, obs),
                (state_in, noise_state),
                (trans_in, trans),
                (noise_in, noise),
                (meas_in, meas),
            )
        )
    ]
    for copy in copies:
        copy.start()
    for copy in copies:
        copy.wait()
    state = noise_state[...]
    state2 = split(state)
    place = lax.broadcasted_iota(jnp.int32, (V, N), 0)
    row, col = row_col(O)
    parts = []
    for k in range(2):
        sensor2 = split(obs[k])
        sensed = dot3(sensor2, state2)
        seen = dot3(sensor2, split(trans[k]))
        inner = dot3(split(sensed), sensor2, ((1,), (1,)))
        variance = noise[k : k + 1, :]
        root = lax.rsqrt(variance)
        root = root * (1.5 - 0.5 * variance * root * root)
        root_col = jnp.sum(jnp.where(row == col, root, 0.0), axis=1, keepdims=True)
        parts.append((sensed, seen, root_col * inner * root, root, root_col))
    inverses = resolvents([part[2] for part in parts], (small_a, small_b))
    steps = []
    for k in range(2):
        sensed, seen, _, root, root_col = parts[k]
        inverse2 = split(root_col * inverses[k] * root)
        pair2 = split(jnp.concatenate([seen, sensed], axis=1))
        solved = dot3(inverse2, pair2)
        value = split(jnp.broadcast_to(meas[k : k + 1, :], (V, O)))
        vec = dot3(split(dot3(value, inverse2)), pair2)
        turned2 = split(jnp.concatenate([seen.T, sensed.T], axis=0))
        full = dot3(turned2, split(solved))
        vecs = jnp.where(place == 0, vec[0:1, N:], jnp.where(place == 1, vec[0:1, 0:N], 0.0))
        steps.append((trans[k].T - full[0:N, N:], state - full[N:, N:], full[0:N, 0:N], vecs))
    move, spread, info, vecs = steps[0]
    pack(pair.at[0], move, spread, info, vecs[0:1], vecs[1:2])
    pack(two_ref, *combine(steps[0:1], steps[1:2], [stack])[0])
    pair[1] = two_ref[...]


def upper(here, axis, step):
    shift = {"x": 5, "c": 4, "z": 2, "y": 0}[axis] + step // 2
    return ((here[0] >> shift) & 1) == 1


def order(flag, mine, theirs, first, second):
    first[...] = jnp.where(flag, theirs[...], mine[...])
    second[...] = jnp.where(flag, mine[...], theirs[...])
    return unpack(first), unpack(second)


def total_kernel(axis, step, here, mine, theirs, after, out, first, second, stack):
    a, b = order(upper(here, axis, step), mine, theirs, first, second)
    pack(out, *combine([a], [b], [stack])[0])


def core_kernel(here, mine, theirs, after, out, half, first, second, stack):
    total_kernel("c", 1, here, mine, theirs, after, out, first, second, stack)
    half[...] = jnp.where(upper(here, "c", 1), out[HALF:, :], out[0:HALF, :])


def slow_kernel(axis, step, here, theirs, pair, after, out, stack):
    flag = upper(here, axis, step)

    @pl.when(flag)
    def _():
        def one(k, carry):
            pack(out.at[k], *combine([unpack(theirs)], [unpack(pair.at[k])], [stack])[0])
            return carry

        lax.fori_loop(0, 2, one, 0)

    @pl.when(jnp.logical_not(flag))
    def _():
        out[...] = pair[...]


def merge_kernel(here, late, early, after, out, stack):
    z_up, c_up = upper(here, "z", 2), upper(here, "c", 1)

    @pl.when(jnp.logical_and(z_up, c_up))
    def _():
        pack(out, *combine([unpack(late)], [unpack(early)], [stack])[0])

    @pl.when(jnp.logical_not(z_up))
    def _():
        out[...] = late[...]

    @pl.when(jnp.logical_not(c_up))
    def _():
        out[...] = early[...]


def steps_kernel(here, theirs, low, pair, after, out, whole, stack, stack_b):
    x_up = upper(here, "x", 1)
    held = jnp.logical_or(upper(here, "z", 2), upper(here, "c", 1))

    @pl.when(jnp.logical_and(x_up, held))
    def _():
        pack(whole, *combine([unpack(theirs)], [unpack(low)], [stack])[0])

    @pl.when(jnp.logical_not(x_up))
    def _():
        whole[...] = low[...]

    @pl.when(jnp.logical_not(held))
    def _():
        whole[...] = theirs[...]

    @pl.when(jnp.logical_or(x_up, held))
    def _():
        first = unpack(whole)
        done = combine(
            [first, first], [unpack(pair.at[0]), unpack(pair.at[1])], [stack, stack_b]
        )
        pack(out.at[0], *done[0])
        pack(out.at[1], *done[1])

    @pl.when(jnp.logical_not(jnp.logical_or(x_up, held)))
    def _():
        out[...] = pair[...]


def prior_kernel(whole, mean, cov, mean_out, cov_out, stack):
    state = jnp.broadcast_to(mean[...], (V, N))
    mean_out[...], cov_out[...] = apply_state(state, cov[...], [unpack(whole)], [stack])[0]


HN = N // 2


def second_kernel(here, mine, other, mean, cov, after, theirs, out, stack):
    flag = upper(here, "c", 1)
    theirs[0:HALF, :] = jnp.where(flag, other[...], mine[...])
    theirs[HALF:, :] = jnp.where(flag, mine[...], other[...])
    mean_b, cov_b = apply_state(mean[...], cov[...], [unpack(theirs)], [stack])[0]
    row, col = row_col(HN)
    last = cov_b[HN:, HN:]
    out[0:HN, 0:HN] = jnp.where(row <= col, cov_b[0:HN, 0:HN], last)
    out[0:HN, HN:] = cov_b[0:HN, HN:]
    diag = jnp.sum(jnp.where(row == col, last, 0.0), axis=0, keepdims=True)
    out[HN : HN + 8, :] = mean_b[0:8]
    out[HN + 8 :, :] = jnp.broadcast_to(jnp.concatenate([diag, diag], axis=1), (8, N))


def final_kernel(here, state_a, state_b, mean, cov, pair, means, covs, packed, prior, stack, stack_b):
    packed[...] = jnp.where(upper(here, "x", 1), state_b[...], state_a[...])
    flag = upper(here, "x", 2)
    row, col = row_col(HN)
    mixed = packed[0:HN, 0:HN]
    turned = mixed.T
    side = packed[0:HN, HN:]
    last = jnp.where(
        row == col, packed[HN + 8 : HN + 9, 0:HN], jnp.where(row > col, mixed, turned)
    )
    prior[0:HN, 0:HN] = jnp.where(flag, jnp.where(row <= col, mixed, turned), cov[0:HN, 0:HN])
    prior[0:HN, HN:] = jnp.where(flag, side, cov[0:HN, HN:])
    prior[HN:, 0:HN] = jnp.where(flag, side.T, cov[HN:, 0:HN])
    prior[HN:, HN:] = jnp.where(flag, last, cov[HN:, HN:])
    mean_in = jnp.broadcast_to(jnp.where(flag, packed[HN : HN + 1, :], mean[...]), (V, N))
    done = apply_state(mean_in, prior[...], [unpack(pair.at[0]), unpack(pair.at[1])], [stack, stack_b])
    for k in range(2):
        means[k : k + 1, :] = done[k][0][0:1]
        covs[k] = done[k][1]


def call(kernel, places, outs, scratch, products):
    spaces = {"s": pltpu.SMEM, "v": pltpu.VMEM, "a": pl.ANY, "h": pltpu.HBM}
    vmem = pl.BlockSpec(memory_space=pltpu.VMEM)
    shapes = [jax.ShapeDtypeStruct(shape, F32) for shape in outs]
    buffers = [pltpu.VMEM(shape, F32) if isinstance(shape, tuple) else shape for shape in scratch]
    return pl.pallas_call(
        kernel,
        out_shape=shapes if len(shapes) > 1 else shapes[0],
        in_specs=[pl.BlockSpec(memory_space=spaces[place]) for place in places],
        out_specs=[vmem] * len(shapes) if len(shapes) > 1 else vmem,
        scratch_shapes=buffers,
        compiler_params=pltpu.CompilerParams(vmem_limit_bytes=24 << 20),
        cost_estimate=pl.CostEstimate(
            flops=products * 6 * N**3, transcendentals=0, bytes_accessed=8 * N * N
        ),
    )


ELEMENT = (ROWS, N)
PAIR = (2, ROWS, N)
HALF = ROWS // 2
STACK = (2 * N, N)
PACKED = (HN + 16, N)


def on_device(transition, observe, noise_obs, measured, noise_state, prior_mean, prior_cov):
    here = lax.axis_index(AXES).astype(jnp.int32)[None]
    mean = prior_mean[None]

    def swap(part, axis, step):
        size = lax.axis_size(axis)
        return lax.ppermute(part, axis, [(k, k ^ step) for k in range(size)])

    def total(axis, step, mine, theirs, after):
        kernel = functools.partial(total_kernel, axis, step)
        run = call(kernel, "svva", [ELEMENT], [ELEMENT, ELEMENT, STACK], 14)
        return run(here, mine, theirs, after)

    def slow(axis, step, theirs, pair, after):
        kernel = functools.partial(slow_kernel, axis, step)
        return call(kernel, "svva", [PAIR], [STACK], 28)(here, theirs, pair, after)

    merge = call(merge_kernel, "svva", [ELEMENT], [STACK], 14)
    steps = call(steps_kernel, "svvva", [PAIR], [ELEMENT, STACK, STACK], 42)

    inputs = [(2, N, N), (2, O, N), (2, O), (2, O), (N, N)]
    build = call(
        build_kernel,
        "hhhhh",
        [ELEMENT, PAIR],
        inputs + [pltpu.SemaphoreType.DMA((5,)), STACK, (2 * O, O), (2 * O, O)],
        30,
    )
    core = call(core_kernel, "svva", [ELEMENT, (HALF, N)], [ELEMENT, ELEMENT, STACK], 14)
    prior = call(prior_kernel, "vvv", [(V, N), (N, N)], [STACK], 14)
    second = call(second_kernel, "svvvva", [ELEMENT, PACKED], [STACK], 14)
    final = call(final_kernel, "svvvvv", [(2, N), (2, N, N)], [PACKED, (N, N), STACK, STACK], 24)

    arrays = (transition, observe, noise_obs, measured, noise_state)
    whole, pair = build(*(pltpu.with_memory_space_constraint(a, pltpu.HBM) for a in arrays))
    y1 = swap(whole, "y", 1)
    whole = total("y", 1, whole, y1, here)
    y2 = swap(whole, "y", 2)
    pair = slow("y", 1, y1, pair, here)
    whole = total("y", 2, whole, y2, pair)
    z1 = swap(whole, "z", 1)
    pair = slow("y", 2, y2, pair, here)
    whole = total("z", 1, whole, z1, pair)
    z2 = swap(whole, "z", 2)
    pair = slow("z", 1, z1, pair, here)
    whole = total("z", 2, whole, z2, pair)
    c1 = swap(whole, "c", 1)
    whole, half = core(here, whole, c1, here)
    x1 = swap(half, "x", 1)
    mean_a, cov_a = prior(whole, mean, prior_cov)
    low = merge(here, c1, z2, mean_a)
    x1_other = swap(x1, "c", 1)
    theirs, packed = second(here, x1, x1_other, mean_a, cov_a, low)
    state_a = lax.ppermute(packed, "x", [(0, 2)])
    state_b = lax.ppermute(packed, "x", [(0, 3)])
    pair = steps(here, theirs, low, pair, packed)
    return final(here, state_a, state_b, mean, prior_cov, pair)


def solution(mesh):
    split_mesh = Mesh(mesh.devices.reshape(4, 2, 4, 4), AXES)
    return jax.shard_map(
        on_device,
        mesh=split_mesh,
        in_specs=(
            P(AXES, None, None),
            P(AXES, None, None),
            P(AXES, None),
            P(AXES, None),
            P(),
            P(),
            P(),
        ),
        out_specs=(P(AXES, None), P(AXES, None, None)),
        check_vma=False,
    )
```

time: 537 us -> 110 us (0.20)
  the two profiles are of different devices: /device:TPU:0 before, /device:TPU:127 now
where the time goes in v1:
time: 110 us
  Pallas kernels  54.3 us (49%)
  waiting for transfers between devices  45 us (41%)
  starting transfers between devices  10.1 us (9%)
    ppermute x7, waiting for transfers between devices, swap(): return lax.ppermute(part, axis, [(k, k ^ step) for k in range(size)])  45 us
    pallas_call x3, Pallas kernels, slow(): return call(kernel, 'svva', [PAIR], [STACK], 28)(here, theirs, pair, after)  12.4 us
    pallas_call x4, Pallas kernels, total(): return run(here, mine, theirs, after)  8.94 us
    pallas_call x1, Pallas kernels, on_device(): pair = steps(here, theirs, low, pair, packed)  8.18 us
    ppermute x7, starting transfers between devices, swap(): return lax.ppermute(part, axis, [(k, k ^ step) for k in range(size)])  8.16 us
    pallas_call x1, Pallas kernels, on_device(): return final(here, state_a, state_b, mean, prior_cov, pair)  7.1 us
    pallas_call x1, Pallas kernels, on_device(): build(*(pltpu.with_memory_space_constraint(a, pltpu.HBM) for a in arrays))  5.11 us
    pallas_call x1, Pallas kernels, on_device(): theirs, packed = second(here, x1, x1_other, mean_a, cov_a, low)  3.68 us
  transfers between devices with their start and end apart: 9, of which 6 were waited for; matrix products, arithmetic and copies ran while one was open for 0% of the time, Pallas kernels for 24%

profile of v1, /device:TPU:127, one launch (start us, length us, event | category | flops | bytes accessed | tf_op | source)
XLA Modules:
  0.0 110.2 jit_solution(17679819637017880982)
XLA Ops:
  0.6 5.1 %shard_map.86 = (f32[528,256]{1,0:T(8,128)S(1)}, f32[2,528,256]{2,1,0:T(8,128)S(1)}) custom-call(f32[2,256,256]{2,1,0:T(8,128)} %trans_in.1, f32[2,64,256]{2,1,0:T(8,128)} %obs_in.1, f32[2,64]{1,0:T(2,128)} %noise_in.1, f32[2,64]{1,0:T(2,128)} %meas_in.1, f32[256,256]{1,0:T(8,128)} %state_in.1), custom_call_target="tpu_custom_call" | custom-call | flops 3019898880 | bytes 524288 | tf_op jit(solution)/shard_map/pallas_call | solution.py:389
  5.7 0.5 collective-permute-start
  6.3 12.7 %collective-permute-done.theirs = f32[528,256]{1,0:T(8,128)S(1)} collective-permute-done((f32[528,256]{1,0:T(8,128)S(1)}, f32[528,256]{1,0:T(8,128)S(1)}, u32[]{:S(2)}, u32[]{:S(2)}) %collective-permute-start) | collective-permute-done | bytes 540704 | tf_op jit(solution)/shard_map/ppermute | solution.py:361
  19.0 2.1 %shard_map.87.mine = f32[528,256]{1,0:T(8,128)S(1)} custom-call(s32[1]{0:T(128)} %bitcast.here.after, f32[528,256]{1,0:T(8,128)S(1)} %get-tuple-element.10.mine, f32[528,256]{1,0:T(8,128)S(1)} %collective-permute-done.theirs, s32[1]{0:T(128)} %bitcast.here.after), custom_call_target="tpu_custom_call" | custom-call | flops 1409286144 | bytes 524288 | tf_op jit(solution)/shard_map/pallas_call | solution.py:366
  21.1 1.0 collective-permute-start.1
  22.1 4.1 %shard_map.88.after.pair = f32[2,528,256]{2,1,0:T(8,128)S(1)} custom-call(s32[1]{0:T(128)} %bitcast.here.after, f32[528,256]{1,0:T(8,128)S(1)} %collective-permute-done.theirs, f32[2,528,256]{2,1,0:T(8,128)S(1)} %get-tuple-element.11.pair, s32[1]{0:T(128)} %bitcast.here.after), custom_call_target="tpu_custom_call" | custom-call | flops 2818572288 | bytes 524288 | tf_op jit(solution)/shard_map/pallas_call | solution.py:370
  26.2 8.8 %collective-permute-done.1.theirs = f32[528,256]{1,0:T(8,128)S(1)} collective-permute-done((f32[528,256]{1,0:T(8,128)S(1)}, f32[528,256]{1,0:T(8,128)S(1)}, u32[]{:S(2)}, u32[]{:S(2)}) %collective-permute-start.1) | collective-permute-done | bytes 540704 | tf_op jit(solution)/shard_map/ppermute | solution.py:361
  35.0 2.1 %shard_map.89.mine = f32[528,256]{1,0:T(8,128)S(1)} custom-call(s32[1]{0:T(128)} %bitcast.here.after, f32[528,256]{1,0:T(8,128)S(1)} %shard_map.87.mine, f32[528,256]{1,0:T(8,128)S(1)} %collective-permute-done.1.theirs, f32[2,528,256]{2,1,0:T(8,128)S(1)} %shard_map.88.after.pair), custom_call_target="tpu_custom_call" | custom-call | flops 1409286144 | bytes 524288 | tf_op jit(solution)/shard_map/pallas_call | solution.py:366
  37.0 0.2 collective-permute-start.2
  37.2 4.2 %shard_map.90.after.pair = f32[2,528,256]{2,1,0:T(8,128)S(1)} custom-call(s32[1]{0:T(128)} %bitcast.here.after, f32[528,256]{1,0:T(8,128)S(1)} %collective-permute-done.1.theirs, f32[2,528,256]{2,1,0:T(8,128)S(1)} %shard_map.88.after.pair, s32[1]{0:T(128)} %bitcast.here.after), custom_call_target="tpu_custom_call" | custom-call | flops 2818572288 | bytes 524288 | tf_op jit(solution)/shard_map/pallas_call | solution.py:370
  41.4 7.1 %collective-permute-done.2.theirs = f32[528,256]{1,0:T(8,128)S(1)} collective-permute-done((f32[528,256]{1,0:T(8,128)S(1)}, f32[528,256]{1,0:T(8,128)S(1)}, u32[]{:S(2)}, u32[]{:S(2)}) %collective-permute-start.2) | collective-permute-done | bytes 540704 | tf_op jit(solution)/shard_map/ppermute | solution.py:361
  48.6 2.1 %shard_map.91.mine = f32[528,256]{1,0:T(8,128)S(1)} custom-call(s32[1]{0:T(128)} %bitcast.here.after, f32[528,256]{1,0:T(8,128)S(1)} %shard_map.89.mine, f32[528,256]{1,0:T(8,128)S(1)} %collective-permute-done.2.theirs, f32[2,528,256]{2,1,0:T(8,128)S(1)} %shard_map.90.after.pair), custom_call_target="tpu_custom_call" | custom-call | flops 1409286144 | bytes 524288 | tf_op jit(solution)/shard_map/pallas_call | solution.py:366
  50.6 0.3 collective-permute-start.3
  51.0 4.1 %shard_map.92.after.pair = f32[2,528,256]{2,1,0:T(8,128)S(1)} custom-call(s32[1]{0:T(128)} %bitcast.here.after, f32[528,256]{1,0:T(8,128)S(1)} %collective-permute-done.2.theirs, f32[2,528,256]{2,1,0:T(8,128)S(1)} %shard_map.90.after.pair, s32[1]{0:T(128)} %bitcast.here.after), custom_call_target="tpu_custom_call" | custom-call | flops 2818572288 | bytes 524288 | tf_op jit(solution)/shard_map/pallas_call | solution.py:370
  55.1 7.7 %collective-permute-done.3.theirs.early = f32[528,256]{1,0:T(8,128)S(1)} collective-permute-done((f32[528,256]{1,0:T(8,128)S(1)}, f32[528,256]{1,0:T(8,128)S(1)}, u32[]{:S(2)}, u32[]{:S(2)}) %collective-permute-start.3) | collective-permute-done | bytes 540704 | tf_op jit(solution)/shard_map/ppermute | solution.py:361
  62.8 2.7 %shard_map.93.mine = f32[528,256]{1,0:T(8,128)S(1)} custom-call(s32[1]{0:T(128)} %bitcast.here.after, f32[528,256]{1,0:T(8,128)S(1)} %shard_map.91.mine, f32[528,256]{1,0:T(8,128)S(1)} %collective-permute-done.3.theirs.early, f32[2,528,256]{2,1,0:T(8,128)S(1)} %shard_map.92.after.pair), custom_call_target="tpu_custom_call" | custom-call | flops 1409286144 | bytes 524288 | tf_op jit(solution)/shard_map/pallas_call | solution.py:366
  65.5 0.0 copy-start
  65.6 0.0 copy-start.1
  65.6 4.2 %collective-permute-start.4 = (f32[528,256]{1,0:T(8,128)S(1)}, f32[528,256]{1,0:T(8,128)S(1)}, u32[]{:S(2)}, u32[]{:S(2)}) collective-permute-start(f32[528,256]{1,0:T(8,128)S(1)} %shard_map.93.mine), channel_id=1, source_target_pairs={{0,16},{16,0},{1,17},{17,1},{2,18},{18,2},{3,19},{19,3},{4,20},{20... | collective-permute-start | bytes 1622024 | tf_op jit(solution)/shard_map/ppermute | solution.py:361
  69.8 1.6 %collective-permute-done.4.theirs.late = f32[528,256]{1,0:T(8,128)S(1)} collective-permute-done((f32[528,256]{1,0:T(8,128)S(1)}, f32[528,256]{1,0:T(8,128)S(1)}, u32[]{:S(2)}, u32[]{:S(2)}) %collective-permute-start.4) | collective-permute-done | bytes 540704 | tf_op jit(solution)/shard_map/ppermute | solution.py:361
  71.3 2.7 %shard_map.94 = (f32[528,256]{1,0:T(8,128)S(1)}, f32[264,256]{1,0:T(8,128)S(1)}) custom-call(s32[1]{0:T(128)} %bitcast.here.after, f32[528,256]{1,0:T(8,128)S(1)} %shard_map.93.mine, f32[528,256]{1,0:T(8,128)S(1)} %collective-permute-done.4.theirs.late, s32[1]{0:T(128)} %bitcast.here.after), custom_call_target="tpu_custom_call" | custom-call | flops 1409286144 | bytes 524288 | tf_op jit(solution)/shard_map/pallas_call | solution.py:402
  74.1 0.6 collective-permute-start.5
  74.7 7.1 %collective-permute-done.5.mine = f32[264,256]{1,0:T(8,128)S(1)} collective-permute-done((f32[264,256]{1,0:T(8,128)S(1)}, f32[264,256]{1,0:T(8,128)S(1)}, u32[]{:S(2)}, u32[]{:S(2)}) %collective-permute-start.5) | collective-permute-done | bytes 270368 | tf_op jit(solution)/shard_map/ppermute | solution.py:361
  81.8 1.2 %collective-permute-start.6 = (f32[264,256]{1,0:T(8,128)S(1)}, f32[264,256]{1,0:T(8,128)S(1)}, u32[]{:S(2)}, u32[]{:S(2)}) collective-permute-start(f32[264,256]{1,0:T(8,128)S(1)} %collective-permute-done.5.mine), channel_id=1, source_target_pairs={{0,16},{16,0},{1,17},{17,1},{2,18},{18,2},{3,19},{19,3},{4,20},{20... | collective-permute-start | bytes 811016 | tf_op jit(solution)/shard_map/ppermute | solution.py:361
  83.0 0.0 copy-done
  83.0 0.0 copy-done.1
  83.1 3.5 %shard_map.95 = (f32[16,256]{1,0:T(8,128)S(1)}, f32[256,256]{1,0:T(8,128)S(1)}) custom-call(f32[528,256]{1,0:T(8,128)S(1)} %get-tuple-element.13.whole, f32[1,256]{1,0:T(1,128)S(1)} %bitcast.2, f32[256,256]{1,0:T(8,128)S(1)} %copy-done), custom_call_target="tpu_custom_call" | custom-call | flops 1409286144 | bytes 524288 | tf_op jit(solution)/shard_map/pallas_call | solution.py:404
  86.5 2.7 %shard_map.96.after.low = f32[528,256]{1,0:T(8,128)S(1)} custom-call(s32[1]{0:T(128)} %bitcast.here.after, f32[528,256]{1,0:T(8,128)S(1)} %collective-permute-done.4.theirs.late, f32[528,256]{1,0:T(8,128)S(1)} %collective-permute-done.3.theirs.early, f32[16,256]{1,0:T(8,128)S(1)} %get-tuple-element.14.after.mean), custom_call_target="tpu_custom_call" | custom-call | flops 1409286144 | bytes 524288 | tf_op jit(solution)/shard_map/pallas_call | solution.py:405
  89.2 0.0 collective-permute-done.6.other
  89.3 3.7 %shard_map.97 = (f32[528,256]{1,0:T(8,128)S(1)}, f32[144,256]{1,0:T(8,128)S(1)}) custom-call(s32[1]{0:T(128)} %bitcast.here.after, f32[264,256]{1,0:T(8,128)S(1)} %collective-permute-done.5.mine, f32[264,256]{1,0:T(8,128)S(1)} %collective-permute-done.6.other, f32[16,256]{1,0:T(8,128)S(1)} %get-tuple-element.14.after.mean, ...), custom_call_target="tpu_custom_call" | custom-call | flops 1409286144 | bytes 524288 | tf_op jit(solution)/shard_map/pallas_call | solution.py:407
  92.9 1.3 %collective-permute-start.8 = (f32[144,256]{1,0:T(8,128)S(1)}, f32[144,256]{1,0:T(8,128)S(1)}, u32[]{:S(2)}, u32[]{:S(2)}) collective-permute-start(f32[144,256]{1,0:T(8,128)S(1)} %get-tuple-element.16.after), channel_id=1, source_target_pairs={{0,96},{1,97},{2,98},{3,99},{4,100},{5,101},{6,102},{7,103},{8,104... | collective-permute-start | bytes 442376 | tf_op jit(solution)/shard_map/ppermute | solution.py:409
  94.2 0.7 collective-permute-start.7
  94.9 8.2 %shard_map.98.pair = f32[2,528,256]{2,1,0:T(8,128)S(1)} custom-call(s32[1]{0:T(128)} %bitcast.here.after, f32[528,256]{1,0:T(8,128)S(1)} %get-tuple-element.17.theirs, f32[528,256]{1,0:T(8,128)S(1)} %shard_map.96.after.low, f32[2,528,256]{2,1,0:T(8,128)S(1)} %shard_map.92.after.pair, f32[144,256]{1,0:T(8,128)S(1)} %get-tuple-element.16.after), custom_call_target="tpu_custom_call" | custom-call | flops 4227858432 | bytes 524288 | tf_op jit(solution)/shard_map/pallas_call | solution.py:410
  103.1 0.0 collective-permute-done.8.state_b
  103.1 0.0 collective-permute-done.7.state_a
  103.1 7.1 %shard_map.99 = (f32[2,256]{1,0:T(2,128)}, f32[2,256,256]{2,1,0:T(8,128)}) custom-call(s32[1]{0:T(128)} %bitcast.here.after, f32[144,256]{1,0:T(8,128)S(1)} %collective-permute-done.7.state_a, f32[144,256]{1,0:T(8,128)S(1)} %collective-permute-done.8.state_b, f32[1,256]{1,0:T(1,128)S(1)} %bitcast.3, f32[256,256]{1,0:T(8,128)S(1)} %copy-done, ...), custom_call_target="tpu_custom_call" | custom-call | flops 2415919104 | bytes 524288 | tf_op jit(solution)/shard_map/pallas_call | solution.py:411
Async XLA Ops:
  5.7 13.2 %collective-permute-start = (f32[528,256]{1,0:T(8,128)S(1)}, f32[528,256]{1,0:T(8,128)S(1)}, u32[]{:S(2)}, u32[]{:S(2)}) collective-permute-start(f32[528,256]{1,0:T(8,128)S(1)} %get-tuple-element.10.mine), channel_id=1, source_target_pairs={{0,1},{1,0},{2,3},{3,2},{4,5},{5,4},{6,7},{7,6},{8,9},{9,8},{10,11... | collective-permute-start | bytes 1622024 | tf_op jit(solution)/shard_map/ppermute | solution.py:361
  21.1 13.9 %collective-permute-start.1 = (f32[528,256]{1,0:T(8,128)S(1)}, f32[528,256]{1,0:T(8,128)S(1)}, u32[]{:S(2)}, u32[]{:S(2)}) collective-permute-start(f32[528,256]{1,0:T(8,128)S(1)} %shard_map.87.mine), channel_id=1, source_target_pairs={{0,2},{1,3},{2,0},{3,1},{4,6},{5,7},{6,4},{7,5},{8,10},{9,11},{10,... | collective-permute-start | bytes 1622024 | tf_op jit(solution)/shard_map/ppermute | solution.py:361
  37.0 11.5 %collective-permute-start.2 = (f32[528,256]{1,0:T(8,128)S(1)}, f32[528,256]{1,0:T(8,128)S(1)}, u32[]{:S(2)}, u32[]{:S(2)}) collective-permute-start(f32[528,256]{1,0:T(8,128)S(1)} %shard_map.89.mine), channel_id=1, source_target_pairs={{0,4},{4,0},{8,12},{12,8},{1,5},{5,1},{9,13},{13,9},{2,6},{6,2},{1... | collective-permute-start | bytes 1622024 | tf_op jit(solution)/shard_map/ppermute | solution.py:361
  50.6 12.2 %collective-permute-start.3 = (f32[528,256]{1,0:T(8,128)S(1)}, f32[528,256]{1,0:T(8,128)S(1)}, u32[]{:S(2)}, u32[]{:S(2)}) collective-permute-start(f32[528,256]{1,0:T(8,128)S(1)} %shard_map.91.mine), channel_id=1, source_target_pairs={{0,8},{4,12},{8,0},{12,4},{1,9},{5,13},{9,1},{13,5},{2,10},{6,14},... | collective-permute-start | bytes 1622024 | tf_op jit(solution)/shard_map/ppermute | solution.py:361
  65.5 17.5 %copy-start = (f32[256,256]{1,0:T(8,128)S(1)}, f32[256,256]{1,0:T(8,128)}, u32[]{:S(2)}) copy-start(f32[256,256]{1,0:T(8,128)} %cov.3) | copy-start | bytes 786436
  65.6 17.5 %copy-start.1 = (f32[256]{0:T(256)S(1)}, f32[256]{0:T(256)}, u32[]{:S(2)}) copy-start(f32[256]{0:T(256)} %param.12) | copy-start | bytes 3076
  65.6 5.7 %collective-permute-start.4 = (f32[528,256]{1,0:T(8,128)S(1)}, f32[528,256]{1,0:T(8,128)S(1)}, u32[]{:S(2)}, u32[]{:S(2)}) collective-permute-start(f32[528,256]{1,0:T(8,128)S(1)} %shard_map.93.mine), channel_id=1, source_target_pairs={{0,16},{16,0},{1,17},{17,1},{2,18},{18,2},{3,19},{19,3},{4,20},{20... | collective-permute-start | bytes 1622024 | tf_op jit(solution)/shard_map/ppermute | solution.py:361
  74.1 7.7 %collective-permute-start.5 = (f32[264,256]{1,0:T(8,128)S(1)}, f32[264,256]{1,0:T(8,128)S(1)}, u32[]{:S(2)}, u32[]{:S(2)}) collective-permute-start(f32[264,256]{1,0:T(8,128)S(1)} %get-tuple-element.12), channel_id=1, source_target_pairs={{0,32},{32,0},{64,96},{96,64},{1,33},{33,1},{65,97},{97,65},{2,34}... | collective-permute-start | bytes 811016 | tf_op jit(solution)/shard_map/ppermute | solution.py:361
  81.8 7.4 %collective-permute-start.6 = (f32[264,256]{1,0:T(8,128)S(1)}, f32[264,256]{1,0:T(8,128)S(1)}, u32[]{:S(2)}, u32[]{:S(2)}) collective-permute-start(f32[264,256]{1,0:T(8,128)S(1)} %collective-permute-done.5.mine), channel_id=1, source_target_pairs={{0,16},{16,0},{1,17},{17,1},{2,18},{18,2},{3,19},{19,3},{4,20},{20... | collective-permute-start | bytes 811016 | tf_op jit(solution)/shard_map/ppermute | solution.py:361
  92.9 10.2 %collective-permute-start.8 = (f32[144,256]{1,0:T(8,128)S(1)}, f32[144,256]{1,0:T(8,128)S(1)}, u32[]{:S(2)}, u32[]{:S(2)}) collective-permute-start(f32[144,256]{1,0:T(8,128)S(1)} %get-tuple-element.16.after), channel_id=1, source_target_pairs={{0,96},{1,97},{2,98},{3,99},{4,100},{5,101},{6,102},{7,103},{8,104... | collective-permute-start | bytes 442376 | tf_op jit(solution)/shard_map/ppermute | solution.py:409
  94.2 8.9 %collective-permute-start.7 = (f32[144,256]{1,0:T(8,128)S(1)}, f32[144,256]{1,0:T(8,128)S(1)}, u32[]{:S(2)}, u32[]{:S(2)}) collective-permute-start(f32[144,256]{1,0:T(8,128)S(1)} %get-tuple-element.16.after), channel_id=1, source_target_pairs={{0,64},{1,65},{2,66},{3,67},{4,68},{5,69},{6,70},{7,71},{8,72},{9,... | collective-permute-start | bytes 442376 | tf_op jit(solution)/shard_map/ppermute | solution.py:408

commit v2 on v1

--- a/solution.py
+++ b/solution.py
@@ -77,26 +77,29 @@
     return [stack[0:n, :] for stack in stacks]
 
 
-def unpack(ref):
-    move = ref[0:N, :]
-    both = ref[N : 2 * N, :]
-    vecs = ref[2 * N :, :]
+def unpack(move_ref, side_ref):
+    both = side_ref[0:N, :]
+    vecs = side_ref[N:, :]
     row, col = row_col(N)
     turned = both.T
     spread = jnp.where(row <= col, both, turned)
     info = jnp.where(row == col, vecs[2:3, :], jnp.where(row > col, both, turned))
-    return move, spread, info, vecs
-
-
-def pack(ref, move, spread, info, offset, info_vec):
+    return move_ref[...], spread, info, vecs
+
+
+def pack(move_ref, side_ref, move, spread, info, offset, info_vec):
     row, col = row_col(N)
-    ref[0:N, :] = move
-    ref[N : 2 * N, :] = jnp.where(row <= col, spread, info)
+    move_ref[...] = move
+    side_ref[0:N, :] = jnp.where(row <= col, spread, info)
     diag = jnp.sum(jnp.where(row == col, info, 0.0), axis=0, keepdims=True)
     place = lax.broadcasted_iota(jnp.int32, (V, N), 0)
-    ref[2 * N :, :] = jnp.where(
+    side_ref[N:, :] = jnp.where(
         place == 0, offset, jnp.where(place == 1, info_vec, jnp.where(place == 2, diag, 0.0))
     )
+
+
+def parts(ref):
+    return ref.at[0:N], ref.at[N:]
 
 
 def combine(firsts, seconds, stacks):
@@ -148,7 +151,7 @@
 
 
 def build_kernel(
-    trans_in, obs_in, noise_in, meas_in, state_in, two_ref, pair, trans, obs, noise, meas,
+    trans_in, obs_in, noise_in, meas_in, state_in, move_ref, side_ref, pair, trans, obs, noise, meas,
     noise_state, sems, stack, small_a, small_b,
 ):
     copies = [
@@ -171,7 +174,7 @@
     state2 = split(state)
     place = lax.broadcasted_iota(jnp.int32, (V, N), 0)
     row, col = row_col(O)
-    parts = []
+    found = []
     for k in range(2):
         sensor2 = split(obs[k])
         sensed = dot3(sensor2, state2)
@@ -181,11 +184,11 @@
         root = lax.rsqrt(variance)
         root = root * (1.5 - 0.5 * variance * root * root)
         root_col = jnp.sum(jnp.where(row == col, root, 0.0), axis=1, keepdims=True)
-        parts.append((sensed, seen, root_col * inner * root, root, root_col))
-    inverses = resolvents([part[2] for part in parts], (small_a, small_b))
+        found.append((sensed, seen, root_col * inner * root, root, root_col))
+    inverses = resolvents([part[2] for part in found], (small_a, small_b))
     steps = []
     for k in range(2):
-        sensed, seen, _, root, root_col = parts[k]
+        sensed, seen, _, root, root_col = found[k]
         inverse2 = split(root_col * inverses[k] * root)
         pair2 = split(jnp.concatenate([seen, sensed], axis=1))
         solved = dot3(inverse2, pair2)
@@ -196,9 +199,10 @@
         vecs = jnp.where(place == 0, vec[0:1, N:], jnp.where(place == 1, vec[0:1, 0:N], 0.0))
         steps.append((trans[k].T - full[0:N, N:], state - full[N:, N:], full[0:N, 0:N], vecs))
     move, spread, info, vecs = steps[0]
-    pack(pair.at[0], move, spread, info, vecs[0:1], vecs[1:2])
-    pack(two_ref, *combine(steps[0:1], steps[1:2], [stack])[0])
-    pair[1] = two_ref[...]
+    pack(*parts(pair.at[0]), move, spread, info, vecs[0:1], vecs[1:2])
+    pack(move_ref, side_ref, *combine(steps[0:1], steps[1:2], [stack])[0])
+    pair[1, 0:N, :] = move_ref[...]
+    pair[1, N:, :] = side_ref[...]
 
 
 def upper(here, axis, step):
@@ -206,29 +210,59 @@
     return ((here[0] >> shift) & 1) == 1
 
 
-def order(flag, mine, theirs, first, second):
-    first[...] = jnp.where(flag, theirs[...], mine[...])
-    second[...] = jnp.where(flag, mine[...], theirs[...])
-    return unpack(first), unpack(second)
-
-
-def total_kernel(axis, step, here, mine, theirs, after, out, first, second, stack):
-    a, b = order(upper(here, axis, step), mine, theirs, first, second)
-    pack(out, *combine([a], [b], [stack])[0])
-
-
-def core_kernel(here, mine, theirs, after, out, half, first, second, stack):
-    total_kernel("c", 1, here, mine, theirs, after, out, first, second, stack)
-    half[...] = jnp.where(upper(here, "c", 1), out[HALF:, :], out[0:HALF, :])
-
-
-def slow_kernel(axis, step, here, theirs, pair, after, out, stack):
+def sort(flag, ones, others, first, second):
+    for half, one, other in zip((slice(0, N), slice(N, ROWS)), ones, others):
+        first[half, :] = jnp.where(flag, other[...], one[...])
+        second[half, :] = jnp.where(flag, one[...], other[...])
+
+
+def own_kernel(axis, here, ma, mb, pa, pb, na, nb, after, out, first, second, stack):
+    odd = upper(here, axis, 1)
+    for half, mine, prev, later in zip((slice(0, N), slice(N, ROWS)), (ma, mb), (pa, pb), (na, nb)):
+        first[half, :] = jnp.where(odd, prev[...], mine[...])
+        second[half, :] = jnp.where(odd, mine[...], later[...])
+    done = combine([unpack(*parts(first))], [unpack(*parts(second))], [stack])
+    pack(*parts(out), *done[0])
+
+
+def ring_kernel(axis, here, own, pa, pb, na, nb, fa, fb, out_a, out_b, other_a, other_b, held_ref, stack):
+    odd, late = upper(here, axis, 1), upper(here, axis, 2)
+    for half, prev, later, far in zip((slice(0, N), slice(N, ROWS)), (pa, pb), (na, nb), (fa, fb)):
+        held_ref[0, half, :] = jnp.where(odd, later[...], far[...])
+        held_ref[1, half, :] = jnp.where(odd, far[...], prev[...])
+    held_ref[3] = own[...]
+    swapped = late.astype(jnp.int32)
+
+    def one(k, carry):
+        first = held_ref.at[k * (3 - swapped)]
+        second = held_ref.at[1 + k * (1 + swapped)]
+        done = combine([unpack(*parts(first))], [unpack(*parts(second))], [stack])
+        pack(*parts(held_ref.at[2 + 2 * k]), *done[0])
+        return carry
+
+    lax.fori_loop(0, 2, one, 0)
+    other_a[...] = held_ref[2, 0:N, :]
+    other_b[...] = held_ref[2, N:, :]
+    out_a[...] = held_ref[4, 0:N, :]
+    out_b[...] = held_ref[4, N:, :]
+
+
+def core_kernel(here, ma, mb, ta, tb, after, out, half, first, second, stack):
+    flag = upper(here, "c", 1)
+    sort(flag, (ma, mb), (ta, tb), first, second)
+    done = combine([unpack(*parts(first))], [unpack(*parts(second))], [stack])
+    pack(*parts(out), *done[0])
+    half[...] = jnp.where(flag, out[HALF:, :], out[0:HALF, :])
+
+
+def slow_kernel(axis, step, here, ta, tb, pair, after, out, stack):
     flag = upper(here, axis, step)
 
     @pl.when(flag)
     def _():
         def one(k, carry):
-            pack(out.at[k], *combine([unpack(theirs)], [unpack(pair.at[k])], [stack])[0])
+            done = combine([unpack(ta, tb)], [unpack(*parts(pair.at[k]))], [stack])
+            pack(*parts(out.at[k]), *done[0])
             return carry
 
         lax.fori_loop(0, 2, one, 0)
@@ -238,55 +272,77 @@
         out[...] = pair[...]
 
 
-def merge_kernel(here, late, early, after, out, stack):
-    z_up, c_up = upper(here, "z", 2), upper(here, "c", 1)
-
-    @pl.when(jnp.logical_and(z_up, c_up))
-    def _():
-        pack(out, *combine([unpack(late)], [unpack(early)], [stack])[0])
-
-    @pl.when(jnp.logical_not(z_up))
-    def _():
-        out[...] = late[...]
-
-    @pl.when(jnp.logical_not(c_up))
-    def _():
-        out[...] = early[...]
-
-
-def steps_kernel(here, theirs, low, pair, after, out, whole, stack, stack_b):
+def held(here, axes):
+    flag = upper(here, *axes[0])
+    for axis in axes[1:]:
+        flag = jnp.logical_or(flag, upper(here, *axis))
+    return flag
+
+
+Z_LEVEL = (("z", 1), ("z", 2))
+CORE_LEVEL = Z_LEVEL + (("c", 1),)
+
+
+def merge_into(out, has_early, has_late, early, late, stack):
+    @pl.when(jnp.logical_and(has_early, has_late))
+    def _():
+        pack(*parts(out), *combine([unpack(*early)], [unpack(*late)], [stack])[0])
+
+    @pl.when(jnp.logical_not(has_early))
+    def _():
+        out[0:N, :] = late[0][...]
+        out[N:, :] = late[1][...]
+
+    @pl.when(jnp.logical_not(has_late))
+    def _():
+        out[0:N, :] = early[0][...]
+        out[N:, :] = early[1][...]
+
+
+def ringed_kernel(here, oa, ob, pa, pb, after, out, stack):
+    merge_into(out, upper(here, "z", 2), upper(here, "z", 1), (oa, ob), (pa, pb), stack)
+
+
+def cored_kernel(here, ta, tb, low, after, out, stack):
+    merge_into(out, upper(here, "c", 1), held(here, Z_LEVEL), (ta, tb), parts(low), stack)
+
+
+def steps_kernel(here, theirs, low, pair, after, out, held_ref, stack):
     x_up = upper(here, "x", 1)
-    held = jnp.logical_or(upper(here, "z", 2), upper(here, "c", 1))
-
-    @pl.when(jnp.logical_and(x_up, held))
-    def _():
-        pack(whole, *combine([unpack(theirs)], [unpack(low)], [stack])[0])
-
-    @pl.when(jnp.logical_not(x_up))
-    def _():
-        whole[...] = low[...]
-
-    @pl.when(jnp.logical_not(held))
-    def _():
-        whole[...] = theirs[...]
-
-    @pl.when(jnp.logical_or(x_up, held))
-    def _():
-        first = unpack(whole)
-        done = combine(
-            [first, first], [unpack(pair.at[0]), unpack(pair.at[1])], [stack, stack_b]
-        )
-        pack(out.at[0], *done[0])
-        pack(out.at[1], *done[1])
-
-    @pl.when(jnp.logical_not(jnp.logical_or(x_up, held)))
-    def _():
-        out[...] = pair[...]
-
-
-def prior_kernel(whole, mean, cov, mean_out, cov_out, stack):
-    state = jnp.broadcast_to(mean[...], (V, N))
-    mean_out[...], cov_out[...] = apply_state(state, cov[...], [unpack(whole)], [stack])[0]
+    has_low = held(here, CORE_LEVEL)
+    held_ref[0] = theirs[...]
+    held_ref[1] = low[...]
+    held_ref[3:5] = pair[...]
+    both = jnp.logical_and(x_up, has_low)
+    either = jnp.logical_or(x_up, has_low)
+    source = jnp.where(both, 2, jnp.where(has_low, 1, 0))
+
+    def one(k, carry):
+        first = held_ref.at[jnp.where(k == 0, 0, source)]
+        second = held_ref.at[jnp.where(k == 0, 1, k + 2)]
+        done = combine([unpack(*parts(first))], [unpack(*parts(second))], [stack])
+        pack(*parts(held_ref.at[k + 2]), *done[0])
+        return carry
+
+    lax.fori_loop(jnp.where(both, 0, 1), jnp.where(either, 3, 1), one, 0)
+    out[...] = held_ref[3:5]
+
+
+def is_first(here):
+    return (here[0] >> 5) == 0
+
+
+def prior_kernel(here, whole, mean, cov, mean_out, cov_out, stack):
+    @pl.when(is_first(here))
+    def _():
+        state = jnp.broadcast_to(mean[...], (V, N))
+        done = apply_state(state, cov[...], [unpack(*parts(whole))], [stack])
+        mean_out[...], cov_out[...] = done[0]
+
+    @pl.when(jnp.logical_not(is_first(here)))
+    def _():
+        mean_out[...] = jnp.broadcast_to(mean[...], (V, N))
+        cov_out[...] = cov[...]
 
 
 HN = N // 2
@@ -296,14 +352,23 @@
     flag = upper(here, "c", 1)
     theirs[0:HALF, :] = jnp.where(flag, other[...], mine[...])
     theirs[HALF:, :] = jnp.where(flag, mine[...], other[...])
-    mean_b, cov_b = apply_state(mean[...], cov[...], [unpack(theirs)], [stack])[0]
-    row, col = row_col(HN)
-    last = cov_b[HN:, HN:]
-    out[0:HN, 0:HN] = jnp.where(row <= col, cov_b[0:HN, 0:HN], last)
-    out[0:HN, HN:] = cov_b[0:HN, HN:]
-    diag = jnp.sum(jnp.where(row == col, last, 0.0), axis=0, keepdims=True)
-    out[HN : HN + 8, :] = mean_b[0:8]
-    out[HN + 8 :, :] = jnp.broadcast_to(jnp.concatenate([diag, diag], axis=1), (8, N))
+
+    @pl.when(is_first(here))
+    def _():
+        mean_b, cov_b = apply_state(
+            mean[...], cov[...], [unpack(*parts(theirs))], [stack]
+        )[0]
+        row, col = row_col(HN)
+        last = cov_b[HN:, HN:]
+        out[0:HN, 0:HN] = jnp.where(row <= col, cov_b[0:HN, 0:HN], last)
+        out[0:HN, HN:] = cov_b[0:HN, HN:]
+        diag = jnp.sum(jnp.where(row == col, last, 0.0), axis=0, keepdims=True)
+        out[HN : HN + 8, :] = mean_b[0:8]
+        out[HN + 8 :, :] = jnp.broadcast_to(jnp.concatenate([diag, diag], axis=1), (8, N))
+
+    @pl.when(jnp.logical_not(is_first(here)))
+    def _():
+        out[...] = jnp.zeros((HN + 16, N), F32)
 
 
 def final_kernel(here, state_a, state_b, mean, cov, pair, means, covs, packed, prior, stack, stack_b):
@@ -321,7 +386,8 @@
     prior[HN:, 0:HN] = jnp.where(flag, side.T, cov[HN:, 0:HN])
     prior[HN:, HN:] = jnp.where(flag, last, cov[HN:, HN:])
     mean_in = jnp.broadcast_to(jnp.where(flag, packed[HN : HN + 1, :], mean[...]), (V, N))
-    done = apply_state(mean_in, prior[...], [unpack(pair.at[0]), unpack(pair.at[1])], [stack, stack_b])
+    seconds = [unpack(*parts(pair.at[k])) for k in range(2)]
+    done = apply_state(mean_in, prior[...], seconds, [stack, stack_b])
     for k in range(2):
         means[k : k + 1, :] = done[k][0][0:1]
         covs[k] = done[k][1]
@@ -347,6 +413,8 @@
 
 ELEMENT = (ROWS, N)
 PAIR = (2, ROWS, N)
+MOVE = (N, N)
+SIDE = (N + V, N)
 HALF = ROWS // 2
 STACK = (2 * N, N)
 PACKED = (HN + 16, N)
@@ -360,49 +428,56 @@
         size = lax.axis_size(axis)
         return lax.ppermute(part, axis, [(k, k ^ step) for k in range(size)])
 
-    def total(axis, step, mine, theirs, after):
-        kernel = functools.partial(total_kernel, axis, step)
-        run = call(kernel, "svva", [ELEMENT], [ELEMENT, ELEMENT, STACK], 14)
-        return run(here, mine, theirs, after)
+    def ring(axis, mine, after):
+        def turn(part, step):
+            return lax.ppermute(part, axis, [(k, (k + step) % 4) for k in range(4)])
+
+        later_a, prev_b = turn(mine[0], 3), turn(mine[1], 1)
+        prev_a, later_b = turn(mine[0], 1), turn(mine[1], 3)
+        far_a = turn(later_a, 3)
+        far_b = turn(prev_b, 1)
+        kernel = functools.partial(own_kernel, axis)
+        scratch = [ELEMENT, ELEMENT, STACK]
+        near = (prev_a, prev_b, later_a, later_b)
+        own = call(kernel, "svvvvvva", [ELEMENT], scratch, 14)(here, *mine, *near, after)
+        kernel = functools.partial(ring_kernel, axis)
+        run = call(kernel, "svvvvvvv", [MOVE, SIDE] * 2, [(5, *ELEMENT), STACK], 28)
+        whole_a, whole_b, *other = run(here, own, *near, far_a, far_b)
+        return (whole_a, whole_b), (prev_a, prev_b), other
 
     def slow(axis, step, theirs, pair, after):
         kernel = functools.partial(slow_kernel, axis, step)
-        return call(kernel, "svva", [PAIR], [STACK], 28)(here, theirs, pair, after)
-
-    merge = call(merge_kernel, "svva", [ELEMENT], [STACK], 14)
-    steps = call(steps_kernel, "svvva", [PAIR], [ELEMENT, STACK, STACK], 42)
+        return call(kernel, "svvva", [PAIR], [STACK], 28)(here, *theirs, pair, after)
+
+    ringed = call(ringed_kernel, "svvvva", [ELEMENT], [STACK], 14)
+    cored = call(cored_kernel, "svvva", [ELEMENT], [STACK], 14)
+    steps = call(steps_kernel, "svvva", [PAIR], [(5, *ELEMENT), STACK], 42)
 
     inputs = [(2, N, N), (2, O, N), (2, O), (2, O), (N, N)]
     build = call(
         build_kernel,
         "hhhhh",
-        [ELEMENT, PAIR],
+        [MOVE, SIDE, PAIR],
         inputs + [pltpu.SemaphoreType.DMA((5,)), STACK, (2 * O, O), (2 * O, O)],
         30,
     )
-    core = call(core_kernel, "svva", [ELEMENT, (HALF, N)], [ELEMENT, ELEMENT, STACK], 14)
-    prior = call(prior_kernel, "vvv", [(V, N), (N, N)], [STACK], 14)
+    core = call(core_kernel, "svvvva", [ELEMENT, (HALF, N)], [ELEMENT, ELEMENT, STACK], 14)
+    prior = call(prior_kernel, "svvv", [(V, N), (N, N)], [STACK], 14)
     second = call(second_kernel, "svvvva", [ELEMENT, PACKED], [STACK], 14)
     final = call(final_kernel, "svvvvv", [(2, N), (2, N, N)], [PACKED, (N, N), STACK, STACK], 24)
 
     arrays = (transition, observe, noise_obs, measured, noise_state)
-    whole, pair = build(*(pltpu.with_memory_space_constraint(a, pltpu.HBM) for a in arrays))
-    y1 = swap(whole, "y", 1)
-    whole = total("y", 1, whole, y1, here)
-    y2 = swap(whole, "y", 2)
-    pair = slow("y", 1, y1, pair, here)
-    whole = total("y", 2, whole, y2, pair)
-    z1 = swap(whole, "z", 1)
-    pair = slow("y", 2, y2, pair, here)
-    whole = total("z", 1, whole, z1, pair)
-    z2 = swap(whole, "z", 2)
-    pair = slow("z", 1, z1, pair, here)
-    whole = total("z", 2, whole, z2, pair)
-    c1 = swap(whole, "c", 1)
-    whole, half = core(here, whole, c1, here)
+    *whole, pair = build(*(pltpu.with_memory_space_constraint(a, pltpu.HBM) for a in arrays))
+    whole, prev, other = ring("y", whole, here)
+    pair = slow("y", 1, prev, pair, whole[0])
+    pair = slow("y", 2, other, pair, whole[0])
+    whole, prev, other = ring("z", whole, pair)
+    c1 = [swap(half, "c", 1) for half in whole]
+    low = ringed(here, *other, *prev, whole[0])
+    whole, half = core(here, *whole, *c1, low)
     x1 = swap(half, "x", 1)
-    mean_a, cov_a = prior(whole, mean, prior_cov)
-    low = merge(here, c1, z2, mean_a)
+    mean_a, cov_a = prior(here, whole, mean, prior_cov)
+    low = cored(here, *c1, low, mean_a)
     x1_other = swap(x1, "c", 1)
     theirs, packed = second(here, x1, x1_other, mean_a, cov_a, low)
     state_a = lax.ppermute(packed, "x", [(0, 2)])

time: 110 us -> 95.8 us (0.87)
  the two profiles are of different devices: /device:TPU:127 before, /device:TPU:97 now
where the time goes in v2:
time: 95.8 us; the launch traced here: 95.6 us
  Pallas kernels  45.8 us (48%)
  waiting for transfers between devices  29.9 us (31%)
  starting transfers between devices  19.1 us (20%)
    ppermute x12, waiting for transfers between devices, turn(): return lax.ppermute(part, axis, [(k, (k + step) % 4) for k in range(4)])  22.9 us
    ppermute x12, starting transfers between devices, turn(): return lax.ppermute(part, axis, [(k, (k + step) % 4) for k in range(4)])  12.7 us
    pallas_call x2, Pallas kernels, ring(): whole_a, whole_b, *other = run(here, own, *near, far_a, far_b)  9.9 us
    ppermute x4, waiting for transfers between devices, swap(): return lax.ppermute(part, axis, [(k, k ^ step) for k in range(size)])  7.07 us
    pallas_call x1, Pallas kernels, on_device(): return final(here, state_a, state_b, mean, prior_cov, pair)  5.92 us
    pallas_call x1, Pallas kernels, on_device(): pair = steps(here, theirs, low, pair, packed)  5.61 us
    pallas_call x1, Pallas kernels, on_device(): build(*(pltpu.with_memory_space_constraint(a, pltpu.HBM) for a in arrays))  5.11 us
    pallas_call x2, Pallas kernels, ring(): call(kernel, 'svvvvvva', [ELEMENT], scratch, 14)(here, *mine, *near, after)  4.14 us
  transfers between devices with their start and end apart: 18, of which 9 were waited for; matrix products, arithmetic and copies ran while one was open for 0% of the time, Pallas kernels for 19%

profile of v2, /device:TPU:97, one launch (start us, length us, event | category | flops | bytes accessed | tf_op | source)
XLA Modules:
  0.0 95.6 jit_solution(14795011315953676404)
XLA Ops:
  0.6 5.1 %shard_map.86 = (f32[256,256]{1,0:T(8,128)S(1)}, f32[272,256]{1,0:T(8,128)S(1)}, f32[2,528,256]{2,1,0:T(8,128)S(1)}) custom-call(f32[2,256,256]{2,1,0:T(8,128)} %trans_in.1, f32[2,64,256]{2,1,0:T(8,128)} %obs_in.1, f32[2,64]{1,0:T(2,128)} %noise_in.1, f32[2,64]{1,0:T(2,128)} %meas_in.1, f32[256,256]{1,0:T(8,128)} %state_in.1), custom_call_target="tpu_custom_call" | custom-call | flops 3019898880 | bytes 524288 | tf_op jit(solution)/shard_map/pallas_call | solution.py:470
  5.7 1.4 %collective-permute-start.1 = (f32[272,256]{1,0:T(8,128)S(1)}, f32[272,256]{1,0:T(8,128)S(1)}, u32[]{:S(2)}, u32[]{:S(2)}) collective-permute-start(f32[272,256]{1,0:T(8,128)S(1)} %get-tuple-element.20.mb), channel_id=1, source_target_pairs={{0,1},{1,2},{2,3},{3,0},{4,5},{5,6},{6,7},{7,4},{8,9},{9,10},{10,1... | collective-permute-start | bytes 835592 | tf_op jit(solution)/shard_map/ppermute | solution.py:433
  7.1 1.5 %collective-permute-start.2 = (f32[256,256]{1,0:T(8,128)S(1)}, f32[256,256]{1,0:T(8,128)S(1)}, u32[]{:S(2)}, u32[]{:S(2)}) collective-permute-start(f32[256,256]{1,0:T(8,128)S(1)} %get-tuple-element.19.ma), channel_id=1, source_target_pairs={{0,3},{1,0},{2,1},{3,2},{4,7},{5,4},{6,5},{7,6},{8,11},{9,8},{10,9... | collective-permute-start | bytes 786440 | tf_op jit(solution)/shard_map/ppermute | solution.py:433
  8.6 1.4 %collective-permute-start.3 = (f32[272,256]{1,0:T(8,128)S(1)}, f32[272,256]{1,0:T(8,128)S(1)}, u32[]{:S(2)}, u32[]{:S(2)}) collective-permute-start(f32[272,256]{1,0:T(8,128)S(1)} %get-tuple-element.20.mb), channel_id=1, source_target_pairs={{0,3},{1,0},{2,1},{3,2},{4,7},{5,4},{6,5},{7,6},{8,11},{9,8},{10,9... | collective-permute-start | bytes 835592 | tf_op jit(solution)/shard_map/ppermute | solution.py:433
  10.0 0.1 collective-permute-start
  10.1 4.6 %collective-permute-done.1.pb.tb = f32[272,256]{1,0:T(8,128)S(1)} collective-permute-done((f32[272,256]{1,0:T(8,128)S(1)}, f32[272,256]{1,0:T(8,128)S(1)}, u32[]{:S(2)}, u32[]{:S(2)}) %collective-permute-start.1) | collective-permute-done | bytes 278560 | tf_op jit(solution)/shard_map/ppermute | solution.py:433
  14.7 0.0 collective-permute-start.5
  14.7 0.0 collective-permute-done.2.na
  14.7 2.7 %collective-permute-start.4 = (f32[256,256]{1,0:T(8,128)S(1)}, f32[256,256]{1,0:T(8,128)S(1)}, u32[]{:S(2)}, u32[]{:S(2)}) collective-permute-start(f32[256,256]{1,0:T(8,128)S(1)} %collective-permute-done.2.na), channel_id=1, source_target_pairs={{0,3},{1,0},{2,1},{3,2},{4,7},{5,4},{6,5},{7,6},{8,11},{9,8},{10,9... | collective-permute-start | bytes 786440 | tf_op jit(solution)/shard_map/ppermute | solution.py:433
  17.4 2.9 %collective-permute-done.pa.ta = f32[256,256]{1,0:T(8,128)S(1)} collective-permute-done((f32[256,256]{1,0:T(8,128)S(1)}, f32[256,256]{1,0:T(8,128)S(1)}, u32[]{:S(2)}, u32[]{:S(2)}) %collective-permute-start) | collective-permute-done | bytes 262176 | tf_op jit(solution)/shard_map/ppermute | solution.py:433
  20.3 0.0 collective-permute-done.3.nb
  20.3 2.1 %shard_map.87.own = f32[528,256]{1,0:T(8,128)S(1)} custom-call(s32[1]{0:T(128)} %bitcast.here.after, f32[256,256]{1,0:T(8,128)S(1)} %get-tuple-element.19.ma, f32[272,256]{1,0:T(8,128)S(1)} %get-tuple-element.20.mb, f32[256,256]{1,0:T(8,128)S(1)} %collective-permute-done.pa.ta, f32[272,256]{1,0:T(8,128)S(1)} %collective-permute-done.1.pb.tb, ...), custom_call_target="tpu_custom_call" | custom-call | flops 1409286144 | bytes 524288 | tf_op jit(solution)/shard_map/pallas_call | solution.py:442
  22.4 3.2 %collective-permute-done.4.fa = f32[256,256]{1,0:T(8,128)S(1)} collective-permute-done((f32[256,256]{1,0:T(8,128)S(1)}, f32[256,256]{1,0:T(8,128)S(1)}, u32[]{:S(2)}, u32[]{:S(2)}) %collective-permute-start.4) | collective-permute-done | bytes 262176 | tf_op jit(solution)/shard_map/ppermute | solution.py:433
  25.6 0.7 collective-permute-done.5.fb
  26.3 4.3 %shard_map.88 = (f32[256,256]{1,0:T(8,128)S(1)}, f32[272,256]{1,0:T(8,128)S(1)}, f32[256,256]{1,0:T(8,128)S(1)}, f32[272,256]{1,0:T(8,128)S(1)}) custom-call(s32[1]{0:T(128)} %bitcast.here.after, f32[528,256]{1,0:T(8,128)S(1)} %shard_map.87.own, f32[256,256]{1,0:T(8,128)S(1)} %collective-permute-done.pa.ta, f32[272,256]{1,0:T(8,128)S(1)} %collective-permute-done.1.pb.tb, ...), custom_call_target="tpu_custom_call" | custom-call | flops 2818572288 | bytes 524288 | tf_op jit(solution)/shard_map/pallas_call | solution.py:445
  30.6 0.1 collective-permute-start.7
  30.7 1.5 %collective-permute-start.8 = (f32[256,256]{1,0:T(8,128)S(1)}, f32[256,256]{1,0:T(8,128)S(1)}, u32[]{:S(2)}, u32[]{:S(2)}) collective-permute-start(f32[256,256]{1,0:T(8,128)S(1)} %get-tuple-element.21.after.ma), channel_id=1, source_target_pairs={{0,12},{4,0},{8,4},{12,8},{1,13},{5,1},{9,5},{13,9},{2,14},{6,2},{... | collective-permute-start | bytes 786440 | tf_op jit(solution)/shard_map/ppermute | solution.py:433
  32.1 1.3 %collective-permute-start.6 = (f32[256,256]{1,0:T(8,128)S(1)}, f32[256,256]{1,0:T(8,128)S(1)}, u32[]{:S(2)}, u32[]{:S(2)}) collective-permute-start(f32[256,256]{1,0:T(8,128)S(1)} %get-tuple-element.21.after.ma), channel_id=1, source_target_pairs={{0,4},{4,8},{8,12},{12,0},{1,5},{5,9},{9,13},{13,1},{2,6},{6,10},{... | collective-permute-start | bytes 786440 | tf_op jit(solution)/shard_map/ppermute | solution.py:433
  33.4 0.2 collective-permute-start.9
  33.6 0.1 shard_map.89.pair
  33.7 4.7 %collective-permute-done.8.na = f32[256,256]{1,0:T(8,128)S(1)} collective-permute-done((f32[256,256]{1,0:T(8,128)S(1)}, f32[256,256]{1,0:T(8,128)S(1)}, u32[]{:S(2)}, u32[]{:S(2)}) %collective-permute-start.8) | collective-permute-done | bytes 262176 | tf_op jit(solution)/shard_map/ppermute | solution.py:433
  38.3 0.0 collective-permute-start.10
  38.3 0.0 collective-permute-done.7.pb
  38.3 2.7 %collective-permute-start.11 = (f32[272,256]{1,0:T(8,128)S(1)}, f32[272,256]{1,0:T(8,128)S(1)}, u32[]{:S(2)}, u32[]{:S(2)}) collective-permute-start(f32[272,256]{1,0:T(8,128)S(1)} %collective-permute-done.7.pb), channel_id=1, source_target_pairs={{0,4},{4,8},{8,12},{12,0},{1,5},{5,9},{9,13},{13,1},{2,6},{6,10},{... | collective-permute-start | bytes 835592 | tf_op jit(solution)/shard_map/ppermute | solution.py:433
  41.0 0.1 shard_map.90.after.pair
  41.1 1.9 %collective-permute-done.6.pa = f32[256,256]{1,0:T(8,128)S(1)} collective-permute-done((f32[256,256]{1,0:T(8,128)S(1)}, f32[256,256]{1,0:T(8,128)S(1)}, u32[]{:S(2)}, u32[]{:S(2)}) %collective-permute-start.6) | collective-permute-done | bytes 262176 | tf_op jit(solution)/shard_map/ppermute | solution.py:433
  43.0 1.3 %collective-permute-done.9.nb = f32[272,256]{1,0:T(8,128)S(1)} collective-permute-done((f32[272,256]{1,0:T(8,128)S(1)}, f32[272,256]{1,0:T(8,128)S(1)}, u32[]{:S(2)}, u32[]{:S(2)}) %collective-permute-start.9) | collective-permute-done | bytes 278560 | tf_op jit(solution)/shard_map/ppermute | solution.py:433
  44.3 2.1 %shard_map.91.own = f32[528,256]{1,0:T(8,128)S(1)} custom-call(s32[1]{0:T(128)} %bitcast.here.after, f32[256,256]{1,0:T(8,128)S(1)} %get-tuple-element.21.after.ma, f32[272,256]{1,0:T(8,128)S(1)} %get-tuple-element.22.mb, f32[256,256]{1,0:T(8,128)S(1)} %collective-permute-done.6.pa, f32[272,256]{1,0:T(8,128)S(1)} %collective-permute-done.7.pb, ...), custom_call_target="tpu_custom_call" | custom-call | flops 1409286144 | bytes 524288 | tf_op jit(solution)/shard_map/pallas_call | solution.py:442
  46.4 3.5 %collective-permute-done.10.fa = f32[256,256]{1,0:T(8,128)S(1)} collective-permute-done((f32[256,256]{1,0:T(8,128)S(1)}, f32[256,256]{1,0:T(8,128)S(1)}, u32[]{:S(2)}, u32[]{:S(2)}) %collective-permute-start.10) | collective-permute-done | bytes 262176 | tf_op jit(solution)/shard_map/ppermute | solution.py:433
  49.9 0.0 collective-permute-done.11.fb
  49.9 5.6 %shard_map.92 = (f32[256,256]{1,0:T(8,128)S(1)}, f32[272,256]{1,0:T(8,128)S(1)}, f32[256,256]{1,0:T(8,128)S(1)}, f32[272,256]{1,0:T(8,128)S(1)}) custom-call(s32[1]{0:T(128)} %bitcast.here.after, f32[528,256]{1,0:T(8,128)S(1)} %shard_map.91.own, f32[256,256]{1,0:T(8,128)S(1)} %collective-permute-done.6.pa, f32[272,256]{1,0:T(8,128)S(1)} %collective-permute-done.7.pb, ...), custom_call_target="tpu_custom_call" | custom-call | flops 2818572288 | bytes 524288 | tf_op jit(solution)/shard_map/pallas_call | solution.py:445
  55.5 1.8 %collective-permute-start.13 = (f32[272,256]{1,0:T(8,128)S(1)}, f32[272,256]{1,0:T(8,128)S(1)}, u32[]{:S(2)}, u32[]{:S(2)}) collective-permute-start(f32[272,256]{1,0:T(8,128)S(1)} %get-tuple-element.27.mb), channel_id=1, source_target_pairs={{0,16},{16,0},{1,17},{17,1},{2,18},{18,2},{3,19},{19,3},{4,20},{20... | collective-permute-start | bytes 835592 | tf_op jit(solution)/shard_map/ppermute | solution.py:429
  57.3 0.1 collective-permute-start.12
  57.4 2.7 %shard_map.93.after.low = f32[528,256]{1,0:T(8,128)S(1)} custom-call(s32[1]{0:T(128)} %bitcast.here.after, f32[256,256]{1,0:T(8,128)S(1)} %get-tuple-element.28.oa, f32[272,256]{1,0:T(8,128)S(1)} %get-tuple-element.29.ob, f32[256,256]{1,0:T(8,128)S(1)} %collective-permute-done.6.pa, f32[272,256]{1,0:T(8,128)S(1)} %collective-permute-done.7.pb, ...), custom_call_target="tpu_custom_call" | custom-call | flops 1409286144 | bytes 524288 | tf_op jit(solution)/shard_map/pallas_call | solution.py:476
  60.1 0.0 copy-start
  60.1 0.0 copy-start.1
  60.1 0.0 collective-permute-done.12.ta
  60.1 0.0 collective-permute-done.13.tb
  60.2 3.0 %shard_map.94 = (f32[528,256]{1,0:T(8,128)S(1)}, f32[264,256]{1,0:T(8,128)S(1)}) custom-call(s32[1]{0:T(128)} %bitcast.here.after, f32[256,256]{1,0:T(8,128)S(1)} %get-tuple-element.26.after.ma, f32[272,256]{1,0:T(8,128)S(1)} %get-tuple-element.27.mb, f32[256,256]{1,0:T(8,128)S(1)} %collective-permute-done.12.ta, f32[272,256]{1,0:T(8,128)S(1)} %collective-permute-done.13.tb, ...), custom_call_target="tpu_custom_call" | custom-call | flops 1409286144 | bytes 524288 | tf_op jit(solution)/shard_map/pallas_call | solution.py:477
  63.1 1.3 %collective-permute-start.14 = (f32[264,256]{1,0:T(8,128)S(1)}, f32[264,256]{1,0:T(8,128)S(1)}, u32[]{:S(2)}, u32[]{:S(2)}) collective-permute-start(f32[264,256]{1,0:T(8,128)S(1)} %get-tuple-element.30), channel_id=1, source_target_pairs={{0,32},{32,0},{64,96},{96,64},{1,33},{33,1},{65,97},{97,65},{2,34}... | collective-permute-start | bytes 811016 | tf_op jit(solution)/shard_map/ppermute | solution.py:429
  64.4 7.1 %collective-permute-done.14.mine = f32[264,256]{1,0:T(8,128)S(1)} collective-permute-done((f32[264,256]{1,0:T(8,128)S(1)}, f32[264,256]{1,0:T(8,128)S(1)}, u32[]{:S(2)}, u32[]{:S(2)}) %collective-permute-start.14) | collective-permute-done | bytes 270368 | tf_op jit(solution)/shard_map/ppermute | solution.py:429
  71.5 0.6 collective-permute-start.15
  72.1 0.0 copy-done
  72.1 0.0 copy-done.1
  72.1 3.3 %shard_map.95 = (f32[16,256]{1,0:T(8,128)S(1)}, f32[256,256]{1,0:T(8,128)S(1)}) custom-call(s32[1]{0:T(128)} %bitcast.here.after, f32[528,256]{1,0:T(8,128)S(1)} %get-tuple-element.31.whole, f32[1,256]{1,0:T(1,128)S(1)} %bitcast.2, f32[256,256]{1,0:T(8,128)S(1)} %copy-done), custom_call_target="tpu_custom_call" | custom-call | flops 1409286144 | bytes 524288 | tf_op jit(solution)/shard_map/pallas_call | solution.py:479
  75.4 2.7 %shard_map.96.after.low = f32[528,256]{1,0:T(8,128)S(1)} custom-call(s32[1]{0:T(128)} %bitcast.here.after, f32[256,256]{1,0:T(8,128)S(1)} %collective-permute-done.12.ta, f32[272,256]{1,0:T(8,128)S(1)} %collective-permute-done.13.tb, f32[528,256]{1,0:T(8,128)S(1)} %shard_map.93.after.low, f32[16,256]{1,0:T(8,128)S(1)} %get-tuple-element.32.after.mean), custom_call_target="tpu_custom_call" | custom-call | flops 1409286144 | bytes 524288 | tf_op jit(solution)/shard_map/pallas_call | solution.py:480
  78.1 0.0 collective-permute-done.15.other
  78.1 3.3 %shard_map.97 = (f32[528,256]{1,0:T(8,128)S(1)}, f32[144,256]{1,0:T(8,128)S(1)}) custom-call(s32[1]{0:T(128)} %bitcast.here.after, f32[264,256]{1,0:T(8,128)S(1)} %collective-permute-done.14.mine, f32[264,256]{1,0:T(8,128)S(1)} %collective-permute-done.15.other, f32[16,256]{1,0:T(8,128)S(1)} %get-tuple-element.32.after.mean, ...), custom_call_target="tpu_custom_call" | custom-call | flops 1409286144 | bytes 524288 | tf_op jit(solution)/shard_map/pallas_call | solution.py:482
  81.4 1.3 %collective-permute-start.17 = (f32[144,256]{1,0:T(8,128)S(1)}, f32[144,256]{1,0:T(8,128)S(1)}, u32[]{:S(2)}, u32[]{:S(2)}) collective-permute-start(f32[144,256]{1,0:T(8,128)S(1)} %get-tuple-element.34.after), channel_id=1, source_target_pairs={{0,96},{1,97},{2,98},{3,99},{4,100},{5,101},{6,102},{7,103},{8,104... | collective-permute-start | bytes 442376 | tf_op jit(solution)/shard_map/ppermute | solution.py:484
  82.7 1.3 %collective-permute-start.16 = (f32[144,256]{1,0:T(8,128)S(1)}, f32[144,256]{1,0:T(8,128)S(1)}, u32[]{:S(2)}, u32[]{:S(2)}) collective-permute-start(f32[144,256]{1,0:T(8,128)S(1)} %get-tuple-element.34.after), channel_id=1, source_target_pairs={{0,64},{1,65},{2,66},{3,67},{4,68},{5,69},{6,70},{7,71},{8,72},{9,... | collective-permute-start | bytes 442376 | tf_op jit(solution)/shard_map/ppermute | solution.py:483
  84.0 5.6 %shard_map.98.pair = f32[2,528,256]{2,1,0:T(8,128)S(1)} custom-call(s32[1]{0:T(128)} %bitcast.here.after, f32[528,256]{1,0:T(8,128)S(1)} %get-tuple-element.35.theirs, f32[528,256]{1,0:T(8,128)S(1)} %shard_map.96.after.low, f32[2,528,256]{2,1,0:T(8,128)S(1)} %shard_map.90.after.pair, f32[144,256]{1,0:T(8,128)S(1)} %get-tuple-element.34.after), custom_call_target="tpu_custom_call" | custom-call | flops 4227858432 | bytes 524288 | tf_op jit(solution)/shard_map/pallas_call | solution.py:485
  89.7 0.0 collective-permute-done.17.state_b
  89.7 0.0 collective-permute-done.16.state_a
  89.7 5.9 %shard_map.99 = (f32[2,256]{1,0:T(2,128)}, f32[2,256,256]{2,1,0:T(8,128)}) custom-call(s32[1]{0:T(128)} %bitcast.here.after, f32[144,256]{1,0:T(8,128)S(1)} %collective-permute-done.16.state_a, f32[144,256]{1,0:T(8,128)S(1)} %collective-permute-done.17.state_b, f32[1,256]{1,0:T(1,128)S(1)} %bitcast.3, f32[256,256]{1,0:T(8,128)S(1)} %copy-done, ...), custom_call_target="tpu_custom_call" | custom-call | flops 2415919104 | bytes 524288 | tf_op jit(solution)/shard_map/pallas_call | solution.py:486
Async XLA Ops:
  5.7 8.9 %collective-permute-start.1 = (f32[272,256]{1,0:T(8,128)S(1)}, f32[272,256]{1,0:T(8,128)S(1)}, u32[]{:S(2)}, u32[]{:S(2)}) collective-permute-start(f32[272,256]{1,0:T(8,128)S(1)} %get-tuple-element.20.mb), channel_id=1, source_target_pairs={{0,1},{1,2},{2,3},{3,0},{4,5},{5,6},{6,7},{7,4},{8,9},{9,10},{10,1... | collective-permute-start | bytes 835592 | tf_op jit(solution)/shard_map/ppermute | solution.py:433
  7.1 7.6 %collective-permute-start.2 = (f32[256,256]{1,0:T(8,128)S(1)}, f32[256,256]{1,0:T(8,128)S(1)}, u32[]{:S(2)}, u32[]{:S(2)}) collective-permute-start(f32[256,256]{1,0:T(8,128)S(1)} %get-tuple-element.19.ma), channel_id=1, source_target_pairs={{0,3},{1,0},{2,1},{3,2},{4,7},{5,4},{6,5},{7,6},{8,11},{9,8},{10,9... | collective-permute-start | bytes 786440 | tf_op jit(solution)/shard_map/ppermute | solution.py:433
  8.6 11.7 %collective-permute-start.3 = (f32[272,256]{1,0:T(8,128)S(1)}, f32[272,256]{1,0:T(8,128)S(1)}, u32[]{:S(2)}, u32[]{:S(2)}) collective-permute-start(f32[272,256]{1,0:T(8,128)S(1)} %get-tuple-element.20.mb), channel_id=1, source_target_pairs={{0,3},{1,0},{2,1},{3,2},{4,7},{5,4},{6,5},{7,6},{8,11},{9,8},{10,9... | collective-permute-start | bytes 835592 | tf_op jit(solution)/shard_map/ppermute | solution.py:433
  10.0 10.3 %collective-permute-start = (f32[256,256]{1,0:T(8,128)S(1)}, f32[256,256]{1,0:T(8,128)S(1)}, u32[]{:S(2)}, u32[]{:S(2)}) collective-permute-start(f32[256,256]{1,0:T(8,128)S(1)} %get-tuple-element.19.ma), channel_id=1, source_target_pairs={{0,1},{1,2},{2,3},{3,0},{4,5},{5,6},{6,7},{7,4},{8,9},{9,10},{10,1... | collective-permute-start | bytes 786440 | tf_op jit(solution)/shard_map/ppermute | solution.py:433
  14.7 11.6 %collective-permute-start.5 = (f32[272,256]{1,0:T(8,128)S(1)}, f32[272,256]{1,0:T(8,128)S(1)}, u32[]{:S(2)}, u32[]{:S(2)}) collective-permute-start(f32[272,256]{1,0:T(8,128)S(1)} %collective-permute-done.1.pb.tb), channel_id=1, source_target_pairs={{0,1},{1,2},{2,3},{3,0},{4,5},{5,6},{6,7},{7,4},{8,9},{9,10},{10,1... | collective-permute-start | bytes 835592 | tf_op jit(solution)/shard_map/ppermute | solution.py:433
  14.7 10.9 %collective-permute-start.4 = (f32[256,256]{1,0:T(8,128)S(1)}, f32[256,256]{1,0:T(8,128)S(1)}, u32[]{:S(2)}, u32[]{:S(2)}) collective-permute-start(f32[256,256]{1,0:T(8,128)S(1)} %collective-permute-done.2.na), channel_id=1, source_target_pairs={{0,3},{1,0},{2,1},{3,2},{4,7},{5,4},{6,5},{7,6},{8,11},{9,8},{10,9... | collective-permute-start | bytes 786440 | tf_op jit(solution)/shard_map/ppermute | solution.py:433
  30.6 7.8 %collective-permute-start.7 = (f32[272,256]{1,0:T(8,128)S(1)}, f32[272,256]{1,0:T(8,128)S(1)}, u32[]{:S(2)}, u32[]{:S(2)}) collective-permute-start(f32[272,256]{1,0:T(8,128)S(1)} %get-tuple-element.22.mb), channel_id=1, source_target_pairs={{0,4},{4,8},{8,12},{12,0},{1,5},{5,9},{9,13},{13,1},{2,6},{6,10},{... | collective-permute-start | bytes 835592 | tf_op jit(solution)/shard_map/ppermute | solution.py:433
  30.7 7.7 %collective-permute-start.8 = (f32[256,256]{1,0:T(8,128)S(1)}, f32[256,256]{1,0:T(8,128)S(1)}, u32[]{:S(2)}, u32[]{:S(2)}) collective-permute-start(f32[256,256]{1,0:T(8,128)S(1)} %get-tuple-element.21.after.ma), channel_id=1, source_target_pairs={{0,12},{4,0},{8,4},{12,8},{1,13},{5,1},{9,5},{13,9},{2,14},{6,2},{... | collective-permute-start | bytes 786440 | tf_op jit(solution)/shard_map/ppermute | solution.py:433
  32.1 10.9 %collective-permute-start.6 = (f32[256,256]{1,0:T(8,128)S(1)}, f32[256,256]{1,0:T(8,128)S(1)}, u32[]{:S(2)}, u32[]{:S(2)}) collective-permute-start(f32[256,256]{1,0:T(8,128)S(1)} %get-tuple-element.21.after.ma), channel_id=1, source_target_pairs={{0,4},{4,8},{8,12},{12,0},{1,5},{5,9},{9,13},{13,1},{2,6},{6,10},{... | collective-permute-start | bytes 786440 | tf_op jit(solution)/shard_map/ppermute | solution.py:433
  33.4 10.9 %collective-permute-start.9 = (f32[272,256]{1,0:T(8,128)S(1)}, f32[272,256]{1,0:T(8,128)S(1)}, u32[]{:S(2)}, u32[]{:S(2)}) collective-permute-start(f32[272,256]{1,0:T(8,128)S(1)} %get-tuple-element.22.mb), channel_id=1, source_target_pairs={{0,12},{4,0},{8,4},{12,8},{1,13},{5,1},{9,5},{13,9},{2,14},{6,2},{... | collective-permute-start | bytes 835592 | tf_op jit(solution)/shard_map/ppermute | solution.py:433
  38.3 11.6 %collective-permute-start.10 = (f32[256,256]{1,0:T(8,128)S(1)}, f32[256,256]{1,0:T(8,128)S(1)}, u32[]{:S(2)}, u32[]{:S(2)}) collective-permute-start(f32[256,256]{1,0:T(8,128)S(1)} %collective-permute-done.8.na), channel_id=1, source_target_pairs={{0,12},{4,0},{8,4},{12,8},{1,13},{5,1},{9,5},{13,9},{2,14},{6,2},{... | collective-permute-start | bytes 786440 | tf_op jit(solution)/shard_map/ppermute | solution.py:433
  38.3 11.6 %collective-permute-start.11 = (f32[272,256]{1,0:T(8,128)S(1)}, f32[272,256]{1,0:T(8,128)S(1)}, u32[]{:S(2)}, u32[]{:S(2)}) collective-permute-start(f32[272,256]{1,0:T(8,128)S(1)} %collective-permute-done.7.pb), channel_id=1, source_target_pairs={{0,4},{4,8},{8,12},{12,0},{1,5},{5,9},{9,13},{13,1},{2,6},{6,10},{... | collective-permute-start | bytes 835592 | tf_op jit(solution)/shard_map/ppermute | solution.py:433
  55.5 4.6 %collective-permute-start.13 = (f32[272,256]{1,0:T(8,128)S(1)}, f32[272,256]{1,0:T(8,128)S(1)}, u32[]{:S(2)}, u32[]{:S(2)}) collective-permute-start(f32[272,256]{1,0:T(8,128)S(1)} %get-tuple-element.27.mb), channel_id=1, source_target_pairs={{0,16},{16,0},{1,17},{17,1},{2,18},{18,2},{3,19},{19,3},{4,20},{20... | collective-permute-start | bytes 835592 | tf_op jit(solution)/shard_map/ppermute | solution.py:429
  57.3 2.8 %collective-permute-start.12 = (f32[256,256]{1,0:T(8,128)S(1)}, f32[256,256]{1,0:T(8,128)S(1)}, u32[]{:S(2)}, u32[]{:S(2)}) collective-permute-start(f32[256,256]{1,0:T(8,128)S(1)} %get-tuple-element.26.after.ma), channel_id=1, source_target_pairs={{0,16},{16,0},{1,17},{17,1},{2,18},{18,2},{3,19},{19,3},{4,20},{20... | collective-permute-start | bytes 786440 | tf_op jit(solution)/shard_map/ppermute | solution.py:429
  60.1 12.0 %copy-start = (f32[256,256]{1,0:T(8,128)S(1)}, f32[256,256]{1,0:T(8,128)}, u32[]{:S(2)}) copy-start(f32[256,256]{1,0:T(8,128)} %cov.3) | copy-start | bytes 786436
  60.1 12.0 %copy-start.1 = (f32[256]{0:T(256)S(1)}, f32[256]{0:T(256)}, u32[]{:S(2)}) copy-start(f32[256]{0:T(256)} %param.12) | copy-start | bytes 3076
  63.1 8.4 %collective-permute-start.14 = (f32[264,256]{1,0:T(8,128)S(1)}, f32[264,256]{1,0:T(8,128)S(1)}, u32[]{:S(2)}, u32[]{:S(2)}) collective-permute-start(f32[264,256]{1,0:T(8,128)S(1)} %get-tuple-element.30), channel_id=1, source_target_pairs={{0,32},{32,0},{64,96},{96,64},{1,33},{33,1},{65,97},{97,65},{2,34}... | collective-permute-start | bytes 811016 | tf_op jit(solution)/shard_map/ppermute | solution.py:429
  71.5 6.6 %collective-permute-start.15 = (f32[264,256]{1,0:T(8,128)S(1)}, f32[264,256]{1,0:T(8,128)S(1)}, u32[]{:S(2)}, u32[]{:S(2)}) collective-permute-start(f32[264,256]{1,0:T(8,128)S(1)} %collective-permute-done.14.mine), channel_id=1, source_target_pairs={{0,16},{16,0},{1,17},{17,1},{2,18},{18,2},{3,19},{19,3},{4,20},{20... | collective-permute-start | bytes 811016 | tf_op jit(solution)/shard_map/ppermute | solution.py:429
  81.4 8.2 %collective-permute-start.17 = (f32[144,256]{1,0:T(8,128)S(1)}, f32[144,256]{1,0:T(8,128)S(1)}, u32[]{:S(2)}, u32[]{:S(2)}) collective-permute-start(f32[144,256]{1,0:T(8,128)S(1)} %get-tuple-element.34.after), channel_id=1, source_target_pairs={{0,96},{1,97},{2,98},{3,99},{4,100},{5,101},{6,102},{7,103},{8,104... | collective-permute-start | bytes 442376 | tf_op jit(solution)/shard_map/ppermute | solution.py:484
  82.7 6.9 %collective-permute-start.16 = (f32[144,256]{1,0:T(8,128)S(1)}, f32[144,256]{1,0:T(8,128)S(1)}, u32[]{:S(2)}, u32[]{:S(2)}) collective-permute-start(f32[144,256]{1,0:T(8,128)S(1)} %get-tuple-element.34.after), channel_id=1, source_target_pairs={{0,64},{1,65},{2,66},{3,67},{4,68},{5,69},{6,70},{7,71},{8,72},{9,... | collective-permute-start | bytes 442376 | tf_op jit(solution)/shard_map/ppermute | solution.py:483

commit v3 on v2

--- a/solution.py
+++ b/solution.py
@@ -14,7 +14,7 @@
 O = 64
 V = 16
 ROWS = 2 * N + V
-TOL = 1e-6
+TOL = 1e-5
 F32 = jnp.float32
 BF16 = jnp.bfloat16
 
@@ -43,37 +43,59 @@
     )
 
 
-def resolvents(coupled, stacks):
+def norm(array):
+    return jnp.sqrt(jnp.sum(array * array))
+
+
+def resolvents(coupled, stacks, tight=True):
     n = coupled[0].shape[0]
     row, col = row_col(n)
     eye = jnp.where(row == col, 1.0, 0.0).astype(F32)
-    rate = jnp.float32(0.0)
-    for each, stack in zip(coupled, stacks):
-        size = jnp.abs(each)
-        bound = jnp.minimum(
-            jnp.max(jnp.sum(size, axis=0, keepdims=True)), jnp.sqrt(jnp.sum(size * size))
-        )
-        scale = 2.0 / (2.0 + bound)
-        error = eye - scale * (eye + each)
-        stack[0:n, :] = scale * (eye + error)
-        stack[n:, :] = error
-        rate = jnp.maximum(rate, jnp.minimum(bound * scale * 0.5, 0.9999998))
-
-    @pl.when(rate * rate > TOL)
+    bound = norm(coupled[0])
+    for each in coupled[1:]:
+        bound = jnp.maximum(bound, norm(each))
+
+    def rate_of(bound):
+        return jnp.minimum(bound * bound / (bound * bound + 8.0 * bound + 8.0), 0.9999998)
+
+    def start(bound):
+        scale = 1.0 / (bound * bound + 8.0 * bound + 8.0)
+        for each, stack in zip(coupled, stacks):
+            stack[0:n, :] = (8.0 * scale) * ((bound + 1.0) * eye - each)
+        return scale
+
+    loose = rate_of(bound)
+    start(bound)
+
+    @pl.when(loose > TOL)
     def _():
-        for stack in stacks:
-            factor = split(stack[n:, :])
-            stack[n:, :] = dot3(factor, factor)
-
-    def sweep(rate):
-        for stack in stacks:
-            both = split(stack[...])
-            fresh = dot3(both, (both[0][n:], both[1][n:]))
-            stack[0:n, :] = stack[0:n, :] + fresh[0:n]
-            stack[n:, :] = fresh[n:]
-        return rate * rate
-
-    lax.while_loop(lambda rate: rate > TOL, sweep, rate * rate)
+        for each, stack in zip(coupled, stacks):
+            each2 = split(each)
+            stack[n:, :] = dot3(each2, each2)
+
+        def tighten():
+            squared = norm(stacks[0][n:, :])
+            for stack in stacks[1:]:
+                squared = jnp.maximum(squared, norm(stack[n:, :]))
+            return jnp.minimum(bound, jnp.sqrt(squared))
+
+        tighter = lax.cond(loose * loose > TOL, tighten, lambda: bound) if tight else bound
+        scale = start(tighter)
+        for each, stack in zip(coupled, stacks):
+            stack[n:, :] = (tighter * tighter * scale) * eye + (8.0 * scale) * (
+                stack[n:, :] - tighter * each
+            )
+
+        def sweep(rate):
+            for stack in stacks:
+                both = split(stack[...])
+                fresh = dot3(both, (both[0][n:], both[1][n:]))
+                stack[0:n, :] = stack[0:n, :] + fresh[0:n]
+                stack[n:, :] = fresh[n:]
+            return rate * rate
+
+        lax.while_loop(lambda rate: rate > TOL, sweep, rate_of(tighter))
+
     return [stack[0:n, :] for stack in stacks]
 
 
@@ -102,14 +124,14 @@
     return ref.at[0:N], ref.at[N:]
 
 
-def combine(firsts, seconds, stacks):
+def combine(firsts, seconds, stacks, tight=True):
     pairs = []
     for (move_a, spr_a, mat_a, vecs_a), (move_b, spr_b, mat_b, vecs_b) in zip(firsts, seconds):
         move_a2, spr_a2, mat_b2 = split(move_a), split(spr_a), split(mat_b)
         up = dot3(rows(mat_b2, split(vecs_b)), spr_a2)
         seen = dot3(rows(move_a2, split(vecs_a)), mat_b2)
         pairs.append((up, seen, move_a2, spr_a2))
-    settled = resolvents([pair[0][0:N] for pair in pairs], stacks)
+    settled = resolvents([pair[0][0:N] for pair in pairs], stacks, tight)
     out = []
     for first, second, pair, settle in zip(firsts, seconds, pairs, settled):
         up, seen, move_a2, spr_a2 = pair
@@ -168,16 +190,18 @@
     ]
     for copy in copies:
         copy.start()
-    for copy in copies:
-        copy.wait()
+    for k in (0, 1, 3, 4):
+        copies[k].wait()
     state = noise_state[...]
     state2 = split(state)
     place = lax.broadcasted_iota(jnp.int32, (V, N), 0)
     row, col = row_col(O)
     found = []
+    sensors = [split(obs[k]) for k in range(2)]
+    all_sensed = [dot3(sensor2, state2) for sensor2 in sensors]
+    copies[2].wait()
     for k in range(2):
-        sensor2 = split(obs[k])
-        sensed = dot3(sensor2, state2)
+        sensor2, sensed = sensors[k], all_sensed[k]
         seen = dot3(sensor2, split(trans[k]))
         inner = dot3(split(sensed), sensor2, ((1,), (1,)))
         variance = noise[k : k + 1, :]
@@ -185,7 +209,7 @@
         root = root * (1.5 - 0.5 * variance * root * root)
         root_col = jnp.sum(jnp.where(row == col, root, 0.0), axis=1, keepdims=True)
         found.append((sensed, seen, root_col * inner * root, root, root_col))
-    inverses = resolvents([part[2] for part in found], (small_a, small_b))
+    inverses = resolvents([part[2] for part in found], (small_a, small_b), False)
     steps = []
     for k in range(2):
         sensed, seen, _, root, root_col = found[k]
@@ -200,7 +224,7 @@
         steps.append((trans[k].T - full[0:N, N:], state - full[N:, N:], full[0:N, 0:N], vecs))
     move, spread, info, vecs = steps[0]
     pack(*parts(pair.at[0]), move, spread, info, vecs[0:1], vecs[1:2])
-    pack(move_ref, side_ref, *combine(steps[0:1], steps[1:2], [stack])[0])
+    pack(move_ref, side_ref, *combine(steps[0:1], steps[1:2], [stack], False)[0])
     pair[1, 0:N, :] = move_ref[...]
     pair[1, N:, :] = side_ref[...]
 
@@ -208,12 +232,6 @@
 def upper(here, axis, step):
     shift = {"x": 5, "c": 4, "z": 2, "y": 0}[axis] + step // 2
     return ((here[0] >> shift) & 1) == 1
-
-
-def sort(flag, ones, others, first, second):
-    for half, one, other in zip((slice(0, N), slice(N, ROWS)), ones, others):
-        first[half, :] = jnp.where(flag, other[...], one[...])
-        second[half, :] = jnp.where(flag, one[...], other[...])
 
 
 def own_kernel(axis, here, ma, mb, pa, pb, na, nb, after, out, first, second, stack):
@@ -221,11 +239,12 @@
     for half, mine, prev, later in zip((slice(0, N), slice(N, ROWS)), (ma, mb), (pa, pb), (na, nb)):
         first[half, :] = jnp.where(odd, prev[...], mine[...])
         second[half, :] = jnp.where(odd, mine[...], later[...])
-    done = combine([unpack(*parts(first))], [unpack(*parts(second))], [stack])
+    done = combine([unpack(*parts(first))], [unpack(*parts(second))], [stack], False)
     pack(*parts(out), *done[0])
 
 
-def ring_kernel(axis, here, own, pa, pb, na, nb, fa, fb, out_a, out_b, other_a, other_b, held_ref, stack):
+def ring_kernel(axis, here, own, pa, pb, na, nb, fa, fb, *refs):
+    *out, other_a, other_b, held_ref, stack = refs
     odd, late = upper(here, axis, 1), upper(here, axis, 2)
     for half, prev, later, far in zip((slice(0, N), slice(N, ROWS)), (pa, pb), (na, nb), (fa, fb)):
         held_ref[0, half, :] = jnp.where(odd, later[...], far[...])
@@ -236,40 +255,39 @@
     def one(k, carry):
         first = held_ref.at[k * (3 - swapped)]
         second = held_ref.at[1 + k * (1 + swapped)]
-        done = combine([unpack(*parts(first))], [unpack(*parts(second))], [stack])
+        done = combine([unpack(*parts(first))], [unpack(*parts(second))], [stack], False)
         pack(*parts(held_ref.at[2 + 2 * k]), *done[0])
         return carry
 
     lax.fori_loop(0, 2, one, 0)
     other_a[...] = held_ref[2, 0:N, :]
     other_b[...] = held_ref[2, N:, :]
-    out_a[...] = held_ref[4, 0:N, :]
-    out_b[...] = held_ref[4, N:, :]
-
-
-def core_kernel(here, ma, mb, ta, tb, after, out, half, first, second, stack):
+    if len(out) == 1:
+        out[0][...] = held_ref[4]
+    else:
+        out[0][...] = held_ref[4, 0:N, :]
+        out[1][...] = held_ref[4, N:, :]
+
+
+def core_kernel(here, mine, theirs, after, out, half, first, second, stack):
     flag = upper(here, "c", 1)
-    sort(flag, (ma, mb), (ta, tb), first, second)
-    done = combine([unpack(*parts(first))], [unpack(*parts(second))], [stack])
+    first[...] = jnp.where(flag, theirs[...], mine[...])
+    second[...] = jnp.where(flag, mine[...], theirs[...])
+    done = combine([unpack(*parts(first))], [unpack(*parts(second))], [stack], False)
     pack(*parts(out), *done[0])
     half[...] = jnp.where(flag, out[HALF:, :], out[0:HALF, :])
 
 
-def slow_kernel(axis, step, here, ta, tb, pair, after, out, stack):
-    flag = upper(here, axis, step)
-
-    @pl.when(flag)
-    def _():
-        def one(k, carry):
-            done = combine([unpack(ta, tb)], [unpack(*parts(pair.at[k]))], [stack])
-            pack(*parts(out.at[k]), *done[0])
-            return carry
-
-        lax.fori_loop(0, 2, one, 0)
-
-    @pl.when(jnp.logical_not(flag))
-    def _():
-        out[...] = pair[...]
+def slow_kernel(step, here, ta, tb, pair, after, out, stack):
+    out[...] = pair[...]
+
+    def one(k, carry):
+        second = out.at[k]
+        done = combine([unpack(ta, tb)], [unpack(*parts(second))], [stack], False)
+        pack(*parts(second), *done[0])
+        return carry
+
+    lax.fori_loop(0, 2 * upper(here, "y", step).astype(jnp.int32), one, 0)
 
 
 def held(here, axes):
@@ -286,7 +304,7 @@
 def merge_into(out, has_early, has_late, early, late, stack):
     @pl.when(jnp.logical_and(has_early, has_late))
     def _():
-        pack(*parts(out), *combine([unpack(*early)], [unpack(*late)], [stack])[0])
+        pack(*parts(out), *combine([unpack(*early)], [unpack(*late)], [stack], False)[0])
 
     @pl.when(jnp.logical_not(has_early))
     def _():
@@ -303,46 +321,57 @@
     merge_into(out, upper(here, "z", 2), upper(here, "z", 1), (oa, ob), (pa, pb), stack)
 
 
-def cored_kernel(here, ta, tb, low, after, out, stack):
-    merge_into(out, upper(here, "c", 1), held(here, Z_LEVEL), (ta, tb), parts(low), stack)
-
-
-def steps_kernel(here, theirs, low, pair, after, out, held_ref, stack):
-    x_up = upper(here, "x", 1)
-    has_low = held(here, CORE_LEVEL)
+def cored_kernel(here, theirs, low, pair, after, low_out, out, held_ref, stack):
+    c_up, has_low = upper(here, "c", 1), held(here, Z_LEVEL)
     held_ref[0] = theirs[...]
     held_ref[1] = low[...]
     held_ref[3:5] = pair[...]
-    both = jnp.logical_and(x_up, has_low)
-    either = jnp.logical_or(x_up, has_low)
+    both = jnp.logical_and(c_up, has_low)
+    steps = jnp.logical_and(jnp.logical_or(c_up, has_low), jnp.logical_not(is_first(here)))
     source = jnp.where(both, 2, jnp.where(has_low, 1, 0))
 
     def one(k, carry):
         first = held_ref.at[jnp.where(k == 0, 0, source)]
         second = held_ref.at[jnp.where(k == 0, 1, k + 2)]
-        done = combine([unpack(*parts(first))], [unpack(*parts(second))], [stack])
+        done = combine([unpack(*parts(first))], [unpack(*parts(second))], [stack], False)
         pack(*parts(held_ref.at[k + 2]), *done[0])
         return carry
 
-    lax.fori_loop(jnp.where(both, 0, 1), jnp.where(either, 3, 1), one, 0)
+    lax.fori_loop(jnp.where(both, 0, 1), jnp.where(steps, 3, 1), one, 0)
+    low_out[...] = held_ref[source]
     out[...] = held_ref[3:5]
+
+
+def steps_kernel(here, theirs, pair, after, out, stack):
+    out[...] = pair[...]
+
+    def one(k, carry):
+        second = out.at[k]
+        done = combine([unpack(*parts(theirs))], [unpack(*parts(second))], [stack])
+        pack(*parts(second), *done[0])
+        return carry
+
+    lax.fori_loop(0, 2 * upper(here, "x", 1).astype(jnp.int32), one, 0)
 
 
 def is_first(here):
     return (here[0] >> 5) == 0
 
 
-def prior_kernel(here, whole, mean, cov, mean_out, cov_out, stack):
-    @pl.when(is_first(here))
-    def _():
-        state = jnp.broadcast_to(mean[...], (V, N))
-        done = apply_state(state, cov[...], [unpack(*parts(whole))], [stack])
-        mean_out[...], cov_out[...] = done[0]
-
-    @pl.when(jnp.logical_not(is_first(here)))
-    def _():
-        mean_out[...] = jnp.broadcast_to(mean[...], (V, N))
-        cov_out[...] = cov[...]
+def prior_kernel(here, whole, low, mean, cov, means, covs, held_ref, stack):
+    state = jnp.broadcast_to(mean[...], (V, N))
+    for k, ref in enumerate((whole, low)):
+        held_ref[k] = ref[...]
+        means[k] = state
+        covs[k] = cov[...]
+
+    def one(k, carry):
+        done = apply_state(state, cov[...], [unpack(*parts(held_ref.at[k]))], [stack])
+        means[k], covs[k] = done[0]
+        return carry
+
+    count = 1 + held(here, CORE_LEVEL).astype(jnp.int32)
+    lax.fori_loop(0, jnp.where(is_first(here), count, 0), one, 0)
 
 
 HN = N // 2
@@ -356,7 +385,7 @@
     @pl.when(is_first(here))
     def _():
         mean_b, cov_b = apply_state(
-            mean[...], cov[...], [unpack(*parts(theirs))], [stack]
+            mean[0], cov[0], [unpack(*parts(theirs))], [stack]
         )[0]
         row, col = row_col(HN)
         last = cov_b[HN:, HN:]
@@ -381,11 +410,11 @@
     last = jnp.where(
         row == col, packed[HN + 8 : HN + 9, 0:HN], jnp.where(row > col, mixed, turned)
     )
-    prior[0:HN, 0:HN] = jnp.where(flag, jnp.where(row <= col, mixed, turned), cov[0:HN, 0:HN])
-    prior[0:HN, HN:] = jnp.where(flag, side, cov[0:HN, HN:])
-    prior[HN:, 0:HN] = jnp.where(flag, side.T, cov[HN:, 0:HN])
-    prior[HN:, HN:] = jnp.where(flag, last, cov[HN:, HN:])
-    mean_in = jnp.broadcast_to(jnp.where(flag, packed[HN : HN + 1, :], mean[...]), (V, N))
+    prior[0:HN, 0:HN] = jnp.where(flag, jnp.where(row <= col, mixed, turned), cov[1, 0:HN, 0:HN])
+    prior[0:HN, HN:] = jnp.where(flag, side, cov[1, 0:HN, HN:])
+    prior[HN:, 0:HN] = jnp.where(flag, side.T, cov[1, HN:, 0:HN])
+    prior[HN:, HN:] = jnp.where(flag, last, cov[1, HN:, HN:])
+    mean_in = jnp.broadcast_to(jnp.where(flag, packed[HN : HN + 1, :], mean[1, 0:1, :]), (V, N))
     seconds = [unpack(*parts(pair.at[k])) for k in range(2)]
     done = apply_state(mean_in, prior[...], seconds, [stack, stack_b])
     for k in range(2):
@@ -441,17 +470,18 @@
         near = (prev_a, prev_b, later_a, later_b)
         own = call(kernel, "svvvvvva", [ELEMENT], scratch, 14)(here, *mine, *near, after)
         kernel = functools.partial(ring_kernel, axis)
-        run = call(kernel, "svvvvvvv", [MOVE, SIDE] * 2, [(5, *ELEMENT), STACK], 28)
-        whole_a, whole_b, *other = run(here, own, *near, far_a, far_b)
-        return (whole_a, whole_b), (prev_a, prev_b), other
-
-    def slow(axis, step, theirs, pair, after):
-        kernel = functools.partial(slow_kernel, axis, step)
+        outs = ([MOVE, SIDE] if axis == "y" else [ELEMENT]) + [MOVE, SIDE]
+        run = call(kernel, "svvvvvvv", outs, [(5, *ELEMENT), STACK], 28)
+        *whole, other_a, other_b = run(here, own, *near, far_a, far_b)
+        return whole, (prev_a, prev_b), (other_a, other_b)
+
+    def slow(step, theirs, pair, after):
+        kernel = functools.partial(slow_kernel, step)
         return call(kernel, "svvva", [PAIR], [STACK], 28)(here, *theirs, pair, after)
 
     ringed = call(ringed_kernel, "svvvva", [ELEMENT], [STACK], 14)
-    cored = call(cored_kernel, "svvva", [ELEMENT], [STACK], 14)
-    steps = call(steps_kernel, "svvva", [PAIR], [(5, *ELEMENT), STACK], 42)
+    cored = call(cored_kernel, "svvva", [ELEMENT, PAIR], [(5, *ELEMENT), STACK], 42)
+    steps = call(steps_kernel, "svva", [PAIR], [STACK], 28)
 
     inputs = [(2, N, N), (2, O, N), (2, O), (2, O), (N, N)]
     build = call(
@@ -461,29 +491,29 @@
         inputs + [pltpu.SemaphoreType.DMA((5,)), STACK, (2 * O, O), (2 * O, O)],
         30,
     )
-    core = call(core_kernel, "svvvva", [ELEMENT, (HALF, N)], [ELEMENT, ELEMENT, STACK], 14)
-    prior = call(prior_kernel, "svvv", [(V, N), (N, N)], [STACK], 14)
+    core = call(core_kernel, "svva", [ELEMENT, (HALF, N)], [ELEMENT, ELEMENT, STACK], 14)
+    prior = call(prior_kernel, "svvvv", [(2, V, N), (2, N, N)], [(2, *ELEMENT), STACK], 28)
     second = call(second_kernel, "svvvva", [ELEMENT, PACKED], [STACK], 14)
     final = call(final_kernel, "svvvvv", [(2, N), (2, N, N)], [PACKED, (N, N), STACK, STACK], 24)
 
     arrays = (transition, observe, noise_obs, measured, noise_state)
     *whole, pair = build(*(pltpu.with_memory_space_constraint(a, pltpu.HBM) for a in arrays))
     whole, prev, other = ring("y", whole, here)
-    pair = slow("y", 1, prev, pair, whole[0])
-    pair = slow("y", 2, other, pair, whole[0])
+    pair = slow(1, prev, pair, whole[0])
+    pair = slow(2, other, pair, whole[0])
     whole, prev, other = ring("z", whole, pair)
-    c1 = [swap(half, "c", 1) for half in whole]
+    c1 = swap(whole[0], "c", 1)
     low = ringed(here, *other, *prev, whole[0])
-    whole, half = core(here, *whole, *c1, low)
+    whole, half = core(here, whole[0], c1, low)
     x1 = swap(half, "x", 1)
-    mean_a, cov_a = prior(here, whole, mean, prior_cov)
-    low = cored(here, *c1, low, mean_a)
+    low, pair = cored(here, c1, low, pair, whole)
+    means, covs = prior(here, whole, low, mean, prior_cov)
     x1_other = swap(x1, "c", 1)
-    theirs, packed = second(here, x1, x1_other, mean_a, cov_a, low)
+    theirs, packed = second(here, x1, x1_other, means, covs, pair)
     state_a = lax.ppermute(packed, "x", [(0, 2)])
     state_b = lax.ppermute(packed, "x", [(0, 3)])
-    pair = steps(here, theirs, low, pair, packed)
-    return final(here, state_a, state_b, mean, prior_cov, pair)
+    pair = steps(here, theirs, pair, packed)
+    return final(here, state_a, state_b, means, covs, pair)
 
 
 def solution(mesh):

time: 95.8 us -> 93.7 us (0.978)
  the two profiles are of different devices: /device:TPU:97 before, /device:TPU:101 now
where the time goes in v3:
time: 93.7 us; the launch traced here: 93.5 us
  waiting for transfers between devices  37.9 us (40%)
  Pallas kernels  35.8 us (38%)
  starting transfers between devices  18.9 us (20%)
    ppermute x12, waiting for transfers between devices, turn(): return lax.ppermute(part, axis, [(k, (k + step) % 4) for k in range(4)])  22.7 us
    ppermute x12, starting transfers between devices, turn(): return lax.ppermute(part, axis, [(k, (k + step) % 4) for k in range(4)])  12.7 us
    pallas_call x2, Pallas kernels, ring(): *whole, other_a, other_b = run(here, own, *near, far_a, far_b)  8.5 us
    ppermute x3, waiting for transfers between devices, swap(): return lax.ppermute(part, axis, [(k, k ^ step) for k in range(size)])  7.79 us
    ppermute x1, waiting for transfers between devices, on_device(): state_a = lax.ppermute(packed, 'x', [(0, 2)])  7.45 us
    pallas_call x1, Pallas kernels, on_device(): low, pair = cored(here, c1, low, pair, whole)  6.98 us
    pallas_call x1, Pallas kernels, on_device(): return final(here, state_a, state_b, means, covs, pair)  5.74 us
    pallas_call x1, Pallas kernels, on_device(): build(*(pltpu.with_memory_space_constraint(a, pltpu.HBM) for a in arrays))  4.91 us
  transfers between devices with their start and end apart: 17, of which 10 were waited for; matrix products, arithmetic and copies ran while one was open for 0% of the time, Pallas kernels for 15%

profile of v3, /device:TPU:101, one launch (start us, length us, event | category | flops | bytes accessed | tf_op | source)
XLA Modules:
  0.0 93.5 jit_solution(6699214137450456460)
XLA Ops:
  0.6 4.9 %shard_map.86 = (f32[256,256]{1,0:T(8,128)S(1)}, f32[272,256]{1,0:T(8,128)S(1)}, f32[2,528,256]{2,1,0:T(8,128)S(1)}) custom-call(f32[2,256,256]{2,1,0:T(8,128)} %trans_in.1, f32[2,64,256]{2,1,0:T(8,128)} %obs_in.1, f32[2,64]{1,0:T(2,128)} %noise_in.1, f32[2,64]{1,0:T(2,128)} %meas_in.1, f32[256,256]{1,0:T(8,128)} %state_in.1), custom_call_target="tpu_custom_call" | custom-call | flops 3019898880 | bytes 524288 | tf_op jit(solution)/shard_map/pallas_call | solution.py:500
  5.6 1.4 %collective-permute-start.1 = (f32[272,256]{1,0:T(8,128)S(1)}, f32[272,256]{1,0:T(8,128)S(1)}, u32[]{:S(2)}, u32[]{:S(2)}) collective-permute-start(f32[272,256]{1,0:T(8,128)S(1)} %get-tuple-element.21.mb), channel_id=1, source_target_pairs={{0,1},{1,2},{2,3},{3,0},{4,5},{5,6},{6,7},{7,4},{8,9},{9,10},{10,1... | collective-permute-start | bytes 835592 | tf_op jit(solution)/shard_map/ppermute | solution.py:462
  6.9 1.5 %collective-permute-start.2 = (f32[256,256]{1,0:T(8,128)S(1)}, f32[256,256]{1,0:T(8,128)S(1)}, u32[]{:S(2)}, u32[]{:S(2)}) collective-permute-start(f32[256,256]{1,0:T(8,128)S(1)} %get-tuple-element.20.ma), channel_id=1, source_target_pairs={{0,3},{1,0},{2,1},{3,2},{4,7},{5,4},{6,5},{7,6},{8,11},{9,8},{10,9... | collective-permute-start | bytes 786440 | tf_op jit(solution)/shard_map/ppermute | solution.py:462
  8.4 1.4 %collective-permute-start.3 = (f32[272,256]{1,0:T(8,128)S(1)}, f32[272,256]{1,0:T(8,128)S(1)}, u32[]{:S(2)}, u32[]{:S(2)}) collective-permute-start(f32[272,256]{1,0:T(8,128)S(1)} %get-tuple-element.21.mb), channel_id=1, source_target_pairs={{0,3},{1,0},{2,1},{3,2},{4,7},{5,4},{6,5},{7,6},{8,11},{9,8},{10,9... | collective-permute-start | bytes 835592 | tf_op jit(solution)/shard_map/ppermute | solution.py:462
  9.8 0.1 collective-permute-start
  9.9 4.6 %collective-permute-done.1.pb.tb = f32[272,256]{1,0:T(8,128)S(1)} collective-permute-done((f32[272,256]{1,0:T(8,128)S(1)}, f32[272,256]{1,0:T(8,128)S(1)}, u32[]{:S(2)}, u32[]{:S(2)}) %collective-permute-start.1) | collective-permute-done | bytes 278560 | tf_op jit(solution)/shard_map/ppermute | solution.py:462
  14.5 0.0 collective-permute-start.5
  14.5 0.0 collective-permute-done.2.na
  14.5 2.7 %collective-permute-start.4 = (f32[256,256]{1,0:T(8,128)S(1)}, f32[256,256]{1,0:T(8,128)S(1)}, u32[]{:S(2)}, u32[]{:S(2)}) collective-permute-start(f32[256,256]{1,0:T(8,128)S(1)} %collective-permute-done.2.na), channel_id=1, source_target_pairs={{0,3},{1,0},{2,1},{3,2},{4,7},{5,4},{6,5},{7,6},{8,11},{9,8},{10,9... | collective-permute-start | bytes 786440 | tf_op jit(solution)/shard_map/ppermute | solution.py:462
  17.2 2.9 %collective-permute-done.pa.ta = f32[256,256]{1,0:T(8,128)S(1)} collective-permute-done((f32[256,256]{1,0:T(8,128)S(1)}, f32[256,256]{1,0:T(8,128)S(1)}, u32[]{:S(2)}, u32[]{:S(2)}) %collective-permute-start) | collective-permute-done | bytes 262176 | tf_op jit(solution)/shard_map/ppermute | solution.py:462
  20.1 0.0 collective-permute-done.3.nb
  20.1 2.1 %shard_map.87.own = f32[528,256]{1,0:T(8,128)S(1)} custom-call(s32[1]{0:T(128)} %bitcast.here.after, f32[256,256]{1,0:T(8,128)S(1)} %get-tuple-element.20.ma, f32[272,256]{1,0:T(8,128)S(1)} %get-tuple-element.21.mb, f32[256,256]{1,0:T(8,128)S(1)} %collective-permute-done.pa.ta, f32[272,256]{1,0:T(8,128)S(1)} %collective-permute-done.1.pb.tb, ...), custom_call_target="tpu_custom_call" | custom-call | flops 1409286144 | bytes 524288 | tf_op jit(solution)/shard_map/pallas_call | solution.py:471
  22.2 3.2 %collective-permute-done.4.fa = f32[256,256]{1,0:T(8,128)S(1)} collective-permute-done((f32[256,256]{1,0:T(8,128)S(1)}, f32[256,256]{1,0:T(8,128)S(1)}, u32[]{:S(2)}, u32[]{:S(2)}) %collective-permute-start.4) | collective-permute-done | bytes 262176 | tf_op jit(solution)/shard_map/ppermute | solution.py:462
  25.4 0.7 collective-permute-done.5.fb
  26.1 4.2 %shard_map.88 = (f32[256,256]{1,0:T(8,128)S(1)}, f32[272,256]{1,0:T(8,128)S(1)}, f32[256,256]{1,0:T(8,128)S(1)}, f32[272,256]{1,0:T(8,128)S(1)}) custom-call(s32[1]{0:T(128)} %bitcast.here.after, f32[528,256]{1,0:T(8,128)S(1)} %shard_map.87.own, f32[256,256]{1,0:T(8,128)S(1)} %collective-permute-done.pa.ta, f32[272,256]{1,0:T(8,128)S(1)} %collective-permute-done.1.pb.tb, ...), custom_call_target="tpu_custom_call" | custom-call | flops 2818572288 | bytes 524288 | tf_op jit(solution)/shard_map/pallas_call | solution.py:475
  30.3 0.1 collective-permute-start.7
  30.4 1.5 %collective-permute-start.8 = (f32[256,256]{1,0:T(8,128)S(1)}, f32[256,256]{1,0:T(8,128)S(1)}, u32[]{:S(2)}, u32[]{:S(2)}) collective-permute-start(f32[256,256]{1,0:T(8,128)S(1)} %get-tuple-element.22.after.ma), channel_id=1, source_target_pairs={{0,12},{4,0},{8,4},{12,8},{1,13},{5,1},{9,5},{13,9},{2,14},{6,2},{... | collective-permute-start | bytes 786440 | tf_op jit(solution)/shard_map/ppermute | solution.py:462
  31.9 1.3 %collective-permute-start.6 = (f32[256,256]{1,0:T(8,128)S(1)}, f32[256,256]{1,0:T(8,128)S(1)}, u32[]{:S(2)}, u32[]{:S(2)}) collective-permute-start(f32[256,256]{1,0:T(8,128)S(1)} %get-tuple-element.22.after.ma), channel_id=1, source_target_pairs={{0,4},{4,8},{8,12},{12,0},{1,5},{5,9},{9,13},{13,1},{2,6},{6,10},{... | collective-permute-start | bytes 786440 | tf_op jit(solution)/shard_map/ppermute | solution.py:462
  33.2 0.2 collective-permute-start.9
  33.3 0.2 shard_map.89.pair
  33.6 4.5 %collective-permute-done.8.na = f32[256,256]{1,0:T(8,128)S(1)} collective-permute-done((f32[256,256]{1,0:T(8,128)S(1)}, f32[256,256]{1,0:T(8,128)S(1)}, u32[]{:S(2)}, u32[]{:S(2)}) %collective-permute-start.8) | collective-permute-done | bytes 262176 | tf_op jit(solution)/shard_map/ppermute | solution.py:462
  38.1 0.0 collective-permute-start.10
  38.1 0.0 collective-permute-done.7.pb
  38.1 2.7 %collective-permute-start.11 = (f32[272,256]{1,0:T(8,128)S(1)}, f32[272,256]{1,0:T(8,128)S(1)}, u32[]{:S(2)}, u32[]{:S(2)}) collective-permute-start(f32[272,256]{1,0:T(8,128)S(1)} %collective-permute-done.7.pb), channel_id=1, source_target_pairs={{0,4},{4,8},{8,12},{12,0},{1,5},{5,9},{9,13},{13,1},{2,6},{6,10},{... | collective-permute-start | bytes 835592 | tf_op jit(solution)/shard_map/ppermute | solution.py:462
  40.8 0.1 shard_map.90.after.pair
  40.8 1.9 %collective-permute-done.6.pa = f32[256,256]{1,0:T(8,128)S(1)} collective-permute-done((f32[256,256]{1,0:T(8,128)S(1)}, f32[256,256]{1,0:T(8,128)S(1)}, u32[]{:S(2)}, u32[]{:S(2)}) %collective-permute-start.6) | collective-permute-done | bytes 262176 | tf_op jit(solution)/shard_map/ppermute | solution.py:462
  42.8 1.3 %collective-permute-done.9.nb = f32[272,256]{1,0:T(8,128)S(1)} collective-permute-done((f32[272,256]{1,0:T(8,128)S(1)}, f32[272,256]{1,0:T(8,128)S(1)}, u32[]{:S(2)}, u32[]{:S(2)}) %collective-permute-start.9) | collective-permute-done | bytes 278560 | tf_op jit(solution)/shard_map/ppermute | solution.py:462
  44.0 2.0 %shard_map.91.own = f32[528,256]{1,0:T(8,128)S(1)} custom-call(s32[1]{0:T(128)} %bitcast.here.after, f32[256,256]{1,0:T(8,128)S(1)} %get-tuple-element.22.after.ma, f32[272,256]{1,0:T(8,128)S(1)} %get-tuple-element.23.mb, f32[256,256]{1,0:T(8,128)S(1)} %collective-permute-done.6.pa, f32[272,256]{1,0:T(8,128)S(1)} %collective-permute-done.7.pb, ...), custom_call_target="tpu_custom_call" | custom-call | flops 1409286144 | bytes 524288 | tf_op jit(solution)/shard_map/pallas_call | solution.py:471
  46.1 3.6 %collective-permute-done.10.fa = f32[256,256]{1,0:T(8,128)S(1)} collective-permute-done((f32[256,256]{1,0:T(8,128)S(1)}, f32[256,256]{1,0:T(8,128)S(1)}, u32[]{:S(2)}, u32[]{:S(2)}) %collective-permute-start.10) | collective-permute-done | bytes 262176 | tf_op jit(solution)/shard_map/ppermute | solution.py:462
  49.7 0.0 collective-permute-done.11.fb
  49.7 4.3 %shard_map.92 = (f32[528,256]{1,0:T(8,128)S(1)}, f32[256,256]{1,0:T(8,128)S(1)}, f32[272,256]{1,0:T(8,128)S(1)}) custom-call(s32[1]{0:T(128)} %bitcast.here.after, f32[528,256]{1,0:T(8,128)S(1)} %shard_map.91.own, f32[256,256]{1,0:T(8,128)S(1)} %collective-permute-done.6.pa, f32[272,256]{1,0:T(8,128)S(1)} %collective-permute-done.7.pb, ...), custom_call_target="tpu_custom_call" | custom-call | flops 2818572288 | bytes 524288 | tf_op jit(solution)/shard_map/pallas_call | solution.py:475
  53.9 3.1 %collective-permute-start.12 = (f32[528,256]{1,0:T(8,128)S(1)}, f32[528,256]{1,0:T(8,128)S(1)}, u32[]{:S(2)}, u32[]{:S(2)}) collective-permute-start(f32[528,256]{1,0:T(8,128)S(1)} %get-tuple-element.27.after.mine), channel_id=1, source_target_pairs={{0,16},{16,0},{1,17},{17,1},{2,18},{18,2},{3,19},{19,3},{4,20},{20... | collective-permute-start | bytes 1622024 | tf_op jit(solution)/shard_map/ppermute | solution.py:458
  57.0 2.1 %shard_map.93.after.low = f32[528,256]{1,0:T(8,128)S(1)} custom-call(s32[1]{0:T(128)} %bitcast.here.after, f32[256,256]{1,0:T(8,128)S(1)} %get-tuple-element.28.oa, f32[272,256]{1,0:T(8,128)S(1)} %get-tuple-element.29.ob, f32[256,256]{1,0:T(8,128)S(1)} %collective-permute-done.6.pa, f32[272,256]{1,0:T(8,128)S(1)} %collective-permute-done.7.pb, ...), custom_call_target="tpu_custom_call" | custom-call | flops 1409286144 | bytes 524288 | tf_op jit(solution)/shard_map/pallas_call | solution.py:506
  59.1 0.0 collective-permute-done.12.theirs
  59.1 3.0 %shard_map.94 = (f32[528,256]{1,0:T(8,128)S(1)}, f32[264,256]{1,0:T(8,128)S(1)}) custom-call(s32[1]{0:T(128)} %bitcast.here.after, f32[528,256]{1,0:T(8,128)S(1)} %get-tuple-element.27.after.mine, f32[528,256]{1,0:T(8,128)S(1)} %collective-permute-done.12.theirs, f32[528,256]{1,0:T(8,128)S(1)} %shard_map.93.after.low), custom_call_target="tpu_custom_call" | custom-call | flops 1409286144 | bytes 524288 | tf_op jit(solution)/shard_map/pallas_call | solution.py:507
  62.0 0.3 collective-permute-start.13
  62.4 7.8 %collective-permute-done.13.mine = f32[264,256]{1,0:T(8,128)S(1)} collective-permute-done((f32[264,256]{1,0:T(8,128)S(1)}, f32[264,256]{1,0:T(8,128)S(1)}, u32[]{:S(2)}, u32[]{:S(2)}) %collective-permute-start.13) | collective-permute-done | bytes 270368 | tf_op jit(solution)/shard_map/ppermute | solution.py:458
  70.2 0.9 collective-permute-start.14
  71.0 0.0 copy-start
  71.0 0.0 copy-start.1
  71.0 7.0 %shard_map.95 = (f32[528,256]{1,0:T(8,128)S(1)}, f32[2,528,256]{2,1,0:T(8,128)S(1)}) custom-call(s32[1]{0:T(128)} %bitcast.here.after, f32[528,256]{1,0:T(8,128)S(1)} %collective-permute-done.12.theirs, f32[528,256]{1,0:T(8,128)S(1)} %shard_map.93.after.low, f32[2,528,256]{2,1,0:T(8,128)S(1)} %shard_map.90.after.pair, ...), custom_call_target="tpu_custom_call" | custom-call | flops 4227858432 | bytes 524288 | tf_op jit(solution)/shard_map/pallas_call | solution.py:509
  78.0 0.0 copy-done
  78.0 0.0 copy-done.1
  78.0 0.1 shard_map.96
  78.2 0.0 collective-permute-done.14.other
  78.2 0.1 shard_map.97
  78.2 0.7 collective-permute-start.16
  78.9 1.3 %collective-permute-start.15 = (f32[144,256]{1,0:T(8,128)S(1)}, f32[144,256]{1,0:T(8,128)S(1)}, u32[]{:S(2)}, u32[]{:S(2)}) collective-permute-start(f32[144,256]{1,0:T(8,128)S(1)} %get-tuple-element.36.after), channel_id=1, source_target_pairs={{0,64},{1,65},{2,66},{3,67},{4,68},{5,69},{6,70},{7,71},{8,72},{9,... | collective-permute-start | bytes 442376 | tf_op jit(solution)/shard_map/ppermute | solution.py:513
  80.2 0.1 shard_map.98.pair
  80.3 0.0 collective-permute-done.16.state_b
  80.3 7.4 %collective-permute-done.15.state_a = f32[144,256]{1,0:T(8,128)S(1)} collective-permute-done((f32[144,256]{1,0:T(8,128)S(1)}, f32[144,256]{1,0:T(8,128)S(1)}, u32[]{:S(2)}, u32[]{:S(2)}) %collective-permute-start.15) | collective-permute-done | bytes 147488 | tf_op jit(solution)/shard_map/ppermute | solution.py:513
  87.8 5.7 %shard_map.99 = (f32[2,256]{1,0:T(2,128)}, f32[2,256,256]{2,1,0:T(8,128)}) custom-call(s32[1]{0:T(128)} %bitcast.here.after, f32[144,256]{1,0:T(8,128)S(1)} %collective-permute-done.15.state_a, f32[144,256]{1,0:T(8,128)S(1)} %collective-permute-done.16.state_b, f32[2,16,256]{2,1,0:T(8,128)S(1)} %get-tuple-element.33.mean, ...), custom_call_target="tpu_custom_call" | custom-call | flops 2415919104 | bytes 524288 | tf_op jit(solution)/shard_map/pallas_call | solution.py:516
Async XLA Ops:
  5.6 8.9 %collective-permute-start.1 = (f32[272,256]{1,0:T(8,128)S(1)}, f32[272,256]{1,0:T(8,128)S(1)}, u32[]{:S(2)}, u32[]{:S(2)}) collective-permute-start(f32[272,256]{1,0:T(8,128)S(1)} %get-tuple-element.21.mb), channel_id=1, source_target_pairs={{0,1},{1,2},{2,3},{3,0},{4,5},{5,6},{6,7},{7,4},{8,9},{9,10},{10,1... | collective-permute-start | bytes 835592 | tf_op jit(solution)/shard_map/ppermute | solution.py:462
  6.9 7.6 %collective-permute-start.2 = (f32[256,256]{1,0:T(8,128)S(1)}, f32[256,256]{1,0:T(8,128)S(1)}, u32[]{:S(2)}, u32[]{:S(2)}) collective-permute-start(f32[256,256]{1,0:T(8,128)S(1)} %get-tuple-element.20.ma), channel_id=1, source_target_pairs={{0,3},{1,0},{2,1},{3,2},{4,7},{5,4},{6,5},{7,6},{8,11},{9,8},{10,9... | collective-permute-start | bytes 786440 | tf_op jit(solution)/shard_map/ppermute | solution.py:462
  8.4 11.7 %collective-permute-start.3 = (f32[272,256]{1,0:T(8,128)S(1)}, f32[272,256]{1,0:T(8,128)S(1)}, u32[]{:S(2)}, u32[]{:S(2)}) collective-permute-start(f32[272,256]{1,0:T(8,128)S(1)} %get-tuple-element.21.mb), channel_id=1, source_target_pairs={{0,3},{1,0},{2,1},{3,2},{4,7},{5,4},{6,5},{7,6},{8,11},{9,8},{10,9... | collective-permute-start | bytes 835592 | tf_op jit(solution)/shard_map/ppermute | solution.py:462
  9.8 10.3 %collective-permute-start = (f32[256,256]{1,0:T(8,128)S(1)}, f32[256,256]{1,0:T(8,128)S(1)}, u32[]{:S(2)}, u32[]{:S(2)}) collective-permute-start(f32[256,256]{1,0:T(8,128)S(1)} %get-tuple-element.20.ma), channel_id=1, source_target_pairs={{0,1},{1,2},{2,3},{3,0},{4,5},{5,6},{6,7},{7,4},{8,9},{9,10},{10,1... | collective-permute-start | bytes 786440 | tf_op jit(solution)/shard_map/ppermute | solution.py:462
  14.5 11.6 %collective-permute-start.5 = (f32[272,256]{1,0:T(8,128)S(1)}, f32[272,256]{1,0:T(8,128)S(1)}, u32[]{:S(2)}, u32[]{:S(2)}) collective-permute-start(f32[272,256]{1,0:T(8,128)S(1)} %collective-permute-done.1.pb.tb), channel_id=1, source_target_pairs={{0,1},{1,2},{2,3},{3,0},{4,5},{5,6},{6,7},{7,4},{8,9},{9,10},{10,1... | collective-permute-start | bytes 835592 | tf_op jit(solution)/shard_map/ppermute | solution.py:462
  14.5 10.9 %collective-permute-start.4 = (f32[256,256]{1,0:T(8,128)S(1)}, f32[256,256]{1,0:T(8,128)S(1)}, u32[]{:S(2)}, u32[]{:S(2)}) collective-permute-start(f32[256,256]{1,0:T(8,128)S(1)} %collective-permute-done.2.na), channel_id=1, source_target_pairs={{0,3},{1,0},{2,1},{3,2},{4,7},{5,4},{6,5},{7,6},{8,11},{9,8},{10,9... | collective-permute-start | bytes 786440 | tf_op jit(solution)/shard_map/ppermute | solution.py:462
  30.3 7.8 %collective-permute-start.7 = (f32[272,256]{1,0:T(8,128)S(1)}, f32[272,256]{1,0:T(8,128)S(1)}, u32[]{:S(2)}, u32[]{:S(2)}) collective-permute-start(f32[272,256]{1,0:T(8,128)S(1)} %get-tuple-element.23.mb), channel_id=1, source_target_pairs={{0,4},{4,8},{8,12},{12,0},{1,5},{5,9},{9,13},{13,1},{2,6},{6,10},{... | collective-permute-start | bytes 835592 | tf_op jit(solution)/shard_map/ppermute | solution.py:462
  30.4 7.7 %collective-permute-start.8 = (f32[256,256]{1,0:T(8,128)S(1)}, f32[256,256]{1,0:T(8,128)S(1)}, u32[]{:S(2)}, u32[]{:S(2)}) collective-permute-start(f32[256,256]{1,0:T(8,128)S(1)} %get-tuple-element.22.after.ma), channel_id=1, source_target_pairs={{0,12},{4,0},{8,4},{12,8},{1,13},{5,1},{9,5},{13,9},{2,14},{6,2},{... | collective-permute-start | bytes 786440 | tf_op jit(solution)/shard_map/ppermute | solution.py:462
  31.9 10.9 %collective-permute-start.6 = (f32[256,256]{1,0:T(8,128)S(1)}, f32[256,256]{1,0:T(8,128)S(1)}, u32[]{:S(2)}, u32[]{:S(2)}) collective-permute-start(f32[256,256]{1,0:T(8,128)S(1)} %get-tuple-element.22.after.ma), channel_id=1, source_target_pairs={{0,4},{4,8},{8,12},{12,0},{1,5},{5,9},{9,13},{13,1},{2,6},{6,10},{... | collective-permute-start | bytes 786440 | tf_op jit(solution)/shard_map/ppermute | solution.py:462
  33.2 10.9 %collective-permute-start.9 = (f32[272,256]{1,0:T(8,128)S(1)}, f32[272,256]{1,0:T(8,128)S(1)}, u32[]{:S(2)}, u32[]{:S(2)}) collective-permute-start(f32[272,256]{1,0:T(8,128)S(1)} %get-tuple-element.23.mb), channel_id=1, source_target_pairs={{0,12},{4,0},{8,4},{12,8},{1,13},{5,1},{9,5},{13,9},{2,14},{6,2},{... | collective-permute-start | bytes 835592 | tf_op jit(solution)/shard_map/ppermute | solution.py:462
  38.1 11.6 %collective-permute-start.10 = (f32[256,256]{1,0:T(8,128)S(1)}, f32[256,256]{1,0:T(8,128)S(1)}, u32[]{:S(2)}, u32[]{:S(2)}) collective-permute-start(f32[256,256]{1,0:T(8,128)S(1)} %collective-permute-done.8.na), channel_id=1, source_target_pairs={{0,12},{4,0},{8,4},{12,8},{1,13},{5,1},{9,5},{13,9},{2,14},{6,2},{... | collective-permute-start | bytes 786440 | tf_op jit(solution)/shard_map/ppermute | solution.py:462
  38.1 11.6 %collective-permute-start.11 = (f32[272,256]{1,0:T(8,128)S(1)}, f32[272,256]{1,0:T(8,128)S(1)}, u32[]{:S(2)}, u32[]{:S(2)}) collective-permute-start(f32[272,256]{1,0:T(8,128)S(1)} %collective-permute-done.7.pb), channel_id=1, source_target_pairs={{0,4},{4,8},{8,12},{12,0},{1,5},{5,9},{9,13},{13,1},{2,6},{6,10},{... | collective-permute-start | bytes 835592 | tf_op jit(solution)/shard_map/ppermute | solution.py:462
  53.9 5.1 %collective-permute-start.12 = (f32[528,256]{1,0:T(8,128)S(1)}, f32[528,256]{1,0:T(8,128)S(1)}, u32[]{:S(2)}, u32[]{:S(2)}) collective-permute-start(f32[528,256]{1,0:T(8,128)S(1)} %get-tuple-element.27.after.mine), channel_id=1, source_target_pairs={{0,16},{16,0},{1,17},{17,1},{2,18},{18,2},{3,19},{19,3},{4,20},{20... | collective-permute-start | bytes 1622024 | tf_op jit(solution)/shard_map/ppermute | solution.py:458
  62.0 8.1 %collective-permute-start.13 = (f32[264,256]{1,0:T(8,128)S(1)}, f32[264,256]{1,0:T(8,128)S(1)}, u32[]{:S(2)}, u32[]{:S(2)}) collective-permute-start(f32[264,256]{1,0:T(8,128)S(1)} %get-tuple-element.30), channel_id=1, source_target_pairs={{0,32},{32,0},{64,96},{96,64},{1,33},{33,1},{65,97},{97,65},{2,34}... | collective-permute-start | bytes 811016 | tf_op jit(solution)/shard_map/ppermute | solution.py:458
  70.2 8.0 %collective-permute-start.14 = (f32[264,256]{1,0:T(8,128)S(1)}, f32[264,256]{1,0:T(8,128)S(1)}, u32[]{:S(2)}, u32[]{:S(2)}) collective-permute-start(f32[264,256]{1,0:T(8,128)S(1)} %collective-permute-done.13.mine), channel_id=1, source_target_pairs={{0,16},{16,0},{1,17},{17,1},{2,18},{18,2},{3,19},{19,3},{4,20},{20... | collective-permute-start | bytes 811016 | tf_op jit(solution)/shard_map/ppermute | solution.py:458
  71.0 7.0 %copy-start = (f32[256,256]{1,0:T(8,128)S(1)}, f32[256,256]{1,0:T(8,128)}, u32[]{:S(2)}) copy-start(f32[256,256]{1,0:T(8,128)} %cov.1) | copy-start | bytes 786436
  71.0 7.0 %copy-start.1 = (f32[256]{0:T(256)S(1)}, f32[256]{0:T(256)}, u32[]{:S(2)}) copy-start(f32[256]{0:T(256)} %param.12) | copy-start | bytes 3076
  78.2 2.1 %collective-permute-start.16 = (f32[144,256]{1,0:T(8,128)S(1)}, f32[144,256]{1,0:T(8,128)S(1)}, u32[]{:S(2)}, u32[]{:S(2)}) collective-permute-start(f32[144,256]{1,0:T(8,128)S(1)} %get-tuple-element.36.after), channel_id=1, source_target_pairs={{0,96},{1,97},{2,98},{3,99},{4,100},{5,101},{6,102},{7,103},{8,104... | collective-permute-start | bytes 442376 | tf_op jit(solution)/shard_map/ppermute | solution.py:514
  78.9 8.8 %collective-permute-start.15 = (f32[144,256]{1,0:T(8,128)S(1)}, f32[144,256]{1,0:T(8,128)S(1)}, u32[]{:S(2)}, u32[]{:S(2)}) collective-permute-start(f32[144,256]{1,0:T(8,128)S(1)} %get-tuple-element.36.after), channel_id=1, source_target_pairs={{0,64},{1,65},{2,66},{3,67},{4,68},{5,69},{6,70},{7,71},{8,72},{9,... | collective-permute-start | bytes 442376 | tf_op jit(solution)/shard_map/ppermute | solution.py:513

commit v4 on v3

--- a/solution.py
+++ b/solution.py
@@ -140,12 +140,13 @@
         row_r = vecs_a + up[N + 1 : N + 2]
         row_s = vecs_b[1:2] - seen[N : N + 1]
         third2 = split(dot3(rows(move_a2, spr_a2, split(row_r)), split(settle)))
-        fourth = dot3(third2, split(move_b))
+        move_b2 = split(move_b)
+        fourth = dot3(third2, move_b2)
         back2 = (third2[0][0:N], third2[1][0:N])
         fifth = dot3(
             rows(split(seen[0:N]), split(jnp.broadcast_to(row_s, (V, N)))), back2, ((1,), (1,))
         )
-        spread = dot3(split(move_b.T), split(fourth[N : 2 * N])) + spr_b
+        spread = dot3(move_b2, split(fourth[N : 2 * N]), ((0,), (0,))) + spr_b
         out.append(
             (
                 fourth[0:N],
@@ -166,8 +167,9 @@
     for (move_b, spr_b, _, vecs_b), up, settle in zip(seconds, ups, settled):
         row_r = mean + up[N + 1 : N + 2]
         third = dot3(rows(cov2, split(row_r)), split(settle))
-        fourth = dot3(split(third), split(move_b))
-        spread = dot3(split(move_b.T), split(fourth[0:N])) + spr_b
+        move_b2 = split(move_b)
+        fourth = dot3(split(third), move_b2)
+        spread = dot3(move_b2, split(fourth[0:N]), ((0,), (0,))) + spr_b
         out.append((fourth[N:] + vecs_b[0:1], spread))
     return out
 

time: 93.7 us -> 93.6 us (level)
  no operation moved by 1% of the time
where the time goes in v4:
time: 93.6 us; the launch traced here: 93.5 us
  waiting for transfers between devices  37.9 us (40%)
  Pallas kernels  35.8 us (38%)
  starting transfers between devices  19 us (20%)
    ppermute x12, waiting for transfers between devices, turn(): return lax.ppermute(part, axis, [(k, (k + step) % 4) for k in range(4)])  22.7 us
    ppermute x12, starting transfers between devices, turn(): return lax.ppermute(part, axis, [(k, (k + step) % 4) for k in range(4)])  12.7 us
    pallas_call x2, Pallas kernels, ring(): *whole, other_a, other_b = run(here, own, *near, far_a, far_b)  8.49 us
    ppermute x3, waiting for transfers between devices, swap(): return lax.ppermute(part, axis, [(k, k ^ step) for k in range(size)])  7.77 us
    ppermute x1, waiting for transfers between devices, on_device(): state_a = lax.ppermute(packed, 'x', [(0, 2)])  7.43 us
    pallas_call x1, Pallas kernels, on_device(): low, pair = cored(here, c1, low, pair, whole)  6.98 us
    pallas_call x1, Pallas kernels, on_device(): return final(here, state_a, state_b, means, covs, pair)  5.74 us
    pallas_call x1, Pallas kernels, on_device(): build(*(pltpu.with_memory_space_constraint(a, pltpu.HBM) for a in arrays))  4.91 us
  transfers between devices with their start and end apart: 17, of which 10 were waited for; matrix products, arithmetic and copies ran while one was open for 0% of the time, Pallas kernels for 15%

profile of v4, /device:TPU:101, one launch (start us, length us, event | category | flops | bytes accessed | tf_op | source)
XLA Modules:
  0.0 93.5 jit_solution(5082194448465335316)
XLA Ops:
  0.6 4.9 %shard_map.86 = (f32[256,256]{1,0:T(8,128)S(1)}, f32[272,256]{1,0:T(8,128)S(1)}, f32[2,528,256]{2,1,0:T(8,128)S(1)}) custom-call(f32[2,256,256]{2,1,0:T(8,128)} %trans_in.1, f32[2,64,256]{2,1,0:T(8,128)} %obs_in.1, f32[2,64]{1,0:T(2,128)} %noise_in.1, f32[2,64]{1,0:T(2,128)} %meas_in.1, f32[256,256]{1,0:T(8,128)} %state_in.1), custom_call_target="tpu_custom_call" | custom-call | flops 3019898880 | bytes 524288 | tf_op jit(solution)/shard_map/pallas_call | solution.py:502
  5.6 1.4 %collective-permute-start.1 = (f32[272,256]{1,0:T(8,128)S(1)}, f32[272,256]{1,0:T(8,128)S(1)}, u32[]{:S(2)}, u32[]{:S(2)}) collective-permute-start(f32[272,256]{1,0:T(8,128)S(1)} %get-tuple-element.21.mb), channel_id=1, source_target_pairs={{0,1},{1,2},{2,3},{3,0},{4,5},{5,6},{6,7},{7,4},{8,9},{9,10},{10,1... | collective-permute-start | bytes 835592 | tf_op jit(solution)/shard_map/ppermute | solution.py:464
  6.9 1.5 %collective-permute-start.2 = (f32[256,256]{1,0:T(8,128)S(1)}, f32[256,256]{1,0:T(8,128)S(1)}, u32[]{:S(2)}, u32[]{:S(2)}) collective-permute-start(f32[256,256]{1,0:T(8,128)S(1)} %get-tuple-element.20.ma), channel_id=1, source_target_pairs={{0,3},{1,0},{2,1},{3,2},{4,7},{5,4},{6,5},{7,6},{8,11},{9,8},{10,9... | collective-permute-start | bytes 786440 | tf_op jit(solution)/shard_map/ppermute | solution.py:464
  8.4 1.4 %collective-permute-start.3 = (f32[272,256]{1,0:T(8,128)S(1)}, f32[272,256]{1,0:T(8,128)S(1)}, u32[]{:S(2)}, u32[]{:S(2)}) collective-permute-start(f32[272,256]{1,0:T(8,128)S(1)} %get-tuple-element.21.mb), channel_id=1, source_target_pairs={{0,3},{1,0},{2,1},{3,2},{4,7},{5,4},{6,5},{7,6},{8,11},{9,8},{10,9... | collective-permute-start | bytes 835592 | tf_op jit(solution)/shard_map/ppermute | solution.py:464
  9.8 0.1 collective-permute-start
  9.9 4.6 %collective-permute-done.1.pb.tb = f32[272,256]{1,0:T(8,128)S(1)} collective-permute-done((f32[272,256]{1,0:T(8,128)S(1)}, f32[272,256]{1,0:T(8,128)S(1)}, u32[]{:S(2)}, u32[]{:S(2)}) %collective-permute-start.1) | collective-permute-done | bytes 278560 | tf_op jit(solution)/shard_map/ppermute | solution.py:464
  14.5 0.0 collective-permute-start.5
  14.5 0.0 collective-permute-done.2.na
  14.5 2.7 %collective-permute-start.4 = (f32[256,256]{1,0:T(8,128)S(1)}, f32[256,256]{1,0:T(8,128)S(1)}, u32[]{:S(2)}, u32[]{:S(2)}) collective-permute-start(f32[256,256]{1,0:T(8,128)S(1)} %collective-permute-done.2.na), channel_id=1, source_target_pairs={{0,3},{1,0},{2,1},{3,2},{4,7},{5,4},{6,5},{7,6},{8,11},{9,8},{10,9... | collective-permute-start | bytes 786440 | tf_op jit(solution)/shard_map/ppermute | solution.py:464
  17.2 2.9 %collective-permute-done.pa.ta = f32[256,256]{1,0:T(8,128)S(1)} collective-permute-done((f32[256,256]{1,0:T(8,128)S(1)}, f32[256,256]{1,0:T(8,128)S(1)}, u32[]{:S(2)}, u32[]{:S(2)}) %collective-permute-start) | collective-permute-done | bytes 262176 | tf_op jit(solution)/shard_map/ppermute | solution.py:464
  20.1 0.0 collective-permute-done.3.nb
  20.1 2.1 %shard_map.87.own = f32[528,256]{1,0:T(8,128)S(1)} custom-call(s32[1]{0:T(128)} %bitcast.here.after, f32[256,256]{1,0:T(8,128)S(1)} %get-tuple-element.20.ma, f32[272,256]{1,0:T(8,128)S(1)} %get-tuple-element.21.mb, f32[256,256]{1,0:T(8,128)S(1)} %collective-permute-done.pa.ta, f32[272,256]{1,0:T(8,128)S(1)} %collective-permute-done.1.pb.tb, ...), custom_call_target="tpu_custom_call" | custom-call | flops 1409286144 | bytes 524288 | tf_op jit(solution)/shard_map/pallas_call | solution.py:473
  22.2 3.2 %collective-permute-done.4.fa = f32[256,256]{1,0:T(8,128)S(1)} collective-permute-done((f32[256,256]{1,0:T(8,128)S(1)}, f32[256,256]{1,0:T(8,128)S(1)}, u32[]{:S(2)}, u32[]{:S(2)}) %collective-permute-start.4) | collective-permute-done | bytes 262176 | tf_op jit(solution)/shard_map/ppermute | solution.py:464
  25.4 0.7 collective-permute-done.5.fb
  26.1 4.2 %shard_map.88 = (f32[256,256]{1,0:T(8,128)S(1)}, f32[272,256]{1,0:T(8,128)S(1)}, f32[256,256]{1,0:T(8,128)S(1)}, f32[272,256]{1,0:T(8,128)S(1)}) custom-call(s32[1]{0:T(128)} %bitcast.here.after, f32[528,256]{1,0:T(8,128)S(1)} %shard_map.87.own, f32[256,256]{1,0:T(8,128)S(1)} %collective-permute-done.pa.ta, f32[272,256]{1,0:T(8,128)S(1)} %collective-permute-done.1.pb.tb, ...), custom_call_target="tpu_custom_call" | custom-call | flops 2818572288 | bytes 524288 | tf_op jit(solution)/shard_map/pallas_call | solution.py:477
  30.3 0.1 collective-permute-start.7
  30.4 1.5 %collective-permute-start.8 = (f32[256,256]{1,0:T(8,128)S(1)}, f32[256,256]{1,0:T(8,128)S(1)}, u32[]{:S(2)}, u32[]{:S(2)}) collective-permute-start(f32[256,256]{1,0:T(8,128)S(1)} %get-tuple-element.22.after.ma), channel_id=1, source_target_pairs={{0,12},{4,0},{8,4},{12,8},{1,13},{5,1},{9,5},{13,9},{2,14},{6,2},{... | collective-permute-start | bytes 786440 | tf_op jit(solution)/shard_map/ppermute | solution.py:464
  31.9 1.3 %collective-permute-start.6 = (f32[256,256]{1,0:T(8,128)S(1)}, f32[256,256]{1,0:T(8,128)S(1)}, u32[]{:S(2)}, u32[]{:S(2)}) collective-permute-start(f32[256,256]{1,0:T(8,128)S(1)} %get-tuple-element.22.after.ma), channel_id=1, source_target_pairs={{0,4},{4,8},{8,12},{12,0},{1,5},{5,9},{9,13},{13,1},{2,6},{6,10},{... | collective-permute-start | bytes 786440 | tf_op jit(solution)/shard_map/ppermute | solution.py:464
  33.2 0.2 collective-permute-start.9
  33.3 0.2 shard_map.89.pair
  33.6 4.5 %collective-permute-done.8.na = f32[256,256]{1,0:T(8,128)S(1)} collective-permute-done((f32[256,256]{1,0:T(8,128)S(1)}, f32[256,256]{1,0:T(8,128)S(1)}, u32[]{:S(2)}, u32[]{:S(2)}) %collective-permute-start.8) | collective-permute-done | bytes 262176 | tf_op jit(solution)/shard_map/ppermute | solution.py:464
  38.1 0.0 collective-permute-start.10
  38.1 0.0 collective-permute-done.7.pb
  38.1 2.7 %collective-permute-start.11 = (f32[272,256]{1,0:T(8,128)S(1)}, f32[272,256]{1,0:T(8,128)S(1)}, u32[]{:S(2)}, u32[]{:S(2)}) collective-permute-start(f32[272,256]{1,0:T(8,128)S(1)} %collective-permute-done.7.pb), channel_id=1, source_target_pairs={{0,4},{4,8},{8,12},{12,0},{1,5},{5,9},{9,13},{13,1},{2,6},{6,10},{... | collective-permute-start | bytes 835592 | tf_op jit(solution)/shard_map/ppermute | solution.py:464
  40.8 0.1 shard_map.90.after.pair
  40.8 1.9 %collective-permute-done.6.pa = f32[256,256]{1,0:T(8,128)S(1)} collective-permute-done((f32[256,256]{1,0:T(8,128)S(1)}, f32[256,256]{1,0:T(8,128)S(1)}, u32[]{:S(2)}, u32[]{:S(2)}) %collective-permute-start.6) | collective-permute-done | bytes 262176 | tf_op jit(solution)/shard_map/ppermute | solution.py:464
  42.8 1.3 %collective-permute-done.9.nb = f32[272,256]{1,0:T(8,128)S(1)} collective-permute-done((f32[272,256]{1,0:T(8,128)S(1)}, f32[272,256]{1,0:T(8,128)S(1)}, u32[]{:S(2)}, u32[]{:S(2)}) %collective-permute-start.9) | collective-permute-done | bytes 278560 | tf_op jit(solution)/shard_map/ppermute | solution.py:464
  44.0 2.0 %shard_map.91.own = f32[528,256]{1,0:T(8,128)S(1)} custom-call(s32[1]{0:T(128)} %bitcast.here.after, f32[256,256]{1,0:T(8,128)S(1)} %get-tuple-element.22.after.ma, f32[272,256]{1,0:T(8,128)S(1)} %get-tuple-element.23.mb, f32[256,256]{1,0:T(8,128)S(1)} %collective-permute-done.6.pa, f32[272,256]{1,0:T(8,128)S(1)} %collective-permute-done.7.pb, ...), custom_call_target="tpu_custom_call" | custom-call | flops 1409286144 | bytes 524288 | tf_op jit(solution)/shard_map/pallas_call | solution.py:473
  46.1 3.6 %collective-permute-done.10.fa = f32[256,256]{1,0:T(8,128)S(1)} collective-permute-done((f32[256,256]{1,0:T(8,128)S(1)}, f32[256,256]{1,0:T(8,128)S(1)}, u32[]{:S(2)}, u32[]{:S(2)}) %collective-permute-start.10) | collective-permute-done | bytes 262176 | tf_op jit(solution)/shard_map/ppermute | solution.py:464
  49.7 0.0 collective-permute-done.11.fb
  49.7 4.3 %shard_map.92 = (f32[528,256]{1,0:T(8,128)S(1)}, f32[256,256]{1,0:T(8,128)S(1)}, f32[272,256]{1,0:T(8,128)S(1)}) custom-call(s32[1]{0:T(128)} %bitcast.here.after, f32[528,256]{1,0:T(8,128)S(1)} %shard_map.91.own, f32[256,256]{1,0:T(8,128)S(1)} %collective-permute-done.6.pa, f32[272,256]{1,0:T(8,128)S(1)} %collective-permute-done.7.pb, ...), custom_call_target="tpu_custom_call" | custom-call | flops 2818572288 | bytes 524288 | tf_op jit(solution)/shard_map/pallas_call | solution.py:477
  53.9 3.1 %collective-permute-start.12 = (f32[528,256]{1,0:T(8,128)S(1)}, f32[528,256]{1,0:T(8,128)S(1)}, u32[]{:S(2)}, u32[]{:S(2)}) collective-permute-start(f32[528,256]{1,0:T(8,128)S(1)} %get-tuple-element.27.after.mine), channel_id=1, source_target_pairs={{0,16},{16,0},{1,17},{17,1},{2,18},{18,2},{3,19},{19,3},{4,20},{20... | collective-permute-start | bytes 1622024 | tf_op jit(solution)/shard_map/ppermute | solution.py:460
  57.0 2.0 %shard_map.93.after.low = f32[528,256]{1,0:T(8,128)S(1)} custom-call(s32[1]{0:T(128)} %bitcast.here.after, f32[256,256]{1,0:T(8,128)S(1)} %get-tuple-element.28.oa, f32[272,256]{1,0:T(8,128)S(1)} %get-tuple-element.29.ob, f32[256,256]{1,0:T(8,128)S(1)} %collective-permute-done.6.pa, f32[272,256]{1,0:T(8,128)S(1)} %collective-permute-done.7.pb, ...), custom_call_target="tpu_custom_call" | custom-call | flops 1409286144 | bytes 524288 | tf_op jit(solution)/shard_map/pallas_call | solution.py:508
  59.1 0.0 collective-permute-done.12.theirs
  59.1 2.9 %shard_map.94 = (f32[528,256]{1,0:T(8,128)S(1)}, f32[264,256]{1,0:T(8,128)S(1)}) custom-call(s32[1]{0:T(128)} %bitcast.here.after, f32[528,256]{1,0:T(8,128)S(1)} %get-tuple-element.27.after.mine, f32[528,256]{1,0:T(8,128)S(1)} %collective-permute-done.12.theirs, f32[528,256]{1,0:T(8,128)S(1)} %shard_map.93.after.low), custom_call_target="tpu_custom_call" | custom-call | flops 1409286144 | bytes 524288 | tf_op jit(solution)/shard_map/pallas_call | solution.py:509
  62.0 0.3 collective-permute-start.13
  62.4 7.8 %collective-permute-done.13.mine = f32[264,256]{1,0:T(8,128)S(1)} collective-permute-done((f32[264,256]{1,0:T(8,128)S(1)}, f32[264,256]{1,0:T(8,128)S(1)}, u32[]{:S(2)}, u32[]{:S(2)}) %collective-permute-start.13) | collective-permute-done | bytes 270368 | tf_op jit(solution)/shard_map/ppermute | solution.py:460
  70.1 0.9 collective-permute-start.14
  71.0 0.0 copy-start
  71.0 0.0 copy-start.1
  71.0 7.0 %shard_map.95 = (f32[528,256]{1,0:T(8,128)S(1)}, f32[2,528,256]{2,1,0:T(8,128)S(1)}) custom-call(s32[1]{0:T(128)} %bitcast.here.after, f32[528,256]{1,0:T(8,128)S(1)} %collective-permute-done.12.theirs, f32[528,256]{1,0:T(8,128)S(1)} %shard_map.93.after.low, f32[2,528,256]{2,1,0:T(8,128)S(1)} %shard_map.90.after.pair, ...), custom_call_target="tpu_custom_call" | custom-call | flops 4227858432 | bytes 524288 | tf_op jit(solution)/shard_map/pallas_call | solution.py:511
  78.0 0.0 copy-done
  78.0 0.0 copy-done.1
  78.0 0.1 shard_map.96
  78.1 0.0 collective-permute-done.14.other
  78.2 0.1 shard_map.97
  78.2 0.7 collective-permute-start.16
  78.9 1.3 %collective-permute-start.15 = (f32[144,256]{1,0:T(8,128)S(1)}, f32[144,256]{1,0:T(8,128)S(1)}, u32[]{:S(2)}, u32[]{:S(2)}) collective-permute-start(f32[144,256]{1,0:T(8,128)S(1)} %get-tuple-element.36.after), channel_id=1, source_target_pairs={{0,64},{1,65},{2,66},{3,67},{4,68},{5,69},{6,70},{7,71},{8,72},{9,... | collective-permute-start | bytes 442376 | tf_op jit(solution)/shard_map/ppermute | solution.py:515
  80.2 0.1 shard_map.98.pair
  80.3 0.0 collective-permute-done.16.state_b
  80.3 7.4 %collective-permute-done.15.state_a = f32[144,256]{1,0:T(8,128)S(1)} collective-permute-done((f32[144,256]{1,0:T(8,128)S(1)}, f32[144,256]{1,0:T(8,128)S(1)}, u32[]{:S(2)}, u32[]{:S(2)}) %collective-permute-start.15) | collective-permute-done | bytes 147488 | tf_op jit(solution)/shard_map/ppermute | solution.py:515
  87.7 5.7 %shard_map.99 = (f32[2,256]{1,0:T(2,128)}, f32[2,256,256]{2,1,0:T(8,128)}) custom-call(s32[1]{0:T(128)} %bitcast.here.after, f32[144,256]{1,0:T(8,128)S(1)} %collective-permute-done.15.state_a, f32[144,256]{1,0:T(8,128)S(1)} %collective-permute-done.16.state_b, f32[2,16,256]{2,1,0:T(8,128)S(1)} %get-tuple-element.33.mean, ...), custom_call_target="tpu_custom_call" | custom-call | flops 2415919104 | bytes 524288 | tf_op jit(solution)/shard_map/pallas_call | solution.py:518
Async XLA Ops:
  5.6 8.9 %collective-permute-start.1 = (f32[272,256]{1,0:T(8,128)S(1)}, f32[272,256]{1,0:T(8,128)S(1)}, u32[]{:S(2)}, u32[]{:S(2)}) collective-permute-start(f32[272,256]{1,0:T(8,128)S(1)} %get-tuple-element.21.mb), channel_id=1, source_target_pairs={{0,1},{1,2},{2,3},{3,0},{4,5},{5,6},{6,7},{7,4},{8,9},{9,10},{10,1... | collective-permute-start | bytes 835592 | tf_op jit(solution)/shard_map/ppermute | solution.py:464
  6.9 7.6 %collective-permute-start.2 = (f32[256,256]{1,0:T(8,128)S(1)}, f32[256,256]{1,0:T(8,128)S(1)}, u32[]{:S(2)}, u32[]{:S(2)}) collective-permute-start(f32[256,256]{1,0:T(8,128)S(1)} %get-tuple-element.20.ma), channel_id=1, source_target_pairs={{0,3},{1,0},{2,1},{3,2},{4,7},{5,4},{6,5},{7,6},{8,11},{9,8},{10,9... | collective-permute-start | bytes 786440 | tf_op jit(solution)/shard_map/ppermute | solution.py:464
  8.4 11.7 %collective-permute-start.3 = (f32[272,256]{1,0:T(8,128)S(1)}, f32[272,256]{1,0:T(8,128)S(1)}, u32[]{:S(2)}, u32[]{:S(2)}) collective-permute-start(f32[272,256]{1,0:T(8,128)S(1)} %get-tuple-element.21.mb), channel_id=1, source_target_pairs={{0,3},{1,0},{2,1},{3,2},{4,7},{5,4},{6,5},{7,6},{8,11},{9,8},{10,9... | collective-permute-start | bytes 835592 | tf_op jit(solution)/shard_map/ppermute | solution.py:464
  9.8 10.3 %collective-permute-start = (f32[256,256]{1,0:T(8,128)S(1)}, f32[256,256]{1,0:T(8,128)S(1)}, u32[]{:S(2)}, u32[]{:S(2)}) collective-permute-start(f32[256,256]{1,0:T(8,128)S(1)} %get-tuple-element.20.ma), channel_id=1, source_target_pairs={{0,1},{1,2},{2,3},{3,0},{4,5},{5,6},{6,7},{7,4},{8,9},{9,10},{10,1... | collective-permute-start | bytes 786440 | tf_op jit(solution)/shard_map/ppermute | solution.py:464
  14.5 11.6 %collective-permute-start.5 = (f32[272,256]{1,0:T(8,128)S(1)}, f32[272,256]{1,0:T(8,128)S(1)}, u32[]{:S(2)}, u32[]{:S(2)}) collective-permute-start(f32[272,256]{1,0:T(8,128)S(1)} %collective-permute-done.1.pb.tb), channel_id=1, source_target_pairs={{0,1},{1,2},{2,3},{3,0},{4,5},{5,6},{6,7},{7,4},{8,9},{9,10},{10,1... | collective-permute-start | bytes 835592 | tf_op jit(solution)/shard_map/ppermute | solution.py:464
  14.5 10.9 %collective-permute-start.4 = (f32[256,256]{1,0:T(8,128)S(1)}, f32[256,256]{1,0:T(8,128)S(1)}, u32[]{:S(2)}, u32[]{:S(2)}) collective-permute-start(f32[256,256]{1,0:T(8,128)S(1)} %collective-permute-done.2.na), channel_id=1, source_target_pairs={{0,3},{1,0},{2,1},{3,2},{4,7},{5,4},{6,5},{7,6},{8,11},{9,8},{10,9... | collective-permute-start | bytes 786440 | tf_op jit(solution)/shard_map/ppermute | solution.py:464
  30.3 7.8 %collective-permute-start.7 = (f32[272,256]{1,0:T(8,128)S(1)}, f32[272,256]{1,0:T(8,128)S(1)}, u32[]{:S(2)}, u32[]{:S(2)}) collective-permute-start(f32[272,256]{1,0:T(8,128)S(1)} %get-tuple-element.23.mb), channel_id=1, source_target_pairs={{0,4},{4,8},{8,12},{12,0},{1,5},{5,9},{9,13},{13,1},{2,6},{6,10},{... | collective-permute-start | bytes 835592 | tf_op jit(solution)/shard_map/ppermute | solution.py:464
  30.4 7.7 %collective-permute-start.8 = (f32[256,256]{1,0:T(8,128)S(1)}, f32[256,256]{1,0:T(8,128)S(1)}, u32[]{:S(2)}, u32[]{:S(2)}) collective-permute-start(f32[256,256]{1,0:T(8,128)S(1)} %get-tuple-element.22.after.ma), channel_id=1, source_target_pairs={{0,12},{4,0},{8,4},{12,8},{1,13},{5,1},{9,5},{13,9},{2,14},{6,2},{... | collective-permute-start | bytes 786440 | tf_op jit(solution)/shard_map/ppermute | solution.py:464
  31.9 10.9 %collective-permute-start.6 = (f32[256,256]{1,0:T(8,128)S(1)}, f32[256,256]{1,0:T(8,128)S(1)}, u32[]{:S(2)}, u32[]{:S(2)}) collective-permute-start(f32[256,256]{1,0:T(8,128)S(1)} %get-tuple-element.22.after.ma), channel_id=1, source_target_pairs={{0,4},{4,8},{8,12},{12,0},{1,5},{5,9},{9,13},{13,1},{2,6},{6,10},{... | collective-permute-start | bytes 786440 | tf_op jit(solution)/shard_map/ppermute | solution.py:464
  33.2 10.9 %collective-permute-start.9 = (f32[272,256]{1,0:T(8,128)S(1)}, f32[272,256]{1,0:T(8,128)S(1)}, u32[]{:S(2)}, u32[]{:S(2)}) collective-permute-start(f32[272,256]{1,0:T(8,128)S(1)} %get-tuple-element.23.mb), channel_id=1, source_target_pairs={{0,12},{4,0},{8,4},{12,8},{1,13},{5,1},{9,5},{13,9},{2,14},{6,2},{... | collective-permute-start | bytes 835592 | tf_op jit(solution)/shard_map/ppermute | solution.py:464
  38.1 11.6 %collective-permute-start.10 = (f32[256,256]{1,0:T(8,128)S(1)}, f32[256,256]{1,0:T(8,128)S(1)}, u32[]{:S(2)}, u32[]{:S(2)}) collective-permute-start(f32[256,256]{1,0:T(8,128)S(1)} %collective-permute-done.8.na), channel_id=1, source_target_pairs={{0,12},{4,0},{8,4},{12,8},{1,13},{5,1},{9,5},{13,9},{2,14},{6,2},{... | collective-permute-start | bytes 786440 | tf_op jit(solution)/shard_map/ppermute | solution.py:464
  38.1 11.6 %collective-permute-start.11 = (f32[272,256]{1,0:T(8,128)S(1)}, f32[272,256]{1,0:T(8,128)S(1)}, u32[]{:S(2)}, u32[]{:S(2)}) collective-permute-start(f32[272,256]{1,0:T(8,128)S(1)} %collective-permute-done.7.pb), channel_id=1, source_target_pairs={{0,4},{4,8},{8,12},{12,0},{1,5},{5,9},{9,13},{13,1},{2,6},{6,10},{... | collective-permute-start | bytes 835592 | tf_op jit(solution)/shard_map/ppermute | solution.py:464
  53.9 5.1 %collective-permute-start.12 = (f32[528,256]{1,0:T(8,128)S(1)}, f32[528,256]{1,0:T(8,128)S(1)}, u32[]{:S(2)}, u32[]{:S(2)}) collective-permute-start(f32[528,256]{1,0:T(8,128)S(1)} %get-tuple-element.27.after.mine), channel_id=1, source_target_pairs={{0,16},{16,0},{1,17},{17,1},{2,18},{18,2},{3,19},{19,3},{4,20},{20... | collective-permute-start | bytes 1622024 | tf_op jit(solution)/shard_map/ppermute | solution.py:460
  62.0 8.1 %collective-permute-start.13 = (f32[264,256]{1,0:T(8,128)S(1)}, f32[264,256]{1,0:T(8,128)S(1)}, u32[]{:S(2)}, u32[]{:S(2)}) collective-permute-start(f32[264,256]{1,0:T(8,128)S(1)} %get-tuple-element.30), channel_id=1, source_target_pairs={{0,32},{32,0},{64,96},{96,64},{1,33},{33,1},{65,97},{97,65},{2,34}... | collective-permute-start | bytes 811016 | tf_op jit(solution)/shard_map/ppermute | solution.py:460
  70.1 8.0 %collective-permute-start.14 = (f32[264,256]{1,0:T(8,128)S(1)}, f32[264,256]{1,0:T(8,128)S(1)}, u32[]{:S(2)}, u32[]{:S(2)}) collective-permute-start(f32[264,256]{1,0:T(8,128)S(1)} %collective-permute-done.13.mine), channel_id=1, source_target_pairs={{0,16},{16,0},{1,17},{17,1},{2,18},{18,2},{3,19},{19,3},{4,20},{20... | collective-permute-start | bytes 811016 | tf_op jit(solution)/shard_map/ppermute | solution.py:460
  71.0 7.0 %copy-start = (f32[256,256]{1,0:T(8,128)S(1)}, f32[256,256]{1,0:T(8,128)}, u32[]{:S(2)}) copy-start(f32[256,256]{1,0:T(8,128)} %cov.1) | copy-start | bytes 786436
  71.0 7.0 %copy-start.1 = (f32[256]{0:T(256)S(1)}, f32[256]{0:T(256)}, u32[]{:S(2)}) copy-start(f32[256]{0:T(256)} %param.12) | copy-start | bytes 3076
  78.2 2.1 %collective-permute-start.16 = (f32[144,256]{1,0:T(8,128)S(1)}, f32[144,256]{1,0:T(8,128)S(1)}, u32[]{:S(2)}, u32[]{:S(2)}) collective-permute-start(f32[144,256]{1,0:T(8,128)S(1)} %get-tuple-element.36.after), channel_id=1, source_target_pairs={{0,96},{1,97},{2,98},{3,99},{4,100},{5,101},{6,102},{7,103},{8,104... | collective-permute-start | bytes 442376 | tf_op jit(solution)/shard_map/ppermute | solution.py:516
  78.9 8.8 %collective-permute-start.15 = (f32[144,256]{1,0:T(8,128)S(1)}, f32[144,256]{1,0:T(8,128)S(1)}, u32[]{:S(2)}, u32[]{:S(2)}) collective-permute-start(f32[144,256]{1,0:T(8,128)S(1)} %get-tuple-element.36.after), channel_id=1, source_target_pairs={{0,64},{1,65},{2,66},{3,67},{4,68},{5,69},{6,70},{7,71},{8,72},{9,... | collective-permute-start | bytes 442376 | tf_op jit(solution)/shard_map/ppermute | solution.py:515

commit v5 on v4

--- a/solution.py
+++ b/solution.py
@@ -175,7 +175,7 @@
 
 
 def build_kernel(
-    trans_in, obs_in, noise_in, meas_in, state_in, move_ref, side_ref, pair, trans, obs, noise, meas,
+    trans_in, obs_in, noise_in, meas_in, state_in, move_ref, side_ref, one_ref, trans, obs, noise, meas,
     noise_state, sems, stack, small_a, small_b,
 ):
     copies = [
@@ -225,10 +225,8 @@
         vecs = jnp.where(place == 0, vec[0:1, N:], jnp.where(place == 1, vec[0:1, 0:N], 0.0))
         steps.append((trans[k].T - full[0:N, N:], state - full[N:, N:], full[0:N, 0:N], vecs))
     move, spread, info, vecs = steps[0]
-    pack(*parts(pair.at[0]), move, spread, info, vecs[0:1], vecs[1:2])
+    pack(*parts(one_ref), move, spread, info, vecs[0:1], vecs[1:2])
     pack(move_ref, side_ref, *combine(steps[0:1], steps[1:2], [stack], False)[0])
-    pair[1, 0:N, :] = move_ref[...]
-    pair[1, N:, :] = side_ref[...]
 
 
 def upper(here, axis, step):
@@ -271,17 +269,26 @@
         out[1][...] = held_ref[4, N:, :]
 
 
-def core_kernel(here, mine, theirs, after, out, half, first, second, stack):
+def choose(flag, yes, no):
+    return tuple(jnp.where(flag, p, q) for p, q in zip(yes, no))
+
+
+def core_kernel(here, mine, theirs, after, out, half, stack):
     flag = upper(here, "c", 1)
-    first[...] = jnp.where(flag, theirs[...], mine[...])
-    second[...] = jnp.where(flag, mine[...], theirs[...])
-    done = combine([unpack(*parts(first))], [unpack(*parts(second))], [stack], False)
+    own, rest = unpack(*parts(mine)), unpack(*parts(theirs))
+    done = combine([choose(flag, rest, own)], [choose(flag, own, rest)], [stack], False)
     pack(*parts(out), *done[0])
     half[...] = jnp.where(flag, out[HALF:, :], out[0:HALF, :])
 
 
-def slow_kernel(step, here, ta, tb, pair, after, out, stack):
-    out[...] = pair[...]
+def slow_kernel(step, here, ta, tb, *refs):
+    *pair, _, out, stack = refs
+    if len(pair) == 1:
+        out[...] = pair[0][...]
+    else:
+        out[0] = pair[0][...]
+        out[1, 0:N, :] = pair[1][...]
+        out[1, N:, :] = pair[2][...]
 
     def one(k, carry):
         second = out.at[k]
@@ -479,7 +486,8 @@
 
     def slow(step, theirs, pair, after):
         kernel = functools.partial(slow_kernel, step)
-        return call(kernel, "svvva", [PAIR], [STACK], 28)(here, *theirs, pair, after)
+        places = "svv" + "v" * len(pair) + "a"
+        return call(kernel, places, [PAIR], [STACK], 28)(here, *theirs, *pair, after)
 
     ringed = call(ringed_kernel, "svvvva", [ELEMENT], [STACK], 14)
     cored = call(cored_kernel, "svvva", [ELEMENT, PAIR], [(5, *ELEMENT), STACK], 42)
@@ -489,20 +497,21 @@
     build = call(
         build_kernel,
         "hhhhh",
-        [MOVE, SIDE, PAIR],
+        [MOVE, SIDE, ELEMENT],
         inputs + [pltpu.SemaphoreType.DMA((5,)), STACK, (2 * O, O), (2 * O, O)],
         30,
     )
-    core = call(core_kernel, "svva", [ELEMENT, (HALF, N)], [ELEMENT, ELEMENT, STACK], 14)
+    core = call(core_kernel, "svva", [ELEMENT, (HALF, N)], [STACK], 14)
     prior = call(prior_kernel, "svvvv", [(2, V, N), (2, N, N)], [(2, *ELEMENT), STACK], 28)
     second = call(second_kernel, "svvvva", [ELEMENT, PACKED], [STACK], 14)
     final = call(final_kernel, "svvvvv", [(2, N), (2, N, N)], [PACKED, (N, N), STACK, STACK], 24)
 
     arrays = (transition, observe, noise_obs, measured, noise_state)
-    *whole, pair = build(*(pltpu.with_memory_space_constraint(a, pltpu.HBM) for a in arrays))
+    *whole, one = build(*(pltpu.with_memory_space_constraint(a, pltpu.HBM) for a in arrays))
+    steps_two = tuple(whole)
     whole, prev, other = ring("y", whole, here)
-    pair = slow(1, prev, pair, whole[0])
-    pair = slow(2, other, pair, whole[0])
+    pair = slow(1, prev, (one, *steps_two), whole[0])
+    pair = slow(2, other, (pair,), whole[0])
     whole, prev, other = ring("z", whole, pair)
     c1 = swap(whole[0], "c", 1)
     low = ringed(here, *other, *prev, whole[0])

time: 93.6 us -> 93.6 us (level)
  no operation moved by 1% of the time
where the time goes in v5:
time: 93.6 us; the launch traced here: 93.4 us
  waiting for transfers between devices  37.9 us (40%)
  Pallas kernels  35.8 us (38%)
  starting transfers between devices  18.9 us (20%)
    ppermute x12, waiting for transfers between devices, turn(): return lax.ppermute(part, axis, [(k, (k + step) % 4) for k in range(4)])  22.7 us
    ppermute x12, starting transfers between devices, turn(): return lax.ppermute(part, axis, [(k, (k + step) % 4) for k in range(4)])  12.7 us
    pallas_call x2, Pallas kernels, ring(): *whole, other_a, other_b = run(here, own, *near, far_a, far_b)  8.49 us
    ppermute x3, waiting for transfers between devices, swap(): return lax.ppermute(part, axis, [(k, k ^ step) for k in range(size)])  7.78 us
    ppermute x1, waiting for transfers between devices, on_device(): state_a = lax.ppermute(packed, 'x', [(0, 2)])  7.43 us
    pallas_call x1, Pallas kernels, on_device(): low, pair = cored(here, c1, low, pair, whole)  6.98 us
    pallas_call x1, Pallas kernels, on_device(): return final(here, state_a, state_b, means, covs, pair)  5.74 us
    pallas_call x1, Pallas kernels, on_device(): build(*(pltpu.with_memory_space_constraint(a, pltpu.HBM) for a in arrays))  4.91 us
  transfers between devices with their start and end apart: 17, of which 10 were waited for; matrix products, arithmetic and copies ran while one was open for 0% of the time, Pallas kernels for 15%

profile of v5, /device:TPU:101, one launch (start us, length us, event | category | flops | bytes accessed | tf_op | source)
XLA Modules:
  0.0 93.4 jit_solution(3710526438776243387)
XLA Ops:
  0.6 4.9 %shard_map.86 = (f32[256,256]{1,0:T(8,128)S(1)}, f32[272,256]{1,0:T(8,128)S(1)}, f32[528,256]{1,0:T(8,128)S(1)}) custom-call(f32[2,256,256]{2,1,0:T(8,128)} %trans_in.1, f32[2,64,256]{2,1,0:T(8,128)} %obs_in.1, f32[2,64]{1,0:T(2,128)} %noise_in.1, f32[2,64]{1,0:T(2,128)} %meas_in.1, f32[256,256]{1,0:T(8,128)} %state_in.1), custom_call_target="tpu_custom_call" | custom-call | flops 3019898880 | bytes 524288 | tf_op jit(solution)/shard_map/pallas_call | solution.py:510
  5.6 1.4 %collective-permute-start.1 = (f32[272,256]{1,0:T(8,128)S(1)}, f32[272,256]{1,0:T(8,128)S(1)}, u32[]{:S(2)}, u32[]{:S(2)}) collective-permute-start(f32[272,256]{1,0:T(8,128)S(1)} %get-tuple-element.21.mb.refs_2_), channel_id=1, source_target_pairs={{0,1},{1,2},{2,3},{3,0},{4,5},{5,6},{6,7},{7,4},{8,9},{9,10},{10,1... | collective-permute-start | bytes 835592 | tf_op jit(solution)/shard_map/ppermute | solution.py:471
  6.9 1.5 %collective-permute-start.2 = (f32[256,256]{1,0:T(8,128)S(1)}, f32[256,256]{1,0:T(8,128)S(1)}, u32[]{:S(2)}, u32[]{:S(2)}) collective-permute-start(f32[256,256]{1,0:T(8,128)S(1)} %get-tuple-element.20.ma.refs_1_), channel_id=1, source_target_pairs={{0,3},{1,0},{2,1},{3,2},{4,7},{5,4},{6,5},{7,6},{8,11},{9,8},{10,9... | collective-permute-start | bytes 786440 | tf_op jit(solution)/shard_map/ppermute | solution.py:471
  8.4 1.4 %collective-permute-start.3 = (f32[272,256]{1,0:T(8,128)S(1)}, f32[272,256]{1,0:T(8,128)S(1)}, u32[]{:S(2)}, u32[]{:S(2)}) collective-permute-start(f32[272,256]{1,0:T(8,128)S(1)} %get-tuple-element.21.mb.refs_2_), channel_id=1, source_target_pairs={{0,3},{1,0},{2,1},{3,2},{4,7},{5,4},{6,5},{7,6},{8,11},{9,8},{10,9... | collective-permute-start | bytes 835592 | tf_op jit(solution)/shard_map/ppermute | solution.py:471
  9.8 0.1 collective-permute-start
  9.9 4.6 %collective-permute-done.1.pb.tb = f32[272,256]{1,0:T(8,128)S(1)} collective-permute-done((f32[272,256]{1,0:T(8,128)S(1)}, f32[272,256]{1,0:T(8,128)S(1)}, u32[]{:S(2)}, u32[]{:S(2)}) %collective-permute-start.1) | collective-permute-done | bytes 278560 | tf_op jit(solution)/shard_map/ppermute | solution.py:471
  14.5 0.0 collective-permute-start.5
  14.5 0.0 collective-permute-done.2.na
  14.5 2.7 %collective-permute-start.4 = (f32[256,256]{1,0:T(8,128)S(1)}, f32[256,256]{1,0:T(8,128)S(1)}, u32[]{:S(2)}, u32[]{:S(2)}) collective-permute-start(f32[256,256]{1,0:T(8,128)S(1)} %collective-permute-done.2.na), channel_id=1, source_target_pairs={{0,3},{1,0},{2,1},{3,2},{4,7},{5,4},{6,5},{7,6},{8,11},{9,8},{10,9... | collective-permute-start | bytes 786440 | tf_op jit(solution)/shard_map/ppermute | solution.py:471
  17.2 2.9 %collective-permute-done.pa.ta = f32[256,256]{1,0:T(8,128)S(1)} collective-permute-done((f32[256,256]{1,0:T(8,128)S(1)}, f32[256,256]{1,0:T(8,128)S(1)}, u32[]{:S(2)}, u32[]{:S(2)}) %collective-permute-start) | collective-permute-done | bytes 262176 | tf_op jit(solution)/shard_map/ppermute | solution.py:471
  20.1 0.0 collective-permute-done.3.nb
  20.1 2.1 %shard_map.87.own = f32[528,256]{1,0:T(8,128)S(1)} custom-call(s32[1]{0:T(128)} %bitcast.here.after, f32[256,256]{1,0:T(8,128)S(1)} %get-tuple-element.20.ma.refs_1_, f32[272,256]{1,0:T(8,128)S(1)} %get-tuple-element.21.mb.refs_2_, f32[256,256]{1,0:T(8,128)S(1)} %collective-permute-done.pa.ta, f32[272,256]{1,0:T(8,128)S(1)} %collective-permute-done.1.pb.tb, ...), custom_call_target="tpu_custom_call" | custom-call | flops 1409286144 | bytes 524288 | tf_op jit(solution)/shard_map/pallas_call | solution.py:480
  22.2 3.2 %collective-permute-done.4.fa = f32[256,256]{1,0:T(8,128)S(1)} collective-permute-done((f32[256,256]{1,0:T(8,128)S(1)}, f32[256,256]{1,0:T(8,128)S(1)}, u32[]{:S(2)}, u32[]{:S(2)}) %collective-permute-start.4) | collective-permute-done | bytes 262176 | tf_op jit(solution)/shard_map/ppermute | solution.py:471
  25.4 0.7 collective-permute-done.5.fb
  26.1 4.2 %shard_map.88 = (f32[256,256]{1,0:T(8,128)S(1)}, f32[272,256]{1,0:T(8,128)S(1)}, f32[256,256]{1,0:T(8,128)S(1)}, f32[272,256]{1,0:T(8,128)S(1)}) custom-call(s32[1]{0:T(128)} %bitcast.here.after, f32[528,256]{1,0:T(8,128)S(1)} %shard_map.87.own, f32[256,256]{1,0:T(8,128)S(1)} %collective-permute-done.pa.ta, f32[272,256]{1,0:T(8,128)S(1)} %collective-permute-done.1.pb.tb, ...), custom_call_target="tpu_custom_call" | custom-call | flops 2818572288 | bytes 524288 | tf_op jit(solution)/shard_map/pallas_call | solution.py:484
  30.3 0.1 collective-permute-start.7
  30.4 1.5 %collective-permute-start.8 = (f32[256,256]{1,0:T(8,128)S(1)}, f32[256,256]{1,0:T(8,128)S(1)}, u32[]{:S(2)}, u32[]{:S(2)}) collective-permute-start(f32[256,256]{1,0:T(8,128)S(1)} %get-tuple-element.22.refs_3_.refs_1_.ma), channel_id=1, source_target_pairs={{0,12},{4,0},{8,4},{12,8},{1,13},{5,1},{9,5},{13,9},{2,14},{6,2},{... | collective-permute-start | bytes 786440 | tf_op jit(solution)/shard_map/ppermute | solution.py:471
  31.9 1.3 %collective-permute-start.6 = (f32[256,256]{1,0:T(8,128)S(1)}, f32[256,256]{1,0:T(8,128)S(1)}, u32[]{:S(2)}, u32[]{:S(2)}) collective-permute-start(f32[256,256]{1,0:T(8,128)S(1)} %get-tuple-element.22.refs_3_.refs_1_.ma), channel_id=1, source_target_pairs={{0,4},{4,8},{8,12},{12,0},{1,5},{5,9},{9,13},{13,1},{2,6},{6,10},{... | collective-permute-start | bytes 786440 | tf_op jit(solution)/shard_map/ppermute | solution.py:471
  33.2 0.2 collective-permute-start.9
  33.3 0.2 shard_map.89.refs_0_
  33.6 4.5 %collective-permute-done.8.na = f32[256,256]{1,0:T(8,128)S(1)} collective-permute-done((f32[256,256]{1,0:T(8,128)S(1)}, f32[256,256]{1,0:T(8,128)S(1)}, u32[]{:S(2)}, u32[]{:S(2)}) %collective-permute-start.8) | collective-permute-done | bytes 262176 | tf_op jit(solution)/shard_map/ppermute | solution.py:471
  38.1 0.0 collective-permute-start.10
  38.1 0.0 collective-permute-done.7.pb
  38.1 2.7 %collective-permute-start.11 = (f32[272,256]{1,0:T(8,128)S(1)}, f32[272,256]{1,0:T(8,128)S(1)}, u32[]{:S(2)}, u32[]{:S(2)}) collective-permute-start(f32[272,256]{1,0:T(8,128)S(1)} %collective-permute-done.7.pb), channel_id=1, source_target_pairs={{0,4},{4,8},{8,12},{12,0},{1,5},{5,9},{9,13},{13,1},{2,6},{6,10},{... | collective-permute-start | bytes 835592 | tf_op jit(solution)/shard_map/ppermute | solution.py:471
  40.8 0.1 shard_map.90.after.pair
  40.8 1.9 %collective-permute-done.6.pa = f32[256,256]{1,0:T(8,128)S(1)} collective-permute-done((f32[256,256]{1,0:T(8,128)S(1)}, f32[256,256]{1,0:T(8,128)S(1)}, u32[]{:S(2)}, u32[]{:S(2)}) %collective-permute-start.6) | collective-permute-done | bytes 262176 | tf_op jit(solution)/shard_map/ppermute | solution.py:471
  42.8 1.3 %collective-permute-done.9.nb = f32[272,256]{1,0:T(8,128)S(1)} collective-permute-done((f32[272,256]{1,0:T(8,128)S(1)}, f32[272,256]{1,0:T(8,128)S(1)}, u32[]{:S(2)}, u32[]{:S(2)}) %collective-permute-start.9) | collective-permute-done | bytes 278560 | tf_op jit(solution)/shard_map/ppermute | solution.py:471
  44.0 2.0 %shard_map.91.own = f32[528,256]{1,0:T(8,128)S(1)} custom-call(s32[1]{0:T(128)} %bitcast.here.after, f32[256,256]{1,0:T(8,128)S(1)} %get-tuple-element.22.refs_3_.refs_1_.ma, f32[272,256]{1,0:T(8,128)S(1)} %get-tuple-element.23.mb, f32[256,256]{1,0:T(8,128)S(1)} %collective-permute-done.6.pa, f32[272,256]{1,0:T(8,128)S(1)} %collective-permute-done.7.pb, ...), custom_call_target="tpu_custom_call" | custom-call | flops 1409286144 | bytes 524288 | tf_op jit(solution)/shard_map/pallas_call | solution.py:480
  46.1 3.6 %collective-permute-done.10.fa = f32[256,256]{1,0:T(8,128)S(1)} collective-permute-done((f32[256,256]{1,0:T(8,128)S(1)}, f32[256,256]{1,0:T(8,128)S(1)}, u32[]{:S(2)}, u32[]{:S(2)}) %collective-permute-start.10) | collective-permute-done | bytes 262176 | tf_op jit(solution)/shard_map/ppermute | solution.py:471
  49.7 0.0 collective-permute-done.11.fb
  49.7 4.2 %shard_map.92 = (f32[528,256]{1,0:T(8,128)S(1)}, f32[256,256]{1,0:T(8,128)S(1)}, f32[272,256]{1,0:T(8,128)S(1)}) custom-call(s32[1]{0:T(128)} %bitcast.here.after, f32[528,256]{1,0:T(8,128)S(1)} %shard_map.91.own, f32[256,256]{1,0:T(8,128)S(1)} %collective-permute-done.6.pa, f32[272,256]{1,0:T(8,128)S(1)} %collective-permute-done.7.pb, ...), custom_call_target="tpu_custom_call" | custom-call | flops 2818572288 | bytes 524288 | tf_op jit(solution)/shard_map/pallas_call | solution.py:484
  53.9 3.1 %collective-permute-start.12 = (f32[528,256]{1,0:T(8,128)S(1)}, f32[528,256]{1,0:T(8,128)S(1)}, u32[]{:S(2)}, u32[]{:S(2)}) collective-permute-start(f32[528,256]{1,0:T(8,128)S(1)} %get-tuple-element.27.after.mine), channel_id=1, source_target_pairs={{0,16},{16,0},{1,17},{17,1},{2,18},{18,2},{3,19},{19,3},{4,20},{20... | collective-permute-start | bytes 1622024 | tf_op jit(solution)/shard_map/ppermute | solution.py:467
  57.0 2.0 %shard_map.93.after.low = f32[528,256]{1,0:T(8,128)S(1)} custom-call(s32[1]{0:T(128)} %bitcast.here.after, f32[256,256]{1,0:T(8,128)S(1)} %get-tuple-element.28.oa, f32[272,256]{1,0:T(8,128)S(1)} %get-tuple-element.29.ob, f32[256,256]{1,0:T(8,128)S(1)} %collective-permute-done.6.pa, f32[272,256]{1,0:T(8,128)S(1)} %collective-permute-done.7.pb, ...), custom_call_target="tpu_custom_call" | custom-call | flops 1409286144 | bytes 524288 | tf_op jit(solution)/shard_map/pallas_call | solution.py:517
  59.1 0.0 collective-permute-done.12.theirs
  59.1 3.0 %shard_map.94 = (f32[528,256]{1,0:T(8,128)S(1)}, f32[264,256]{1,0:T(8,128)S(1)}) custom-call(s32[1]{0:T(128)} %bitcast.here.after, f32[528,256]{1,0:T(8,128)S(1)} %get-tuple-element.27.after.mine, f32[528,256]{1,0:T(8,128)S(1)} %collective-permute-done.12.theirs, f32[528,256]{1,0:T(8,128)S(1)} %shard_map.93.after.low), custom_call_target="tpu_custom_call" | custom-call | flops 1409286144 | bytes 524288 | tf_op jit(solution)/shard_map/pallas_call | solution.py:518
  62.0 0.3 collective-permute-start.13
  62.3 7.8 %collective-permute-done.13.mine = f32[264,256]{1,0:T(8,128)S(1)} collective-permute-done((f32[264,256]{1,0:T(8,128)S(1)}, f32[264,256]{1,0:T(8,128)S(1)}, u32[]{:S(2)}, u32[]{:S(2)}) %collective-permute-start.13) | collective-permute-done | bytes 270368 | tf_op jit(solution)/shard_map/ppermute | solution.py:467
  70.1 0.9 collective-permute-start.14
  71.0 0.0 copy-start
  71.0 0.0 copy-start.1
  71.0 7.0 %shard_map.95 = (f32[528,256]{1,0:T(8,128)S(1)}, f32[2,528,256]{2,1,0:T(8,128)S(1)}) custom-call(s32[1]{0:T(128)} %bitcast.here.after, f32[528,256]{1,0:T(8,128)S(1)} %collective-permute-done.12.theirs, f32[528,256]{1,0:T(8,128)S(1)} %shard_map.93.after.low, f32[2,528,256]{2,1,0:T(8,128)S(1)} %shard_map.90.after.pair, ...), custom_call_target="tpu_custom_call" | custom-call | flops 4227858432 | bytes 524288 | tf_op jit(solution)/shard_map/pallas_call | solution.py:520
  78.0 0.0 copy-done
  78.0 0.0 copy-done.1
  78.0 0.1 shard_map.96
  78.1 0.0 collective-permute-done.14.other
  78.1 0.1 shard_map.97
  78.2 0.7 collective-permute-start.16
  78.9 1.3 %collective-permute-start.15 = (f32[144,256]{1,0:T(8,128)S(1)}, f32[144,256]{1,0:T(8,128)S(1)}, u32[]{:S(2)}, u32[]{:S(2)}) collective-permute-start(f32[144,256]{1,0:T(8,128)S(1)} %get-tuple-element.36.after), channel_id=1, source_target_pairs={{0,64},{1,65},{2,66},{3,67},{4,68},{5,69},{6,70},{7,71},{8,72},{9,... | collective-permute-start | bytes 442376 | tf_op jit(solution)/shard_map/ppermute | solution.py:524
  80.2 0.1 shard_map.98.pair
  80.3 0.0 collective-permute-done.16.state_b
  80.3 7.4 %collective-permute-done.15.state_a = f32[144,256]{1,0:T(8,128)S(1)} collective-permute-done((f32[144,256]{1,0:T(8,128)S(1)}, f32[144,256]{1,0:T(8,128)S(1)}, u32[]{:S(2)}, u32[]{:S(2)}) %collective-permute-start.15) | collective-permute-done | bytes 147488 | tf_op jit(solution)/shard_map/ppermute | solution.py:524
  87.7 5.7 %shard_map.99 = (f32[2,256]{1,0:T(2,128)}, f32[2,256,256]{2,1,0:T(8,128)}) custom-call(s32[1]{0:T(128)} %bitcast.here.after, f32[144,256]{1,0:T(8,128)S(1)} %collective-permute-done.15.state_a, f32[144,256]{1,0:T(8,128)S(1)} %collective-permute-done.16.state_b, f32[2,16,256]{2,1,0:T(8,128)S(1)} %get-tuple-element.33.mean, ...), custom_call_target="tpu_custom_call" | custom-call | flops 2415919104 | bytes 524288 | tf_op jit(solution)/shard_map/pallas_call | solution.py:527
Async XLA Ops:
  5.6 8.9 %collective-permute-start.1 = (f32[272,256]{1,0:T(8,128)S(1)}, f32[272,256]{1,0:T(8,128)S(1)}, u32[]{:S(2)}, u32[]{:S(2)}) collective-permute-start(f32[272,256]{1,0:T(8,128)S(1)} %get-tuple-element.21.mb.refs_2_), channel_id=1, source_target_pairs={{0,1},{1,2},{2,3},{3,0},{4,5},{5,6},{6,7},{7,4},{8,9},{9,10},{10,1... | collective-permute-start | bytes 835592 | tf_op jit(solution)/shard_map/ppermute | solution.py:471
  6.9 7.6 %collective-permute-start.2 = (f32[256,256]{1,0:T(8,128)S(1)}, f32[256,256]{1,0:T(8,128)S(1)}, u32[]{:S(2)}, u32[]{:S(2)}) collective-permute-start(f32[256,256]{1,0:T(8,128)S(1)} %get-tuple-element.20.ma.refs_1_), channel_id=1, source_target_pairs={{0,3},{1,0},{2,1},{3,2},{4,7},{5,4},{6,5},{7,6},{8,11},{9,8},{10,9... | collective-permute-start | bytes 786440 | tf_op jit(solution)/shard_map/ppermute | solution.py:471
  8.4 11.7 %collective-permute-start.3 = (f32[272,256]{1,0:T(8,128)S(1)}, f32[272,256]{1,0:T(8,128)S(1)}, u32[]{:S(2)}, u32[]{:S(2)}) collective-permute-start(f32[272,256]{1,0:T(8,128)S(1)} %get-tuple-element.21.mb.refs_2_), channel_id=1, source_target_pairs={{0,3},{1,0},{2,1},{3,2},{4,7},{5,4},{6,5},{7,6},{8,11},{9,8},{10,9... | collective-permute-start | bytes 835592 | tf_op jit(solution)/shard_map/ppermute | solution.py:471
  9.8 10.3 %collective-permute-start = (f32[256,256]{1,0:T(8,128)S(1)}, f32[256,256]{1,0:T(8,128)S(1)}, u32[]{:S(2)}, u32[]{:S(2)}) collective-permute-start(f32[256,256]{1,0:T(8,128)S(1)} %get-tuple-element.20.ma.refs_1_), channel_id=1, source_target_pairs={{0,1},{1,2},{2,3},{3,0},{4,5},{5,6},{6,7},{7,4},{8,9},{9,10},{10,1... | collective-permute-start | bytes 786440 | tf_op jit(solution)/shard_map/ppermute | solution.py:471
  14.5 11.6 %collective-permute-start.5 = (f32[272,256]{1,0:T(8,128)S(1)}, f32[272,256]{1,0:T(8,128)S(1)}, u32[]{:S(2)}, u32[]{:S(2)}) collective-permute-start(f32[272,256]{1,0:T(8,128)S(1)} %collective-permute-done.1.pb.tb), channel_id=1, source_target_pairs={{0,1},{1,2},{2,3},{3,0},{4,5},{5,6},{6,7},{7,4},{8,9},{9,10},{10,1... | collective-permute-start | bytes 835592 | tf_op jit(solution)/shard_map/ppermute | solution.py:471
  14.5 10.9 %collective-permute-start.4 = (f32[256,256]{1,0:T(8,128)S(1)}, f32[256,256]{1,0:T(8,128)S(1)}, u32[]{:S(2)}, u32[]{:S(2)}) collective-permute-start(f32[256,256]{1,0:T(8,128)S(1)} %collective-permute-done.2.na), channel_id=1, source_target_pairs={{0,3},{1,0},{2,1},{3,2},{4,7},{5,4},{6,5},{7,6},{8,11},{9,8},{10,9... | collective-permute-start | bytes 786440 | tf_op jit(solution)/shard_map/ppermute | solution.py:471
  30.3 7.8 %collective-permute-start.7 = (f32[272,256]{1,0:T(8,128)S(1)}, f32[272,256]{1,0:T(8,128)S(1)}, u32[]{:S(2)}, u32[]{:S(2)}) collective-permute-start(f32[272,256]{1,0:T(8,128)S(1)} %get-tuple-element.23.mb), channel_id=1, source_target_pairs={{0,4},{4,8},{8,12},{12,0},{1,5},{5,9},{9,13},{13,1},{2,6},{6,10},{... | collective-permute-start | bytes 835592 | tf_op jit(solution)/shard_map/ppermute | solution.py:471
  30.4 7.7 %collective-permute-start.8 = (f32[256,256]{1,0:T(8,128)S(1)}, f32[256,256]{1,0:T(8,128)S(1)}, u32[]{:S(2)}, u32[]{:S(2)}) collective-permute-start(f32[256,256]{1,0:T(8,128)S(1)} %get-tuple-element.22.refs_3_.refs_1_.ma), channel_id=1, source_target_pairs={{0,12},{4,0},{8,4},{12,8},{1,13},{5,1},{9,5},{13,9},{2,14},{6,2},{... | collective-permute-start | bytes 786440 | tf_op jit(solution)/shard_map/ppermute | solution.py:471
  31.9 10.9 %collective-permute-start.6 = (f32[256,256]{1,0:T(8,128)S(1)}, f32[256,256]{1,0:T(8,128)S(1)}, u32[]{:S(2)}, u32[]{:S(2)}) collective-permute-start(f32[256,256]{1,0:T(8,128)S(1)} %get-tuple-element.22.refs_3_.refs_1_.ma), channel_id=1, source_target_pairs={{0,4},{4,8},{8,12},{12,0},{1,5},{5,9},{9,13},{13,1},{2,6},{6,10},{... | collective-permute-start | bytes 786440 | tf_op jit(solution)/shard_map/ppermute | solution.py:471
  33.2 10.9 %collective-permute-start.9 = (f32[272,256]{1,0:T(8,128)S(1)}, f32[272,256]{1,0:T(8,128)S(1)}, u32[]{:S(2)}, u32[]{:S(2)}) collective-permute-start(f32[272,256]{1,0:T(8,128)S(1)} %get-tuple-element.23.mb), channel_id=1, source_target_pairs={{0,12},{4,0},{8,4},{12,8},{1,13},{5,1},{9,5},{13,9},{2,14},{6,2},{... | collective-permute-start | bytes 835592 | tf_op jit(solution)/shard_map/ppermute | solution.py:471
  38.1 11.6 %collective-permute-start.10 = (f32[256,256]{1,0:T(8,128)S(1)}, f32[256,256]{1,0:T(8,128)S(1)}, u32[]{:S(2)}, u32[]{:S(2)}) collective-permute-start(f32[256,256]{1,0:T(8,128)S(1)} %collective-permute-done.8.na), channel_id=1, source_target_pairs={{0,12},{4,0},{8,4},{12,8},{1,13},{5,1},{9,5},{13,9},{2,14},{6,2},{... | collective-permute-start | bytes 786440 | tf_op jit(solution)/shard_map/ppermute | solution.py:471
  38.1 11.6 %collective-permute-start.11 = (f32[272,256]{1,0:T(8,128)S(1)}, f32[272,256]{1,0:T(8,128)S(1)}, u32[]{:S(2)}, u32[]{:S(2)}) collective-permute-start(f32[272,256]{1,0:T(8,128)S(1)} %collective-permute-done.7.pb), channel_id=1, source_target_pairs={{0,4},{4,8},{8,12},{12,0},{1,5},{5,9},{9,13},{13,1},{2,6},{6,10},{... | collective-permute-start | bytes 835592 | tf_op jit(solution)/shard_map/ppermute | solution.py:471
  53.9 5.1 %collective-permute-start.12 = (f32[528,256]{1,0:T(8,128)S(1)}, f32[528,256]{1,0:T(8,128)S(1)}, u32[]{:S(2)}, u32[]{:S(2)}) collective-permute-start(f32[528,256]{1,0:T(8,128)S(1)} %get-tuple-element.27.after.mine), channel_id=1, source_target_pairs={{0,16},{16,0},{1,17},{17,1},{2,18},{18,2},{3,19},{19,3},{4,20},{20... | collective-permute-start | bytes 1622024 | tf_op jit(solution)/shard_map/ppermute | solution.py:467
  62.0 8.1 %collective-permute-start.13 = (f32[264,256]{1,0:T(8,128)S(1)}, f32[264,256]{1,0:T(8,128)S(1)}, u32[]{:S(2)}, u32[]{:S(2)}) collective-permute-start(f32[264,256]{1,0:T(8,128)S(1)} %get-tuple-element.30), channel_id=1, source_target_pairs={{0,32},{32,0},{64,96},{96,64},{1,33},{33,1},{65,97},{97,65},{2,34}... | collective-permute-start | bytes 811016 | tf_op jit(solution)/shard_map/ppermute | solution.py:467
  70.1 8.0 %collective-permute-start.14 = (f32[264,256]{1,0:T(8,128)S(1)}, f32[264,256]{1,0:T(8,128)S(1)}, u32[]{:S(2)}, u32[]{:S(2)}) collective-permute-start(f32[264,256]{1,0:T(8,128)S(1)} %collective-permute-done.13.mine), channel_id=1, source_target_pairs={{0,16},{16,0},{1,17},{17,1},{2,18},{18,2},{3,19},{19,3},{4,20},{20... | collective-permute-start | bytes 811016 | tf_op jit(solution)/shard_map/ppermute | solution.py:467
  71.0 7.0 %copy-start = (f32[256,256]{1,0:T(8,128)S(1)}, f32[256,256]{1,0:T(8,128)}, u32[]{:S(2)}) copy-start(f32[256,256]{1,0:T(8,128)} %cov.1) | copy-start | bytes 786436
  71.0 7.0 %copy-start.1 = (f32[256]{0:T(256)S(1)}, f32[256]{0:T(256)}, u32[]{:S(2)}) copy-start(f32[256]{0:T(256)} %param.12) | copy-start | bytes 3076
  78.2 2.1 %collective-permute-start.16 = (f32[144,256]{1,0:T(8,128)S(1)}, f32[144,256]{1,0:T(8,128)S(1)}, u32[]{:S(2)}, u32[]{:S(2)}) collective-permute-start(f32[144,256]{1,0:T(8,128)S(1)} %get-tuple-element.36.after), channel_id=1, source_target_pairs={{0,96},{1,97},{2,98},{3,99},{4,100},{5,101},{6,102},{7,103},{8,104... | collective-permute-start | bytes 442376 | tf_op jit(solution)/shard_map/ppermute | solution.py:525
  78.9 8.8 %collective-permute-start.15 = (f32[144,256]{1,0:T(8,128)S(1)}, f32[144,256]{1,0:T(8,128)S(1)}, u32[]{:S(2)}, u32[]{:S(2)}) collective-permute-start(f32[144,256]{1,0:T(8,128)S(1)} %get-tuple-element.36.after), channel_id=1, source_target_pairs={{0,64},{1,65},{2,66},{3,67},{4,68},{5,69},{6,70},{7,71},{8,72},{9,... | collective-permute-start | bytes 442376 | tf_op jit(solution)/shard_map/ppermute | solution.py:524
